TPU v7x, 512 devices: a whole 4x8x8 slice. The times are simulated.
512 devices in a mesh: own: 8 (over z_lo, core), dom: 64 (over y, z_hi, x).
Axes of the slice: x: 4, y: 8, z: 8 (z_hi: 2, z_lo: 4; z = z_hi * 4 + z_lo), core: 2. Of those that a mesh axis runs over, the one named last changes fastest.
Arguments:
- background: bfloat16 [1024, 6, 4096], P(('own', 'dom')), may hold values from -6 to 6
- storm_track: float32 [2, 5], replicated, may hold values from 0.02 to 1638.4, as said below
- need_tiles: int32 [512, 32], P(('own', 'dom')), may hold values from 0 to 1023, as said below
- node_cells: int32 [16384, 1024], P(('own', 'dom')), may hold values from 0 to 4030, as said below
- node_fracs: float32 [2, 16384, 1024], P(None, ('own', 'dom')), may hold values from 0 to 1
- slot_count: int32 [16384], P(('own', 'dom')), may hold values from 256 to 1024
- elevation: float32 [8, 2097152], P('own', 'dom'), may hold values from 0 to 2
- bed_level: float32 [8, 2097152], P('own', 'dom'), may hold values from -1 to 1.5
Outputs:
- forcing: bfloat16 [16384, 6, 1024], P(('own', 'dom'))
- surge_level: float32 [8, 2097152], P('own', 'dom')
Inputs may be any that keep to these rules, and one draw needn't show every extreme that they name: `need_tiles`: entries k * 4 to (k + 1) * 4 - 1 of a row name tiles of band k (tiles k * 128 to (k + 1) * 128 - 1); within a row the numbers (tile % 128) // 2 are all different. `node_cells`: value // 64 and value % 64 are both at most 62. `storm_track`: row k: centre column and row in cells, pressure deficit, radius of maximum wind in cells, shape exponent; all positive.
All inputs are finite; a program needn't handle non-finite values.
Results may differ from a plain program's by a relative error of at most 0.0023.
The roundings to bfloat16 on the way count: a program that leaves them out, or rounds other values in their place, can miss the bound.
Values may be sent and summed in bfloat16 or wider, within the bound.
No kernel may reach another device: no remote copies, remote signals or barrier semaphores. Data moves between devices by JAX's collectives and lax.ppermute only.
A program may use at most 64 MiB of HBM per device.

v0:
```python
import jax
import jax.numpy as jnp
from jax import lax
from jax.sharding import PartitionSpec as P

TILE = 64
TCOLS = 32
TILES_DEV = 2
FIELDS = 6
SWEEPS = 4


KAPPA = 0.08


def as_sent(value):

    def short(part):
        return part.astype(jnp.bfloat16) if part.dtype == jnp.float32 else part

    return jax.tree.map(short, value)


def extended(cells, sides, width):
    for axis, dim in sides:
        count = lax.axis_size(axis)
        ends = count - 1
        head = lax.slice_in_dim(cells, 0, width, axis=dim)
        tail = lax.slice_in_dim(cells, cells.shape[dim] - width, cells.shape[dim], axis=dim)
        cells = jnp.concatenate(
            [
                lax.ppermute(tail, axis, [(i, (i + 1) % count) for i in range(ends)]),
                cells,
                lax.ppermute(head, axis, [((i + 1) % count, i) for i in range(ends)]),
            ],
            axis=dim,
        )
    return cells


def from_everyone(value, axis):
    length = lax.axis_size(axis)
    return lax.all_to_all(
        jnp.broadcast_to(value[None], (length, *value.shape)), axis, 0, 0, tiled=True
    )


def laid_out(blocks, dim):
    blocks = jnp.moveaxis(blocks, 0, dim)
    lengths = blocks.shape
    return blocks.reshape(*lengths[:dim], lengths[dim] * lengths[dim + 1], *lengths[dim + 2 :])


def gather_directly(value, axis, dim):
    blocks = from_everyone(value, axis)
    return laid_out(blocks, dim)


def holland(tile_index, background, storm_track):
    cell_index = jnp.arange(TILE * TILE, dtype=jnp.int32)
    cell_row = (cell_index // TILE).astype(jnp.float32)
    cell_col = (cell_index % TILE).astype(jnp.float32)
    tile_row = (tile_index // TCOLS).astype(jnp.float32)
    tile_col = (tile_index % TCOLS).astype(jnp.float32)
    north_cell = tile_row[:, None] * TILE + cell_row[None, :]
    east_cell = tile_col[:, None] * TILE + cell_col[None, :]
    fields = []
    for time_level in range(2):
        offset_x = east_cell - storm_track[time_level, 0]
        offset_y = north_cell - storm_track[time_level, 1]
        radius = jnp.sqrt(offset_x * offset_x + offset_y * offset_y + 1.0)
        radial_ratio = jnp.exp(
            storm_track[time_level, 4] * jnp.log(storm_track[time_level, 3] / radius)
        )
        pressure_decay = jnp.exp(-radial_ratio)
        wind_speed = jnp.sqrt(
            storm_track[time_level, 4] * storm_track[time_level, 2] * radial_ratio * pressure_decay
        )
        fields.append(-wind_speed * offset_y / radius)
        fields.append(wind_speed * offset_x / radius)
        fields.append(-storm_track[time_level, 2] * (1.0 - pressure_decay))
    return (background.astype(jnp.float32) + jnp.stack(fields, axis=1)).astype(jnp.bfloat16)


def interpolate_local(tile_data, node_cells, node_fracs, slot_count):
    blocks = tile_data.shape[0] // 2
    positions = node_cells.shape[1]
    tile_blocks = tile_data.reshape(blocks, 2, FIELDS * TILE, TILE)
    cell_blocks = node_cells.reshape(blocks, 2, positions)
    frac_blocks = jnp.moveaxis(node_fracs.reshape(2, blocks, 2, positions), 1, 0)
    count_blocks = slot_count.reshape(blocks, 2)
    spot_index = jnp.arange(TILE, dtype=jnp.int32)[None, :, None]
    position_index = jnp.arange(positions, dtype=jnp.int32)

    def one_block(packed):
        tile_block, cell_block, frac_block, count_block = packed
        col_first = (cell_block % TILE)[:, None, :]
        row_first = (cell_block // TILE)[:, None, :]
        east_frac = frac_block[0][:, None, :]
        north_frac = frac_block[1][:, None, :]
        col_weights = (
            jnp.where(spot_index == col_first, 1.0 - east_frac, 0.0)
            + jnp.where(spot_index == col_first + 1, east_frac, 0.0)
        ).astype(jnp.bfloat16)
        row_weights = jnp.where(spot_index == row_first, 1.0 - north_frac, 0.0) + jnp.where(
            spot_index == row_first + 1, north_frac, 0.0
        )
        spread = jnp.einsum(
            "bkj,bjn->bkn", tile_block, col_weights, preferred_element_type=jnp.float32
        )
        node_value = jnp.sum(
            spread.reshape(2, FIELDS, TILE, positions) * row_weights[:, None], axis=2
        )
        live = position_index[None, :] < count_block[:, None]
        return jnp.where(live[:, None, :], node_value, jnp.float32(0.0))

    outputs = lax.map(one_block, (tile_blocks, cell_blocks, frac_blocks, count_blocks))
    return outputs.reshape(blocks * 2, FIELDS, positions)


def flux_sweep_local(elevation, bed_level):
    holders = lax.axis_size("dom")
    position = lax.axis_index("dom")
    length = elevation.shape[1]
    face_index = jnp.arange(length + 1, dtype=jnp.int32)[None, :]
    wall_face = (face_index == 0) & (position == 0) | (face_index == length) & (
        position == holders - 1
    )
    surface = elevation
    for sweep_step in range(SWEEPS):
        padded = extended(as_sent(jnp.stack([surface, bed_level])), (("dom", 2),), 1)
        wet_depth = jnp.maximum(padded[0] - padded[1], 0.0)
        slope_drop = padded[0][:, :-1] - padded[0][:, 1:]
        upwind = jnp.where(slope_drop >= 0.0, wet_depth[:, :-1], wet_depth[:, 1:])
        face_flux = jnp.where(wall_face, jnp.float32(0.0), KAPPA * upwind * slope_drop)
        surface = surface - (face_flux[:, 1:] - face_flux[:, :-1])
    return surface


def shards(
    background, storm_track, need_tiles, node_cells, node_fracs, slot_count, elevation, bed_level
):
    holders = lax.axis_size("dom")
    band_size = TILES_DEV * holders
    device_rank = lax.axis_index("own") * holders + lax.axis_index("dom")
    wanted = need_tiles[0]
    own_tiles = device_rank * TILES_DEV + jnp.arange(TILES_DEV, dtype=jnp.int32)
    outgoing = holland(own_tiles, background, storm_track)
    column = gather_directly(outgoing, "own", 0)
    holder = wanted % band_size // TILES_DEV
    within = wanted // band_size * TILES_DEV + wanted % TILES_DEV
    matches = holder[None, :] == jnp.arange(holders, dtype=jnp.int32)[:, None]
    request = jnp.where(
        jnp.any(matches, axis=1), jnp.sum(jnp.where(matches, within[None, :], 0), axis=1), -1
    )
    incoming = lax.all_to_all(request[:, None], "dom", split_axis=0, concat_axis=0, tiled=True)[
        :, 0
    ]
    picked = jnp.take(column, jnp.clip(incoming, 0, column.shape[0] - 1), axis=0)
    picked = jnp.where((incoming >= 0)[:, None, None], picked, jnp.zeros_like(picked))
    returned = lax.all_to_all(picked, "dom", split_axis=0, concat_axis=0, tiled=True)
    arrived = jnp.take(returned, holder, axis=0)
    values = interpolate_local(arrived, node_cells, node_fracs, slot_count)
    forcing = values.astype(jnp.bfloat16)
    pressure = values[:, 5, :].reshape(1, -1)
    surface = flux_sweep_local(elevation, bed_level)
    surge_level = surface - 0.5 * pressure * jnp.clip(surface - bed_level, 0.0, 1.0)
    return (forcing, surge_level)


def solution(mesh):
    placed = (
        P(("own", "dom"), None, None),
        P(),
        P(("own", "dom"), None),
        P(("own", "dom"), None),
        P(None, ("own", "dom"), None),
        P(("own", "dom")),
        P("own", "dom"),
        P("own", "dom"),
    )
    return jax.shard_map(
        shards,
        mesh=mesh,
        in_specs=placed,
        out_specs=(P(("own", "dom"), None, None), P("own", "dom")),
        check_vma=False,
    )
```

profile of v0, /device:TPU:2, one launch (start us, length us, event | category | flops | bytes accessed | tf_op | source)
XLA Modules:
  0.0 342.1 jit_solution(5943306833623007111)
XLA Ops:
  0.6 1.2 convert_bitcast_fusion
  1.9 3.4 collective-permute-start
  5.3 5.7 %collective-permute-start.1 = (bf16[2,1,1]{2,1,0:T(2,128)(2,1)S(1)}, bf16[2,1,1]{2,1,0:T(2,128)(2,1)S(1)}, u32[]{:S(2)}, u32[]{:S(2)}) collective-permute-start(bf16[2,1,1]{2,1,0:T(2,128)(2,1)S(1)} %get-tuple-element.221), channel_id=1, source_target_pairs={{1,0},{2,1},{3,2},{4,3},{5,4},{6,5},{7,6},{8,7},{9,8},{10,9},{11,1... | collective-permute-start | bytes 20 | tf_op jit(solution)/shard_map/ppermute | solution.py:34
  11.5 1.3 fusion.81
  13.7 19.4 %all-to-all-start = ((s32[64,1,1]{2,1,0:T(1,128)}), s32[64,1,1]{2,1,0:T(1,128)S(1)}, u32[]{:S(2)}, u32[]{:S(2)}) async-start(s32[64,1,1]{2,1,0:T(1,128)} %copy.36), calls=%async_computation | async-start | bytes 65536 | tf_op jit(solution)/shard_map/all_to_all | solution.py:156
  34.3 1.7 fusion.80
  38.0 2.8 divide_dynamic-update-slice_fusion.3
  40.8 2.8 divide_dynamic-update-slice_fusion.2
  45.4 2.7 multiply_dynamic-update-slice_fusion.1
  48.1 2.8 divide_dynamic-update-slice_fusion.1
  50.9 2.8 divide_dynamic-update-slice_fusion
  53.8 1.9 copy.39
  55.6 1.6 reshape.1307
  58.0 2.7 multiply_dynamic-update-slice_fusion
  60.7 1.0 add_convert_fusion.2
  61.8 4.6 %dynamic-update-slice.10 = bf16[2,1,32770]{2,1,0:T(2,128)(2,1)S(1)} dynamic-update-slice(bf16[2,1,32770]{2,1,0:T(2,128)(2,1)S(1)} %dynamic-update-slice.9, bf16[2,1,32768]{2,1,0:T(2,128)(2,1)S(1)} %pad_maximum_fusion, s32[]{} %constant.251, s32[]{} %constant.251, s32[]{} %constant.252) | dynamic-update-slice | bytes 262148
  68.4 3.4 collective-permute-start.2
  71.8 2.5 collective-permute-start.3
  74.3 4.6 %dynamic-update-slice.7 = bf16[2,1,32770]{2,1,0:T(2,128)(2,1)S(1)} dynamic-update-slice(bf16[2,1,32770]{2,1,0:T(2,128)(2,1)S(1)} %dynamic-update-slice.6, bf16[2,1,32768]{2,1,0:T(2,128)(2,1)S(1)} %pad_maximum_fusion.1, s32[]{} %constant.251, s32[]{} %constant.251, s32[]{} %constant.252) | dynamic-update-slice | bytes 262148
  80.9 4.8 %collective-permute-start.4 = (bf16[2,1,1]{2,1,0:T(2,128)(2,1)S(1)}, bf16[2,1,1]{2,1,0:T(2,128)(2,1)S(1)}, u32[]{:S(2)}, u32[]{:S(2)}) collective-permute-start(bf16[2,1,1]{2,1,0:T(2,128)(2,1)S(1)} %get-tuple-element.218), channel_id=1, source_target_pairs={{0,1},{1,2},{2,3},{3,4},{4,5},{5,6},{6,7},{7,8},{8,9},{9,10},{10,1... | collective-permute-start | bytes 20 | tf_op jit(solution)/shard_map/ppermute | solution.py:32
  85.7 1.9 collective-permute-start.5
  87.7 4.6 %dynamic-update-slice.4 = bf16[2,1,32770]{2,1,0:T(2,128)(2,1)S(1)} dynamic-update-slice(bf16[2,1,32770]{2,1,0:T(2,128)(2,1)S(1)} %dynamic-update-slice.3, bf16[2,1,32768]{2,1,0:T(2,128)(2,1)S(1)} %pad_maximum_fusion.2, s32[]{} %constant.251, s32[]{} %constant.251, s32[]{} %constant.252) | dynamic-update-slice | bytes 262148
  92.3 4.9 %collective-permute-done.5 = bf16[2,1,1]{2,1,0:T(2,128)(2,1)S(1)} collective-permute-done((bf16[2,1,1]{2,1,0:T(2,128)(2,1)S(1)}, bf16[2,1,1]{2,1,0:T(2,128)(2,1)S(1)}, u32[]{:S(2)}, u32[]{:S(2)}) %collective-permute-start.5) | collective-permute-done | bytes 36 | tf_op jit(solution)/shard_map/ppermute | solution.py:34
  99.4 5.1 %collective-permute-start.6 = (bf16[2,1,1]{2,1,0:T(2,128)(2,1)S(1)}, bf16[2,1,1]{2,1,0:T(2,128)(2,1)S(1)}, u32[]{:S(2)}, u32[]{:S(2)}) collective-permute-start(bf16[2,1,1]{2,1,0:T(2,128)(2,1)S(1)} %get-tuple-element.216), channel_id=1, source_target_pairs={{0,1},{1,2},{2,3},{3,4},{4,5},{5,6},{6,7},{7,8},{8,9},{9,10},{10,1... | collective-permute-start | bytes 20 | tf_op jit(solution)/shard_map/ppermute | solution.py:32
  104.4 1.9 collective-permute-start.7
  106.4 4.6 %dynamic-update-slice.1 = bf16[2,1,32770]{2,1,0:T(2,128)(2,1)S(1)} dynamic-update-slice(bf16[2,1,32770]{2,1,0:T(2,128)(2,1)S(1)} %dynamic-update-slice, bf16[2,1,32768]{2,1,0:T(2,128)(2,1)S(1)} %pad_maximum_fusion.3, s32[]{} %constant.251, s32[]{} %constant.251, s32[]{} %constant.252) | dynamic-update-slice | bytes 262148
  111.0 4.9 %collective-permute-done.7 = bf16[2,1,1]{2,1,0:T(2,128)(2,1)S(1)} collective-permute-done((bf16[2,1,1]{2,1,0:T(2,128)(2,1)S(1)}, bf16[2,1,1]{2,1,0:T(2,128)(2,1)S(1)}, u32[]{:S(2)}, u32[]{:S(2)}) %collective-permute-start.7) | collective-permute-done | bytes 36 | tf_op jit(solution)/shard_map/ppermute | solution.py:34
  116.3 1.7 broadcast_in_dim.155
  118.0 4.6 %all-to-all-start.1 = ((bf16[8,2,6,4096]{3,1,2,0:T(2,128)(2,1)}), bf16[8,2,6,4096]{3,1,2,0:T(2,128)(2,1)S(1)}, u32[]{:S(2)}, u32[]{:S(2)}) async-start(bf16[8,2,6,4096]{3,1,2,0:T(2,128)(2,1)} %broadcast_in_dim.155), calls=%async_computation.1 | async-start | bytes 1572864 | tf_op jit(solution)/shard_map/all_to_all | solution.py:43
  122.7 1.2 clamp_reduce_fusion
  124.0 1.2 compare_reduce_fusion
  125.2 18.3 %all-to-all-done.1 = bf16[8,2,6,4096]{3,1,2,0:T(2,128)(2,1)S(1)} async-done(((bf16[8,2,6,4096]{3,1,2,0:T(2,128)(2,1)}), bf16[8,2,6,4096]{3,1,2,0:T(2,128)(2,1)S(1)}, u32[]{:S(2)}, u32[]{:S(2)}) %all-to-all-start.1) | async-done | bytes 786464 | tf_op jit(solution)/shard_map/all_to_all | solution.py:43
  144.0 2.8 gather_fusion
  146.8 4.0 %select_select_fusion = bf16[64,6,4096]{2,1,0:T(8,128)(2,1)} fusion(bf16[64,6,4096]{2,1,0:T(8,128)(2,1)} %gather_fusion, pred[64]{0:T(512)(128)(4,1)S(1)} %compare_and_fusion.1, pred[64]{0:T(512)(128)(4,1)S(1)} %compare_reduce_fusion), kind=kLoop, calls=%fused_computation.42 | loop fusion | flops 3145728 | bytes 6291584 | tf_op jit(solution)/shard_map/jit(_where)/select_n | solution.py:160
  150.8 25.0 %all-to-all-start.2 = ((bf16[64,6,4096]{2,1,0:T(8,128)(2,1)}), bf16[64,6,4096]{2,1,0:T(8,128)(2,1)}, u32[]{:S(2)}, u32[]{:S(2)}) async-start(bf16[64,6,4096]{2,1,0:T(8,128)(2,1)} %select_select_fusion), calls=%async_computation.2 | async-start | bytes 8388608 | tf_op jit(solution)/shard_map/all_to_all | solution.py:161
  176.5 101.5 %all-to-all-done.2 = bf16[64,6,4096]{2,1,0:T(8,128)(2,1)} async-done(((bf16[64,6,4096]{2,1,0:T(8,128)(2,1)}), bf16[64,6,4096]{2,1,0:T(8,128)(2,1)}, u32[]{:S(2)}, u32[]{:S(2)}) %all-to-all-start.2) | async-done | bytes 3145760 | tf_op jit(solution)/shard_map/all_to_all | solution.py:161
  277.9 4.2 %gather_fusion.1 = bf16[32,6,4096]{2,1,0:T(8,128)(2,1)} fusion(bf16[64,6,4096]{2,1,0:T(8,128)(2,1)} %all-to-all-done.2, s32[1024]{0:T(1024)S(1)} %pad_clamp_fusion), kind=kCustom, calls=%fused_computation.1 | custom fusion | bytes 3145856 | tf_op jit(solution)/shard_map/jit(_take)/gather | solution.py:162
  282.2 4.7 %gather.12 = bf16[16,2,384,64]{3,2,1,0:T(8,128)(2,1)S(1)} reshape(bf16[32,6,4096]{2,1,0:T(8,128)(2,1)} %gather_fusion.1) | data formatting | bytes 3145728 | tf_op jit(solution)/shard_map/jit(_take)/gather | solution.py:162
  286.9 2.0 broadcast_select_fusion
  288.9 3.3 copy.40
  292.3 47.4 %while.14 = (s32[]{:T(128)}, f32[16,2,6,1024]{3,2,1,0:T(8,128)S(1)}, s32[16,2]{1,0:T(8,128)S(1)}, bf16[16,2,384,64]{2,3,1,0:T(8,128)(2,1)S(1)}, s32[16,2,1024]{2...) while((s32[]{:T(128)}, ...), condition=%wide.region_4.5_spmd.clone.clone, body=%wide.region_2.4_spmd.clone.clone.sunk | while | flops 103727104 | bytes 7829657 | solution.py:117
  292.3 0.8 constant_dynamic-slice_fusion.4
  295.3 0.8 constant_dynamic-slice_fusion.4
  298.3 0.8 constant_dynamic-slice_fusion.4
  301.2 0.8 constant_dynamic-slice_fusion.4
  333.8 0.8 constant_dynamic-slice_fusion.4
  339.7 1.2 fusion.79
  341.1 1.0 multiply_subtract_fusion
  (222 shorter events, 53.8 us)
Async XLA Ops:
  0.6 66.9 %copy-start.1 = (f32[1,32768]{1,0:T(1,128)S(1)}, f32[1,32768]{1,0:T(1,128)}, u32[]{:S(2)}) copy-start(f32[1,32768]{1,0:T(1,128)} %param.16) | copy-start | bytes 393220
  1.9 59.8 %collective-permute-start = (bf16[2,1,1]{2,1,0:T(2,128)(2,1)S(1)}, bf16[2,1,1]{2,1,0:T(2,128)(2,1)S(1)}, u32[]{:S(2)}, u32[]{:S(2)}) collective-permute-start(bf16[2,1,1]{2,1,0:T(2,128)(2,1)S(1)} %get-tuple-element.222), channel_id=1, source_target_pairs={{0,1},{1,2},{2,3},{3,4},{4,5},{5,6},{6,7},{7,8},{8,9},{9,10},{10,1... | collective-permute-start | bytes 20 | tf_op jit(solution)/shard_map/ppermute | solution.py:32
  5.3 61.0 %collective-permute-start.1 = (bf16[2,1,1]{2,1,0:T(2,128)(2,1)S(1)}, bf16[2,1,1]{2,1,0:T(2,128)(2,1)S(1)}, u32[]{:S(2)}, u32[]{:S(2)}) collective-permute-start(bf16[2,1,1]{2,1,0:T(2,128)(2,1)S(1)} %get-tuple-element.221), channel_id=1, source_target_pairs={{1,0},{2,1},{3,2},{4,3},{5,4},{6,5},{7,6},{8,7},{9,8},{10,9},{11,1... | collective-permute-start | bytes 20 | tf_op jit(solution)/shard_map/ppermute | solution.py:34
  13.7 102.6 %all-to-all-start = ((s32[64,1,1]{2,1,0:T(1,128)}), s32[64,1,1]{2,1,0:T(1,128)S(1)}, u32[]{:S(2)}, u32[]{:S(2)}) async-start(s32[64,1,1]{2,1,0:T(1,128)} %copy.36), calls=%async_computation | async-start | bytes 65536 | tf_op jit(solution)/shard_map/all_to_all | solution.py:156
  68.4 5.9 %collective-permute-start.2 = (bf16[2,1,1]{2,1,0:T(2,128)(2,1)S(1)}, bf16[2,1,1]{2,1,0:T(2,128)(2,1)S(1)}, u32[]{:S(2)}, u32[]{:S(2)}) collective-permute-start(bf16[2,1,1]{2,1,0:T(2,128)(2,1)S(1)} %get-tuple-element.220), channel_id=1, source_target_pairs={{0,1},{1,2},{2,3},{3,4},{4,5},{5,6},{6,7},{7,8},{8,9},{9,10},{10,1... | collective-permute-start | bytes 20 | tf_op jit(solution)/shard_map/ppermute | solution.py:32
  71.8 7.1 %collective-permute-start.3 = (bf16[2,1,1]{2,1,0:T(2,128)(2,1)S(1)}, bf16[2,1,1]{2,1,0:T(2,128)(2,1)S(1)}, u32[]{:S(2)}, u32[]{:S(2)}) collective-permute-start(bf16[2,1,1]{2,1,0:T(2,128)(2,1)S(1)} %get-tuple-element.219), channel_id=1, source_target_pairs={{1,0},{2,1},{3,2},{4,3},{5,4},{6,5},{7,6},{8,7},{9,8},{10,9},{11,1... | collective-permute-start | bytes 20 | tf_op jit(solution)/shard_map/ppermute | solution.py:34
  80.9 6.7 %collective-permute-start.4 = (bf16[2,1,1]{2,1,0:T(2,128)(2,1)S(1)}, bf16[2,1,1]{2,1,0:T(2,128)(2,1)S(1)}, u32[]{:S(2)}, u32[]{:S(2)}) collective-permute-start(bf16[2,1,1]{2,1,0:T(2,128)(2,1)S(1)} %get-tuple-element.218), channel_id=1, source_target_pairs={{0,1},{1,2},{2,3},{3,4},{4,5},{5,6},{6,7},{7,8},{8,9},{9,10},{10,1... | collective-permute-start | bytes 20 | tf_op jit(solution)/shard_map/ppermute | solution.py:32
  85.7 11.5 %collective-permute-start.5 = (bf16[2,1,1]{2,1,0:T(2,128)(2,1)S(1)}, bf16[2,1,1]{2,1,0:T(2,128)(2,1)S(1)}, u32[]{:S(2)}, u32[]{:S(2)}) collective-permute-start(bf16[2,1,1]{2,1,0:T(2,128)(2,1)S(1)} %get-tuple-element.217), channel_id=1, source_target_pairs={{1,0},{2,1},{3,2},{4,3},{5,4},{6,5},{7,6},{8,7},{9,8},{10,9},{11,1... | collective-permute-start | bytes 20 | tf_op jit(solution)/shard_map/ppermute | solution.py:34
  99.4 7.0 %collective-permute-start.6 = (bf16[2,1,1]{2,1,0:T(2,128)(2,1)S(1)}, bf16[2,1,1]{2,1,0:T(2,128)(2,1)S(1)}, u32[]{:S(2)}, u32[]{:S(2)}) collective-permute-start(bf16[2,1,1]{2,1,0:T(2,128)(2,1)S(1)} %get-tuple-element.216), channel_id=1, source_target_pairs={{0,1},{1,2},{2,3},{3,4},{4,5},{5,6},{6,7},{7,8},{8,9},{9,10},{10,1... | collective-permute-start | bytes 20 | tf_op jit(solution)/shard_map/ppermute | solution.py:32
  104.4 11.5 %collective-permute-start.7 = (bf16[2,1,1]{2,1,0:T(2,128)(2,1)S(1)}, bf16[2,1,1]{2,1,0:T(2,128)(2,1)S(1)}, u32[]{:S(2)}, u32[]{:S(2)}) collective-permute-start(bf16[2,1,1]{2,1,0:T(2,128)(2,1)S(1)} %get-tuple-element.215), channel_id=1, source_target_pairs={{1,0},{2,1},{3,2},{4,3},{5,4},{6,5},{7,6},{8,7},{9,8},{10,9},{11,1... | collective-permute-start | bytes 20 | tf_op jit(solution)/shard_map/ppermute | solution.py:34
  118.0 25.5 %all-to-all-start.1 = ((bf16[8,2,6,4096]{3,1,2,0:T(2,128)(2,1)}), bf16[8,2,6,4096]{3,1,2,0:T(2,128)(2,1)S(1)}, u32[]{:S(2)}, u32[]{:S(2)}) async-start(bf16[8,2,6,4096]{3,1,2,0:T(2,128)(2,1)} %broadcast_in_dim.155), calls=%async_computation.1 | async-start | bytes 1572864 | tf_op jit(solution)/shard_map/all_to_all | solution.py:43
  150.8 127.2 %all-to-all-start.2 = ((bf16[64,6,4096]{2,1,0:T(8,128)(2,1)}), bf16[64,6,4096]{2,1,0:T(8,128)(2,1)}, u32[]{:S(2)}, u32[]{:S(2)}) async-start(bf16[64,6,4096]{2,1,0:T(8,128)(2,1)} %select_select_fusion), calls=%async_computation.2 | async-start | bytes 8388608 | tf_op jit(solution)/shard_map/all_to_all | solution.py:161
  288.9 3.4 copy-start
  292.3 48.8 %copy-start.2 = (f32[1,32768]{1,0:T(1,128)S(1)}, f32[1,32768]{1,0:T(1,128)}, u32[]{:S(2)}) copy-start(f32[1,32768]{1,0:T(1,128)} %param.17) | copy-start | bytes 393220
where the time goes:
time: 347 us; the launch traced here: 342 us
  waiting for transfers between devices  130 us (37%)
  starting transfers between devices  77.6 us (22%)
  other arithmetic  61 us (18%)
  local copies, waits for them, and re-layouts  57.9 us (17%)
  matrix products  9.95 us (3%)
  between operations  4.9 us (1%)
    all_to_all x1, waiting for transfers between devices, shards(): lax.all_to_all(picked, 'dom', split_axis=0, concat_axis=0, tiled=True)  101 us
    all_to_all x1, starting transfers between devices, shards(): lax.all_to_all(picked, 'dom', split_axis=0, concat_axis=0, tiled=True)  25 us
    unnamed x18, local copies, waits for them, and re-layouts  24.3 us
    all_to_all x1, starting transfers between devices, shards(): lax.all_to_all(request[:, None], 'dom', split_axis=0, concat_axis=0, tile...  19.4 us
    all_to_all x1, waiting for transfers between devices, from_everyone(): lax.all_to_all(jnp.broadcast_to(value[None], (length, *value.shape)), axi...  18.3 us
    ppermute x4, starting transfers between devices, extended(): lax.ppermute(tail, axis, [(i, (i + 1) % count) for i in range(ends)])  16.6 us
    unnamed x11, other arithmetic  15.1 us
    slice x16, local copies, waits for them, and re-layouts, one_block(): north_frac = frac_block[1][:, None, :]  13 us
  transfers between devices with their start and end apart: 11, of which 4 were waited for; matrix products, arithmetic and copies ran while one was open for 16% of the time, Pallas kernels for 0%

commit v1 on v0

v1 whole, which is shorter than its diff:
```python
import jax
import jax.numpy as jnp
from jax import lax
from jax.experimental import pallas as pl
from jax.experimental.pallas import tpu as pltpu
from jax.sharding import PartitionSpec as P

TILE = 64
TCOLS = 32
TILES_DEV = 2
FIELDS = 6
SWEEPS = 4
KAPPA = 0.08
NEED = 32
NPS = 1024
LANES = 128
GROUPS = NPS // LANES
N_OWN = 8
N_DOM = 64
BAND = TILES_DEV * N_DOM
CORES = 2
MSG = 16
DEAD_CELL = 0xFFC0
EDGE_SCALE = 2.0**29
FX_STEP = 2.0**-16
FY_TOP = 65535.0


SMALL = pltpu.CompilerParams(vmem_limit_bytes=8 * 2**20)


def iota(shape, dim):
    return lax.broadcasted_iota(jnp.int32, shape, dim)


def holland_kernel(place_ref, track_ref, background_ref, out_ref, rows_ref):
    field = iota((8, LANES), 0)
    lane = iota((8, LANES), 1)
    late = field >= 3
    centre_x, centre_y, deficit, max_radius, exponent = (
        jnp.where(late, track_ref[1, i], track_ref[0, i]) for i in range(5)
    )
    kind = jnp.where(late, field - 3, field)
    strength = exponent * deficit
    left = lane < TILE

    def one_field(tile, chunk):
        tile_index = place_ref[0] * TILES_DEV + tile
        north = (tile_index // TCOLS * TILE + 2 * chunk + lane // TILE).astype(jnp.float32)
        east = (tile_index % TCOLS * TILE + lane % TILE).astype(jnp.float32)
        offset_x = east - centre_x
        offset_y = north - centre_y
        radius = jnp.sqrt(offset_x * offset_x + offset_y * offset_y + 1.0)
        ratio = jnp.exp(exponent * jnp.log(max_radius / radius))
        decay = jnp.exp(-ratio)
        speed = jnp.sqrt(strength * ratio * decay)
        wind = speed * jnp.where(kind == 0, -offset_y, offset_x) / radius
        storm = jnp.where(kind == 2, -deficit * (1.0 - decay), wind)
        piece = background_ref[tile, :, pl.ds(pl.multiple_of(chunk * LANES, LANES), LANES)]
        return piece.astype(jnp.float32) + storm[:FIELDS]

    def step(chunk, carry):
        first = one_field(0, chunk)
        second = one_field(1, chunk)
        even = jnp.where(left[:FIELDS], first, pltpu.roll(second, TILE, 1))
        odd = jnp.where(left[:FIELDS], pltpu.roll(first, TILE, 1), second)
        rows_ref[pl.ds(2 * chunk, FIELDS, stride=TILE), :] = even
        rows_ref[pl.ds(2 * chunk + 1, FIELDS, stride=TILE), :] = odd
        return carry

    lax.fori_loop(0, TILE // 2, step, 0)
    out_ref[...] = rows_ref[...].astype(jnp.bfloat16)


def holland(place, storm_track, background):
    rows = FIELDS * TILE
    return pl.pallas_call(
        holland_kernel,
        out_shape=jax.ShapeDtypeStruct((rows, LANES), jnp.bfloat16),
        in_specs=[
            pl.BlockSpec(memory_space=pltpu.SMEM),
            pl.BlockSpec(memory_space=pltpu.SMEM),
            pl.BlockSpec(memory_space=pltpu.VMEM),
        ],
        out_specs=pl.BlockSpec(memory_space=pltpu.VMEM),
        scratch_shapes=[pltpu.VMEM((rows, LANES), jnp.float32)],
        compiler_params=SMALL,
    )(place, storm_track, background)


def column_code(fraction):
    scaled = fraction * 32768.0
    whole = jnp.floor(scaled)
    code = 2.0 * whole + jnp.where(scaled > whole, 1.0, 0.0)
    return jnp.minimum(code, 65535.0).astype(jnp.int32)


def row_code(fraction):
    return jnp.floor(fraction * FY_TOP + 0.5).astype(jnp.int32)


def edge_code(value):
    return jnp.floor(value * EDGE_SCALE + 0.5).astype(jnp.int32)


def query_kernel(
    need_ref, count_ref, cells_ref, fracs_ref, ehead_ref, etail_ref, bhead_ref, btail_ref, out_ref, stage_ref
):
    for g in range(GROUPS):
        span = slice(g * LANES, (g + 1) * LANES)
        word = cells_ref[:, span] | (column_code(fracs_ref[0, :, span]) << 16)
        stage_ref[pl.ds(g, NEED, stride=MSG), :] = word
    for g in range(GROUPS // 2):
        low = row_code(fracs_ref[1, :, g * LANES : (g + 1) * LANES])
        high = row_code(fracs_ref[1, :, NPS // 2 + g * LANES : NPS // 2 + (g + 1) * LANES])
        stage_ref[pl.ds(GROUPS + g, NEED, stride=MSG), :] = low | (high << 16)
    row = iota((8, LANES), 0)
    lane = iota((8, LANES), 1)
    position = row * LANES + lane
    surface = jnp.where(lane < SWEEPS, ehead_ref[0:1, :], etail_ref[7:8, :])
    bed = jnp.where(lane < SWEEPS, bhead_ref[0:1, :], btail_ref[7:8, :])
    plain = jnp.where(row == 5, edge_code(surface), jnp.where(row == 6, edge_code(bed), -1))

    def clear(d, carry):
        out_ref[d, 8:16, :] = plain
        return carry

    lax.fori_loop(0, N_DOM, clear, 0, unroll=8)

    def place(s, carry):
        tile = need_ref[0, s]
        count = count_ref[s]
        holder = tile % BAND // TILES_DEV
        header = (tile // BAND * TILES_DEV + tile % TILES_DEV) | (count << 16)
        start = pl.multiple_of(s * MSG, MSG)
        out_ref[holder, 0:8, :] = jnp.where(position < count, stage_ref[pl.ds(start, 8), :], DEAD_CELL)
        out_ref[holder, 8:16, :] = jnp.where(
            row < 4, stage_ref[pl.ds(start + 8, 8), :], jnp.where(row == 4, header, plain)
        )
        return carry

    lax.fori_loop(0, NEED, place, 0, unroll=4)


def queries(need_tiles, slot_count, node_cells, node_fracs, elevation, bed_level):
    last = elevation.shape[0] // 8 - 1
    head = pl.BlockSpec((8, LANES), lambda i: (0, 0))
    tail = pl.BlockSpec((8, LANES), lambda i: (last, 0))
    return pl.pallas_call(
        query_kernel,
        grid=(1,),
        out_shape=jax.ShapeDtypeStruct((N_DOM, MSG, LANES), jnp.int32),
        in_specs=[
            pl.BlockSpec(memory_space=pltpu.SMEM),
            pl.BlockSpec(memory_space=pltpu.SMEM),
            pl.BlockSpec(memory_space=pltpu.VMEM),
            pl.BlockSpec(memory_space=pltpu.VMEM),
            head,
            tail,
            head,
            tail,
        ],
        out_specs=pl.BlockSpec(memory_space=pltpu.VMEM),
        scratch_shapes=[pltpu.VMEM((NEED * MSG, LANES), jnp.int32)],
        compiler_params=SMALL,
    )(need_tiles, slot_count, node_cells, node_fracs, elevation, elevation, bed_level, bed_level)


CHUNK = 256


def interpolate_kernel(
    place_ref, header_ref, message_ref, near0, near1, near2, near3, far_ref, out_ref, tiles_ref, x_ref, y_ref, part_ref
):
    own = place_ref[0]
    for shift, ref in enumerate((near0, near1, near2, near3)):
        band = (own + N_OWN - CORES * shift) % N_OWN
        tiles_ref[2 * band] = ref[:, 0:TILE]
        tiles_ref[2 * band + 1] = ref[:, TILE : 2 * TILE]
        band = band + 1 - 2 * (band % CORES)
        tiles_ref[2 * band] = far_ref[shift, :, 0:TILE]
        tiles_ref[2 * band + 1] = far_ref[shift, :, TILE : 2 * TILE]
    spot = iota((TILE, CHUNK), 0).astype(jnp.float32)
    per_chunk = CHUNK // LANES

    def one_slot(s, carry):
        header = header_ref[s]

        @pl.when(header >= 0)
        def _():
            count = header >> 16
            word = message_ref[s, 0:8, :]
            cell = word & 0xFFFF
            x_ref[...] = (cell & (TILE - 1)).astype(jnp.float32) + lax.shift_right_logical(word, 16).astype(
                jnp.float32
            ) * FX_STEP
            pair = message_ref[s, 8:16, :]
            row = (cell // TILE).astype(jnp.float32)
            y_ref[0:4, :] = row[0:4] + (pair[0:4] & 0xFFFF).astype(jnp.float32) * (1.0 / FY_TOP)
            y_ref[4:8, :] = row[4:8] + lax.shift_right_logical(pair[0:4], 16).astype(jnp.float32) * (1.0 / FY_TOP)
            tile = tiles_ref[header & 0xFFFF]
            for c in range(NPS // CHUNK):

                @pl.when(c * CHUNK < count)
                def _():
                    g = c * per_chunk
                    x = jnp.concatenate([x_ref[g + i : g + i + 1, :] for i in range(per_chunk)], axis=1)
                    y = jnp.concatenate([y_ref[g + i : g + i + 1, :] for i in range(per_chunk)], axis=1)
                    columns = jnp.maximum(1.0 - jnp.abs(spot - x), 0.0).astype(jnp.bfloat16)
                    rows = jnp.maximum(1.0 - jnp.abs(spot - y), 0.0)
                    spread = jnp.dot(tile, columns, preferred_element_type=jnp.float32)
                    for f in range(FIELDS):
                        weighed = (spread[f * TILE : (f + 1) * TILE] * rows).reshape(TILE // 8, 8, CHUNK)
                        total = jnp.sum(weighed, axis=0)
                        for i in range(per_chunk):
                            at = (f * GROUPS + g + i) * 8
                            part_ref[at : at + 8, :] = total[:, i * LANES : (i + 1) * LANES]

                @pl.when(c * CHUNK >= count)
                def _():
                    for f in range(FIELDS):
                        at = (f * GROUPS + c * per_chunk) * 8
                        part_ref[at : at + 8 * per_chunk, :] = jnp.zeros((8 * per_chunk, LANES), jnp.float32)

            values = []
            for f in range(FIELDS):
                value = part_ref[pl.ds(f * 64, GROUPS, stride=8), :]
                for i in range(1, 8):
                    value = value + part_ref[pl.ds(f * 64 + i, GROUPS, stride=8), :]
                values.append(value)
            out_ref[s] = jnp.concatenate(values, axis=0).astype(jnp.bfloat16)

        return carry

    lax.fori_loop(0, N_DOM, one_slot, 0)


def interpolate(place, header, message, near, far):
    return pl.pallas_call(
        interpolate_kernel,
        out_shape=jax.ShapeDtypeStruct((N_DOM, FIELDS * GROUPS, LANES), jnp.bfloat16),
        in_specs=[pl.BlockSpec(memory_space=pltpu.SMEM)] * 2 + [pl.BlockSpec(memory_space=pltpu.VMEM)] * 6,
        out_specs=pl.BlockSpec(memory_space=pltpu.VMEM),
        scratch_shapes=[
            pltpu.VMEM((N_OWN * TILES_DEV, FIELDS * TILE, TILE), jnp.bfloat16),
            pltpu.VMEM((GROUPS, LANES), jnp.float32),
            pltpu.VMEM((GROUPS, LANES), jnp.float32),
            pltpu.VMEM((FIELDS * GROUPS * 8, LANES), jnp.float32),
        ],
        compiler_params=SMALL,
    )(place, header, message, *near, far)


def following(x, lane):
    moved = pltpu.roll(x, LANES - 1, 1)
    return jnp.where(lane == LANES - 1, pltpu.roll(moved, x.shape[0] - 1, 0), moved)


def preceding(x, lane):
    moved = pltpu.roll(x, 1, 1)
    return jnp.where(lane == 0, pltpu.roll(moved, 1, 0), moved)


def flux_kernel(place_ref, before_ref, after_ref, elevation_ref, bed_ref, out_ref):
    rows = elevation_ref.shape[0]
    lane8 = iota((8, LANES), 1)
    row8 = iota((8, LANES), 0)

    def ends(which):
        before = before_ref[0, which : which + 1, :].astype(jnp.float32) * (1.0 / EDGE_SCALE)
        after = after_ref[0, which : which + 1, :].astype(jnp.float32) * (1.0 / EDGE_SCALE)
        top = jnp.where((row8 == 7) & (lane8 >= LANES - SWEEPS), before, 0.0)
        bottom = jnp.where((row8 == 0) & (lane8 < SWEEPS), after, 0.0)
        return top, bottom

    surface_top, surface_bottom = ends(5)
    bed_top, bed_bottom = ends(6)
    surface = jnp.concatenate([surface_top, elevation_ref[...], surface_bottom], axis=0)
    bed = jnp.concatenate([bed_top, bed_ref[...], bed_bottom], axis=0)
    lane = iota(surface.shape, 1)
    node = iota(surface.shape, 0) * LANES + lane
    first_wall = jnp.where(place_ref[2] == 0, 8 * LANES - 1, -1)
    last_wall = jnp.where(place_ref[2] == N_DOM - 1, (8 + rows) * LANES - 1, -1)
    open_face = jnp.where((node == first_wall) | (node == last_wall), 0.0, KAPPA)
    for sweep_step in range(SWEEPS):
        wet = jnp.maximum(surface - bed, 0.0)
        drop = surface - following(surface, lane)
        upwind = jnp.where(drop >= 0.0, wet, following(wet, lane))
        flux = open_face * upwind * drop
        surface = surface - (flux - preceding(flux, lane))
    out_ref[...] = surface[8 : 8 + rows]


def flux_sweeps(place, message, elevation, bed_level):
    whole = pl.BlockSpec(elevation.shape, lambda i, place_ref: (0, 0))
    return pl.pallas_call(
        flux_kernel,
        out_shape=jax.ShapeDtypeStruct(elevation.shape, jnp.float32),
        grid_spec=pltpu.PrefetchScalarGridSpec(
            num_scalar_prefetch=1,
            grid=(1,),
            in_specs=[
                pl.BlockSpec((1, 8, LANES), lambda i, place_ref: (place_ref[0], 1, 0)),
                pl.BlockSpec((1, 8, LANES), lambda i, place_ref: (place_ref[1], 1, 0)),
                whole,
                whole,
            ],
            out_specs=whole,
        ),
        compiler_params=SMALL,
    )(place, message, message, elevation, bed_level)


SLOTS8 = 8


def finish_kernel(need_ref, returned_ref, surface_ref, bed_ref, forcing_ref, surge_ref, stage_ref):
    rows = FIELDS * GROUPS

    def eight_slots(b, carry):
        for i in range(SLOTS8):
            s = b * SLOTS8 + i
            block = returned_ref[need_ref[0, s] % BAND // TILES_DEV].astype(jnp.float32)
            stage_ref[i * rows : (i + 1) * rows, :] = block
            here = pl.ds(pl.multiple_of(s * GROUPS, GROUPS), GROUPS)
            surface = surface_ref[here, :]
            wet = jnp.minimum(jnp.maximum(surface - bed_ref[here, :], 0.0), 1.0)
            surge_ref[here, :] = surface - 0.5 * block[rows - GROUPS :] * wet
        slots = pl.ds(pl.multiple_of(b * SLOTS8, SLOTS8), SLOTS8)
        for f in range(FIELDS):
            for g in range(GROUPS):
                piece = stage_ref[pl.ds(f * GROUPS + g, SLOTS8, stride=rows), :]
                forcing_ref[f, slots, g * LANES : (g + 1) * LANES] = piece.astype(jnp.bfloat16)
        return carry

    lax.fori_loop(0, NEED // SLOTS8, eight_slots, 0)


def finish(need_tiles, returned, surface, bed_level):
    vmem = pl.BlockSpec(memory_space=pltpu.VMEM)
    return pl.pallas_call(
        finish_kernel,
        out_shape=(
            jax.ShapeDtypeStruct((FIELDS, NEED, NPS), jnp.bfloat16),
            jax.ShapeDtypeStruct(surface.shape, jnp.float32),
        ),
        in_specs=[pl.BlockSpec(memory_space=pltpu.SMEM), vmem, vmem, vmem],
        out_specs=(vmem, vmem),
        scratch_shapes=[pltpu.VMEM((SLOTS8 * FIELDS * GROUPS, LANES), jnp.float32)],
        compiler_params=SMALL,
    )(need_tiles, returned, surface, bed_level)


def exchange(blocks, axis):
    return lax.all_to_all(blocks, axis, split_axis=0, concat_axis=0, tiled=True)


def shards(
    background, storm_track, need_tiles, node_cells, node_fracs, slot_count, elevation, bed_level
):
    own = lax.axis_index("own")
    dom = lax.axis_index("dom")
    elevation = elevation.reshape(-1, LANES)
    bed_level = bed_level.reshape(-1, LANES)
    tiles = holland((own * N_DOM + dom)[None].astype(jnp.int32), storm_track, background)
    near = [tiles]
    for shift in range(CORES, N_OWN, CORES):
        near.append(lax.ppermute(tiles, "own", [(i, (i + shift) % N_OWN) for i in range(N_OWN)]))
    far = lax.ppermute(jnp.stack(near), "own", [(i, i ^ 1) for i in range(N_OWN)])
    question = queries(need_tiles, slot_count, node_cells, node_fracs, elevation, bed_level)
    message = exchange(question, "dom")
    answers = interpolate(own[None].astype(jnp.int32), message[:, 12, 0], message, near, far)
    returned = exchange(answers, "dom")
    place = jnp.stack([(dom - 1) % N_DOM, (dom + 1) % N_DOM, dom]).astype(jnp.int32)
    surface = flux_sweeps(place, message, elevation, bed_level)
    forcing, surge = finish(need_tiles, returned, surface, bed_level)
    return forcing.transpose(1, 0, 2), surge.reshape(1, -1)


def solution(mesh):
    placed = (
        P(("own", "dom"), None, None),
        P(),
        P(("own", "dom"), None),
        P(("own", "dom"), None),
        P(None, ("own", "dom"), None),
        P(("own", "dom")),
        P("own", "dom"),
        P("own", "dom"),
    )
    return jax.shard_map(
        shards,
        mesh=mesh,
        in_specs=placed,
        out_specs=(P(("own", "dom"), None, None), P("own", "dom")),
        check_vma=False,
    )
```

time: 347 us -> 122 us (0.35)
  the two profiles are of different devices: /device:TPU:2 before, /device:TPU:6 now
where the time goes in v1:
time: 122 us; the launch traced here: 120 us
  starting transfers between devices  52.4 us (43%)
  waiting for transfers between devices  33.1 us (27%)
  Pallas kernels  27.6 us (23%)
  local copies, waits for them, and re-layouts  6.29 us (5%)
    all_to_all x2, starting transfers between devices, exchange(): return lax.all_to_all(blocks, axis, split_axis=0, concat_axis=0, tiled=True)  40.3 us
    all_to_all x2, waiting for transfers between devices, exchange(): return lax.all_to_all(blocks, axis, split_axis=0, concat_axis=0, tiled=True)  23.1 us
    pallas_call x1, Pallas kernels, interpolate(): pl.pallas_call(interpolate_kernel, out_shape=jax.ShapeDtypeStruct((N_DOM,...  17.5 us
    ppermute x3, starting transfers between devices, shards(): lax.ppermute(tiles, 'own', [(i, (i + shift) % N_OWN) for i in range(N_OWN)])  10.1 us
    ppermute x3, waiting for transfers between devices, shards(): lax.ppermute(tiles, 'own', [(i, (i + shift) % N_OWN) for i in range(N_OWN)])  9.53 us
    unnamed x21, local copies, waits for them, and re-layouts  5.06 us
    pallas_call x1, Pallas kernels, holland(): pl.pallas_call(holland_kernel, out_shape=jax.ShapeDtypeStruct((rows, LANE...  5 us
  transfers between devices with their start and end apart: 6, of which 4 were waited for; matrix products, arithmetic and copies ran while one was open for 1% of the time, Pallas kernels for 5%

profile of v1, /device:TPU:6, one launch (start us, length us, event | category | flops | bytes accessed | tf_op | source)
XLA Modules:
  0.0 120.2 jit_solution(7802361239533032974)
XLA Ops:
  0.6 0.0 copy-start.6
  0.6 0.0 copy-start.8
  0.7 0.6 copy-done.6
  1.3 0.0 copy-done.8
  1.3 0.0 copy-start
  1.3 0.9 copy-done
  2.2 0.0 copy-start.2
  2.2 0.9 copy-done.2
  3.1 0.0 copy-start.4
  3.1 0.9 copy-done.4
  4.1 0.0 copy-start.5
  4.1 0.9 copy-done.5
  5.0 2.0 %shard_map.95 = s32[64,16,128]{2,1,0:T(8,128)} custom-call(s32[1,32]{1,0:T(1,128)S(1)} %copy-done.6, s32[32]{0:T(128)S(1)} %copy-done.8, s32[32,1024]{1,0:T(8,128)S(1)} %copy-done.5, f32[2,32,1024]{2,1,0:T(8,128)S(1)} %copy-done.4, f32[256,128]{1,0:T(8,128)S(1)} %bitcast.17, f32[256,128]{1,0:T(8,128)S(1)} %bitcast.18, f32[256,128]{1,0:T(8,128)S(1)} %bitcast.13, ...), custom_call_target="tpu_custom_call" | custom-call | tf_op jit(solution)/shard_map/pallas_call | solution.py:149
  6.9 0.0 copy-start.9
  6.9 19.2 %all-to-all-start = ((s32[64,16,128]{2,1,0:T(8,128)}), s32[64,16,128]{2,1,0:T(8,128)S(1)}, u32[]{:S(2)}, u32[]{:S(2)}) async-start(s32[64,16,128]{2,1,0:T(8,128)} %shard_map.95), calls=%async_computation | async-start | bytes 1048576 | tf_op jit(solution)/shard_map/all_to_all | solution.py:355
  26.1 0.0 copy-done.9
  26.1 0.1 copy.11.background_ref
  26.2 0.0 copy-start.7
  26.2 0.7 copy-done.7
  26.9 5.0 %shard_map.96.near0 = bf16[384,128]{1,0:T(8,128)(2,1)S(1)} custom-call(s32[1]{0:T(128)} %bitcast.3.place_ref, f32[2,5]{1,0:T(2,128)S(1)} %copy-done.7, bf16[2,6,4096]{2,1,0:T(8,128)(2,1)S(1)} %copy.11.background_ref), custom_call_target="tpu_custom_call" | custom-call | tf_op jit(solution)/shard_map/pallas_call | solution.py:77
  31.9 5.2 %collective-permute-start.2 = (bf16[384,128]{1,0:T(8,128)(2,1)S(1)}, bf16[384,128]{1,0:T(8,128)(2,1)S(1)}, u32[]{:S(2)}, u32[]{:S(2)}) collective-permute-start(bf16[384,128]{1,0:T(8,128)(2,1)S(1)} %shard_map.96.near0), channel_id=1, source_target_pairs={{0,384},{64,448},{128,0},{192,64},{256,128},{320,192},{384,256},{4... | collective-permute-start | bytes 294920 | tf_op jit(solution)/shard_map/ppermute | solution.py:368
  37.1 1.9 %collective-permute-start.1 = (bf16[384,128]{1,0:T(8,128)(2,1)S(1)}, bf16[384,128]{1,0:T(8,128)(2,1)S(1)}, u32[]{:S(2)}, u32[]{:S(2)}) collective-permute-start(bf16[384,128]{1,0:T(8,128)(2,1)S(1)} %shard_map.96.near0), channel_id=1, source_target_pairs={{0,256},{64,320},{128,384},{192,448},{256,0},{320,64},{384,128},{4... | collective-permute-start | bytes 294920 | tf_op jit(solution)/shard_map/ppermute | solution.py:368
  39.0 3.0 %collective-permute-start = (bf16[384,128]{1,0:T(8,128)(2,1)S(1)}, bf16[384,128]{1,0:T(8,128)(2,1)S(1)}, u32[]{:S(2)}, u32[]{:S(2)}) collective-permute-start(bf16[384,128]{1,0:T(8,128)(2,1)S(1)} %shard_map.96.near0), channel_id=1, source_target_pairs={{0,128},{64,192},{128,256},{192,320},{256,384},{320,448},{384,0},{... | collective-permute-start | bytes 294920 | tf_op jit(solution)/shard_map/ppermute | solution.py:368
  42.0 0.7 collective-permute-done.2.near3
  42.7 8.9 %collective-permute-done.1.near2 = bf16[384,128]{1,0:T(8,128)(2,1)S(1)} collective-permute-done((bf16[384,128]{1,0:T(8,128)(2,1)S(1)}, bf16[384,128]{1,0:T(8,128)(2,1)S(1)}, u32[]{:S(2)}, u32[]{:S(2)}) %collective-permute-start.1) | collective-permute-done | bytes 98336 | tf_op jit(solution)/shard_map/ppermute | solution.py:368
  51.6 0.0 collective-permute-done.near1
  51.6 0.1 pad_maximum_fusion
  51.6 1.9 %collective-permute-start.3 = (bf16[4,384,128]{2,1,0:T(8,128)(2,1)S(1)}, bf16[4,384,128]{2,1,0:T(8,128)(2,1)S(1)}, u32[]{:S(2)}, u32[]{:S(2)}) collective-permute-start(bf16[4,384,128]{2,1,0:T(8,128)(2,1)S(1)} %pad_maximum_fusion), channel_id=1, source_target_pairs={{0,64},{64,0},{128,192},{192,128},{256,320},{320,256},{384,448},{4... | collective-permute-start | bytes 1179656 | tf_op jit(solution)/shard_map/ppermute | solution.py:369
  53.6 0.0 all-to-all-done.message_ref.before_ref.after_ref
  53.6 1.2 %slice_reduce_fusion.header_ref = s32[64]{0:T(128)S(1)} fusion(s32[64,16,128]{2,1,0:T(8,128)S(1)} %all-to-all-done.message_ref.before_ref.after_ref), kind=kLoop, calls=%fused_computation.1 | loop fusion | bytes 512 | tf_op jit(solution)/shard_map/slice | solution.py:372
  54.8 0.5 collective-permute-done.3.far_ref
  55.2 17.5 %shard_map.97 = bf16[64,48,128]{2,1,0:T(8,128)(2,1)} custom-call(s32[1]{0:T(128)} %bitcast.place_ref, s32[64]{0:T(128)S(1)} %slice_reduce_fusion.header_ref, s32[64,16,128]{2,1,0:T(8,128)S(1)} %all-to-all-done.message_ref.before_ref.after_ref, bf16[384,128]{1,0:T(8,128)(2,1)S(1)} %shard_map.96.near0, bf16[384,128]{1,0:T(8,128)(2,1)S(1)} %collective-permute-done.near1, ...), custom_call_target="tpu_custom_call" | custom-call | tf_op jit(solution)/shard_map/pallas_call | solution.py:239
  72.8 0.0 copy-start.1
  72.8 0.0 copy-start.3
  72.8 21.1 %all-to-all-start.1 = ((bf16[64,48,128]{2,1,0:T(8,128)(2,1)}), bf16[64,48,128]{2,1,0:T(8,128)(2,1)S(1)}, u32[]{:S(2)}, u32[]{:S(2)}) async-start(bf16[64,48,128]{2,1,0:T(8,128)(2,1)} %shard_map.97), calls=%async_computation.1 | async-start | bytes 1572864 | tf_op jit(solution)/shard_map/all_to_all | solution.py:355
  93.9 0.1 pad_add_fusion.place_ref
  94.0 0.0 copy-done.1
  94.0 0.0 copy-done.3
  94.0 1.3 %shard_map.98.surface_ref = f32[256,128]{1,0:T(8,128)S(1)} custom-call(s32[3]{0:T(128)S(1)} %pad_add_fusion.place_ref, s32[64,16,128]{2,1,0:T(8,128)S(1)} %all-to-all-done.message_ref.before_ref.after_ref, s32[64,16,128]{2,1,0:T(8,128)S(1)} %all-to-all-done.message_ref.before_ref.after_ref, f32[256,128]{1,0:T(8,128)S(1)} %bitcast.19, f32[256,128]{1,0:T(8,128)S(1)} %bitcast.15), custom_call_target="tpu_custom_call" | custom-call | tf_op jit(solution)/shard_map/pallas_call | solution.py:296
  95.3 23.1 %all-to-all-done.1.returned_ref = bf16[64,48,128]{2,1,0:T(8,128)(2,1)S(1)} async-done(((bf16[64,48,128]{2,1,0:T(8,128)(2,1)}), bf16[64,48,128]{2,1,0:T(8,128)(2,1)S(1)}, u32[]{:S(2)}, u32[]{:S(2)}) %all-to-all-start.1) | async-done | bytes 786464 | tf_op jit(solution)/shard_map/all_to_all | solution.py:355
  118.4 1.8 %shard_map.99 = (bf16[6,32,1024]{2,1,0:T(8,128)(2,1)}, f32[256,128]{1,0:T(8,128)}) custom-call(s32[1,32]{1,0:T(1,128)S(1)} %copy-done.6, bf16[64,48,128]{2,1,0:T(8,128)(2,1)S(1)} %all-to-all-done.1.returned_ref, f32[256,128]{1,0:T(8,128)S(1)} %shard_map.98.surface_ref, f32[256,128]{1,0:T(8,128)S(1)} %bitcast.16), custom_call_target="tpu_custom_call" | custom-call | tf_op jit(solution)/shard_map/pallas_call | solution.py:341
Async XLA Ops:
  0.6 0.7 copy-start.6
  0.6 0.7 copy-start.8
  1.3 0.9 copy-start
  2.2 0.9 copy-start.2
  3.1 0.9 copy-start.4
  4.1 0.9 copy-start.5
  6.9 19.2 %copy-start.9 = (bf16[2,6,4096]{2,0,1:T(2,128)(2,1)S(1)}, bf16[2,6,4096]{2,0,1:T(2,128)(2,1)}, u32[]{:S(2)}) copy-start(bf16[2,6,4096]{2,0,1:T(2,128)(2,1)} %param.8) | copy-start | bytes 294916
  6.9 46.6 %all-to-all-start = ((s32[64,16,128]{2,1,0:T(8,128)}), s32[64,16,128]{2,1,0:T(8,128)S(1)}, u32[]{:S(2)}, u32[]{:S(2)}) async-start(s32[64,16,128]{2,1,0:T(8,128)} %shard_map.95), calls=%async_computation | async-start | bytes 1048576 | tf_op jit(solution)/shard_map/all_to_all | solution.py:355
  26.2 0.7 copy-start.7
  31.9 10.8 %collective-permute-start.2 = (bf16[384,128]{1,0:T(8,128)(2,1)S(1)}, bf16[384,128]{1,0:T(8,128)(2,1)S(1)}, u32[]{:S(2)}, u32[]{:S(2)}) collective-permute-start(bf16[384,128]{1,0:T(8,128)(2,1)S(1)} %shard_map.96.near0), channel_id=1, source_target_pairs={{0,384},{64,448},{128,0},{192,64},{256,128},{320,192},{384,256},{4... | collective-permute-start | bytes 294920 | tf_op jit(solution)/shard_map/ppermute | solution.py:368
  37.1 14.5 %collective-permute-start.1 = (bf16[384,128]{1,0:T(8,128)(2,1)S(1)}, bf16[384,128]{1,0:T(8,128)(2,1)S(1)}, u32[]{:S(2)}, u32[]{:S(2)}) collective-permute-start(bf16[384,128]{1,0:T(8,128)(2,1)S(1)} %shard_map.96.near0), channel_id=1, source_target_pairs={{0,256},{64,320},{128,384},{192,448},{256,0},{320,64},{384,128},{4... | collective-permute-start | bytes 294920 | tf_op jit(solution)/shard_map/ppermute | solution.py:368
  39.0 12.6 %collective-permute-start = (bf16[384,128]{1,0:T(8,128)(2,1)S(1)}, bf16[384,128]{1,0:T(8,128)(2,1)S(1)}, u32[]{:S(2)}, u32[]{:S(2)}) collective-permute-start(bf16[384,128]{1,0:T(8,128)(2,1)S(1)} %shard_map.96.near0), channel_id=1, source_target_pairs={{0,128},{64,192},{128,256},{192,320},{256,384},{320,448},{384,0},{... | collective-permute-start | bytes 294920 | tf_op jit(solution)/shard_map/ppermute | solution.py:368
  51.6 3.6 %collective-permute-start.3 = (bf16[4,384,128]{2,1,0:T(8,128)(2,1)S(1)}, bf16[4,384,128]{2,1,0:T(8,128)(2,1)S(1)}, u32[]{:S(2)}, u32[]{:S(2)}) collective-permute-start(bf16[4,384,128]{2,1,0:T(8,128)(2,1)S(1)} %pad_maximum_fusion), channel_id=1, source_target_pairs={{0,64},{64,0},{128,192},{192,128},{256,320},{320,256},{384,448},{4... | collective-permute-start | bytes 1179656 | tf_op jit(solution)/shard_map/ppermute | solution.py:369
  72.8 21.3 %copy-start.1 = (f32[1,32768]{1,0:T(1,128)S(1)}, f32[1,32768]{1,0:T(1,128)}, u32[]{:S(2)}) copy-start(f32[1,32768]{1,0:T(1,128)} %param.15) | copy-start | bytes 393220
  72.8 21.3 %copy-start.3 = (f32[1,32768]{1,0:T(1,128)S(1)}, f32[1,32768]{1,0:T(1,128)}, u32[]{:S(2)}) copy-start(f32[1,32768]{1,0:T(1,128)} %param.14) | copy-start | bytes 393220
  72.8 45.6 %all-to-all-start.1 = ((bf16[64,48,128]{2,1,0:T(8,128)(2,1)}), bf16[64,48,128]{2,1,0:T(8,128)(2,1)S(1)}, u32[]{:S(2)}, u32[]{:S(2)}) async-start(bf16[64,48,128]{2,1,0:T(8,128)(2,1)} %shard_map.97), calls=%async_computation.1 | async-start | bytes 1572864 | tf_op jit(solution)/shard_map/all_to_all | solution.py:355

commit v2 on v1

--- a/solution.py
+++ b/solution.py
@@ -18,7 +18,6 @@
 N_OWN = 8
 N_DOM = 64
 BAND = TILES_DEV * N_DOM
-CORES = 2
 MSG = 16
 DEAD_CELL = 0xFFC0
 EDGE_SCALE = 2.0**29
@@ -68,7 +67,7 @@
         rows_ref[pl.ds(2 * chunk + 1, FIELDS, stride=TILE), :] = odd
         return carry
 
-    lax.fori_loop(0, TILE // 2, step, 0)
+    lax.fori_loop(0, TILE // 2, step, 0, unroll=4)
     out_ref[...] = rows_ref[...].astype(jnp.bfloat16)
 
 
@@ -162,84 +161,85 @@
         ],
         out_specs=pl.BlockSpec(memory_space=pltpu.VMEM),
         scratch_shapes=[pltpu.VMEM((NEED * MSG, LANES), jnp.int32)],
-        compiler_params=SMALL,
     )(need_tiles, slot_count, node_cells, node_fracs, elevation, elevation, bed_level, bed_level)
 
 
 CHUNK = 256
-
-
-def interpolate_kernel(
-    place_ref, header_ref, message_ref, near0, near1, near2, near3, far_ref, out_ref, tiles_ref, x_ref, y_ref, part_ref
-):
-    own = place_ref[0]
-    for shift, ref in enumerate((near0, near1, near2, near3)):
-        band = (own + N_OWN - CORES * shift) % N_OWN
-        tiles_ref[2 * band] = ref[:, 0:TILE]
-        tiles_ref[2 * band + 1] = ref[:, TILE : 2 * TILE]
-        band = band + 1 - 2 * (band % CORES)
-        tiles_ref[2 * band] = far_ref[shift, :, 0:TILE]
-        tiles_ref[2 * band + 1] = far_ref[shift, :, TILE : 2 * TILE]
-    spot = iota((TILE, CHUNK), 0).astype(jnp.float32)
-    per_chunk = CHUNK // LANES
-
-    def one_slot(s, carry):
+PER_CHUNK = CHUNK // LANES
+CHUNKS = NPS // CHUNK
+
+
+def interpolate_kernel(header_ref, message_ref, column_ref, out_ref, tiles_ref, x_ref, y_ref, part_ref):
+    for k in range(N_OWN):
+        tiles_ref[2 * k] = column_ref[k, :, 0:TILE]
+        tiles_ref[2 * k + 1] = column_ref[k, :, TILE : 2 * TILE]
+    spot = iota((TILE, LANES), 0).astype(jnp.float32)
+
+    def add_up(slot):
+        values = []
+        for f in range(FIELDS):
+            pieces = [part_ref[pl.ds(f * 64 + i, GROUPS, stride=8), :] for i in range(8)]
+            while len(pieces) > 1:
+                pieces = [a + b for a, b in zip(pieces[::2], pieces[1::2])]
+            values.append(pieces[0])
+        out_ref[slot] = jnp.concatenate(values, axis=0).astype(jnp.bfloat16)
+
+    def hat(ref, g):
+        return jnp.maximum(1.0 - jnp.abs(spot - ref[g : g + 1, :]), 0.0)
+
+    def one_slot(s, header, before, live):
+        add_up(before)
+        word = message_ref[s, 0:8, :]
+        pair = message_ref[s, 8:16, :]
+        cell = word & 0xFFFF
+        row = (cell // TILE).astype(jnp.float32)
+        low = (pair[0:4] & 0xFFFF).astype(jnp.float32)
+        high = lax.shift_right_logical(pair[0:4], 16).astype(jnp.float32)
+        x_ref[...] = (cell & (TILE - 1)).astype(jnp.float32) + lax.shift_right_logical(word, 16).astype(
+            jnp.float32
+        ) * FX_STEP
+        y_ref[0:4, :] = row[0:4] + low * (1.0 / FY_TOP)
+        y_ref[4:8, :] = row[4:8] + high * (1.0 / FY_TOP)
+        tile = tiles_ref[header & 0xFFFF]
+        for c in range(live):
+            g = c * PER_CHUNK
+            groups = range(g, g + PER_CHUNK)
+            columns = jnp.concatenate([hat(x_ref, i).astype(jnp.bfloat16) for i in groups], axis=1)
+            spread = jnp.dot(tile, columns, preferred_element_type=jnp.float32)
+            for i in groups:
+                rows = hat(y_ref, i)
+                lanes = slice((i - g) * LANES, (i - g + 1) * LANES)
+                for f in range(FIELDS):
+                    weighed = (spread[f * TILE : (f + 1) * TILE, lanes] * rows).reshape(TILE // 8, 8, LANES)
+                    at = (f * GROUPS + i) * 8
+                    part_ref[at : at + 8, :] = jnp.sum(weighed, axis=0)
+        dead = (CHUNKS - live) * PER_CHUNK * 8
+        if dead:
+            for f in range(FIELDS):
+                at = (f + 1) * GROUPS * 8 - dead
+                part_ref[at : at + dead, :] = jnp.zeros((dead, LANES), jnp.float32)
+
+    def step(s, last):
         header = header_ref[s]
-
-        @pl.when(header >= 0)
-        def _():
-            count = header >> 16
-            word = message_ref[s, 0:8, :]
-            cell = word & 0xFFFF
-            x_ref[...] = (cell & (TILE - 1)).astype(jnp.float32) + lax.shift_right_logical(word, 16).astype(
-                jnp.float32
-            ) * FX_STEP
-            pair = message_ref[s, 8:16, :]
-            row = (cell // TILE).astype(jnp.float32)
-            y_ref[0:4, :] = row[0:4] + (pair[0:4] & 0xFFFF).astype(jnp.float32) * (1.0 / FY_TOP)
-            y_ref[4:8, :] = row[4:8] + lax.shift_right_logical(pair[0:4], 16).astype(jnp.float32) * (1.0 / FY_TOP)
-            tile = tiles_ref[header & 0xFFFF]
-            for c in range(NPS // CHUNK):
-
-                @pl.when(c * CHUNK < count)
-                def _():
-                    g = c * per_chunk
-                    x = jnp.concatenate([x_ref[g + i : g + i + 1, :] for i in range(per_chunk)], axis=1)
-                    y = jnp.concatenate([y_ref[g + i : g + i + 1, :] for i in range(per_chunk)], axis=1)
-                    columns = jnp.maximum(1.0 - jnp.abs(spot - x), 0.0).astype(jnp.bfloat16)
-                    rows = jnp.maximum(1.0 - jnp.abs(spot - y), 0.0)
-                    spread = jnp.dot(tile, columns, preferred_element_type=jnp.float32)
-                    for f in range(FIELDS):
-                        weighed = (spread[f * TILE : (f + 1) * TILE] * rows).reshape(TILE // 8, 8, CHUNK)
-                        total = jnp.sum(weighed, axis=0)
-                        for i in range(per_chunk):
-                            at = (f * GROUPS + g + i) * 8
-                            part_ref[at : at + 8, :] = total[:, i * LANES : (i + 1) * LANES]
-
-                @pl.when(c * CHUNK >= count)
-                def _():
-                    for f in range(FIELDS):
-                        at = (f * GROUPS + c * per_chunk) * 8
-                        part_ref[at : at + 8 * per_chunk, :] = jnp.zeros((8 * per_chunk, LANES), jnp.float32)
-
-            values = []
-            for f in range(FIELDS):
-                value = part_ref[pl.ds(f * 64, GROUPS, stride=8), :]
-                for i in range(1, 8):
-                    value = value + part_ref[pl.ds(f * 64 + i, GROUPS, stride=8), :]
-                values.append(value)
-            out_ref[s] = jnp.concatenate(values, axis=0).astype(jnp.bfloat16)
-
-        return carry
-
-    lax.fori_loop(0, N_DOM, one_slot, 0)
-
-
-def interpolate(place, header, message, near, far):
+        live = jnp.maximum(((header >> 16) + CHUNK - 1) // CHUNK, 2)
+        before = jnp.where(last < 0, s, last)
+        for m in range(2, CHUNKS + 1):
+
+            @pl.when((header >= 0) & (live == m))
+            def _():
+                one_slot(s, header, before, m)
+
+        return jnp.where(header >= 0, s, last)
+
+    last = lax.fori_loop(0, N_DOM, step, -1)
+    add_up(jnp.maximum(last, 0))
+
+
+def interpolate(header, message, column):
     return pl.pallas_call(
         interpolate_kernel,
         out_shape=jax.ShapeDtypeStruct((N_DOM, FIELDS * GROUPS, LANES), jnp.bfloat16),
-        in_specs=[pl.BlockSpec(memory_space=pltpu.SMEM)] * 2 + [pl.BlockSpec(memory_space=pltpu.VMEM)] * 6,
+        in_specs=[pl.BlockSpec(memory_space=pltpu.SMEM)] + [pl.BlockSpec(memory_space=pltpu.VMEM)] * 2,
         out_specs=pl.BlockSpec(memory_space=pltpu.VMEM),
         scratch_shapes=[
             pltpu.VMEM((N_OWN * TILES_DEV, FIELDS * TILE, TILE), jnp.bfloat16),
@@ -248,7 +248,7 @@
             pltpu.VMEM((FIELDS * GROUPS * 8, LANES), jnp.float32),
         ],
         compiler_params=SMALL,
-    )(place, header, message, *near, far)
+    )(header, message, column)
 
 
 def following(x, lane):
@@ -363,13 +363,10 @@
     elevation = elevation.reshape(-1, LANES)
     bed_level = bed_level.reshape(-1, LANES)
     tiles = holland((own * N_DOM + dom)[None].astype(jnp.int32), storm_track, background)
-    near = [tiles]
-    for shift in range(CORES, N_OWN, CORES):
-        near.append(lax.ppermute(tiles, "own", [(i, (i + shift) % N_OWN) for i in range(N_OWN)]))
-    far = lax.ppermute(jnp.stack(near), "own", [(i, i ^ 1) for i in range(N_OWN)])
+    column = lax.all_gather(tiles, "own")
     question = queries(need_tiles, slot_count, node_cells, node_fracs, elevation, bed_level)
     message = exchange(question, "dom")
-    answers = interpolate(own[None].astype(jnp.int32), message[:, 12, 0], message, near, far)
+    answers = interpolate(message[:, 12, 0], message, column)
     returned = exchange(answers, "dom")
     place = jnp.stack([(dom - 1) % N_DOM, (dom + 1) % N_DOM, dom]).astype(jnp.int32)
     surface = flux_sweeps(place, message, elevation, bed_level)

time: 122 us -> 106 us (0.87)
  blocking collectives: 0 us -> 23.9 us
  starting transfers between devices: 52.4 us -> 29.5 us
  waiting for transfers between devices: 33.1 us -> 25.2 us
  local copies, waits for them, and re-layouts: 6.29 us -> 1.97 us
  Pallas kernels: 27.6 us -> 23.4 us
    all_gather x0 -> x1, blocking collectives: none -> 23.9 us  [shards(): column = lax.all_gather(tiles, 'own')]
    ppermute x4 -> x0, starting transfers between devices: 12.1 us -> none  [the longest x3 10.1 us: shards(): lax.ppermute(tiles, 'own', [(i, (i + shift) % N_OWN) for i in range(N_OWN)])]
    all_to_all x2, starting transfers between devices: 40.3 us -> 29.5 us  [exchange(): return lax.all_to_all(blocks, axis, split_axis=0, concat_axis=0, tiled=True)]
    ppermute x4 -> x0, waiting for transfers between devices: 9.99 us -> none  [the longest x3 9.53 us: shards(): lax.ppermute(tiles, 'own', [(i, (i + shift) % N_OWN) for i in range(N_OWN)])]
    unnamed x21 -> x11, local copies, waits for them, and re-layouts: 5.06 us -> 0.75 us
    pallas_call x1, Pallas kernels: 5 us -> 1.83 us  [holland(): pl.pallas_call(holland_kernel, out_shape=jax.ShapeDtypeStruct((rows, LANE...]
    all_to_all x2, waiting for transfers between devices: 23.1 us -> 25.2 us  [exchange(): return lax.all_to_all(blocks, axis, split_axis=0, concat_axis=0, tiled=True)]
    pallas_call x1, Pallas kernels: 17.5 us -> 16 us  [interpolate(): pl.pallas_call(interpolate_kernel, out_shape=jax.ShapeDtypeStruct((N_DOM,...]
  transfers between devices with their start and end apart: 6 -> 2, of which waited for: 4 -> 1; matrix products, arithmetic and copies ran while one was open for 1% -> 0% of each run, Pallas kernels for 5% -> 3%
where the time goes in v2:
time: 106 us; the launch traced here: 105 us
  starting transfers between devices  29.5 us (28%)
  waiting for transfers between devices  25.2 us (24%)
  blocking collectives  23.9 us (23%)
  Pallas kernels  23.4 us (22%)
  local copies, waits for them, and re-layouts  1.97 us (2%)
    all_to_all x2, starting transfers between devices, exchange(): return lax.all_to_all(blocks, axis, split_axis=0, concat_axis=0, tiled=True)  29.5 us
    all_to_all x2, waiting for transfers between devices, exchange(): return lax.all_to_all(blocks, axis, split_axis=0, concat_axis=0, tiled=True)  25.2 us
    all_gather x1, blocking collectives, shards(): column = lax.all_gather(tiles, 'own')  23.9 us
    pallas_call x1, Pallas kernels, interpolate(): pl.pallas_call(interpolate_kernel, out_shape=jax.ShapeDtypeStruct((N_DOM,...  16 us
    pallas_call x1, Pallas kernels, queries(): pl.pallas_call(query_kernel, grid=(1,), out_shape=jax.ShapeDtypeStruct((N...  2.43 us
  transfers between devices with their start and end apart: 2, of which 1 were waited for; matrix products, arithmetic and copies ran while one was open for 0% of the time, Pallas kernels for 3%

profile of v2, /device:TPU:6, one launch (start us, length us, event | category | flops | bytes accessed | tf_op | source)
XLA Modules:
  0.0 104.8 jit_solution(7563559073907481970)
XLA Ops:
  0.6 2.4 %shard_map.95 = s32[64,16,128]{2,1,0:T(8,128)} custom-call(s32[1,32]{1,0:T(1,128)} %need_ref.3, s32[32]{0:T(128)} %count_ref.1, s32[32,1024]{1,0:T(8,128)} %cells_ref.1, f32[2,32,1024]{2,1,0:T(8,128)} %fracs_ref.1, f32[256,128]{1,0:T(8,128)} %bitcast.14, f32[256,128]{1,0:T(8,128)} %bitcast.15, f32[256,128]{1,0:T(8,128)} %bitcast.10, f32[256,128]{1,0:T(8,128)} %bitcast.11), custom_call_target="tpu_custom_call" | custom-call | tf_op jit(solution)/shard_map/pallas_call | solution.py:148
  3.1 0.0 copy-start.4
  3.1 19.2 %all-to-all-start = ((s32[64,16,128]{2,1,0:T(8,128)}), s32[64,16,128]{2,1,0:T(8,128)S(1)}, u32[]{:S(2)}, u32[]{:S(2)}) async-start(s32[64,16,128]{2,1,0:T(8,128)} %shard_map.95), calls=%async_computation | async-start | bytes 1048576 | tf_op jit(solution)/shard_map/all_to_all | solution.py:355
  22.2 0.0 copy-done.4
  22.3 0.1 copy.11.background_ref
  22.3 0.0 copy-start.3
  22.3 0.7 copy-done.3
  23.0 1.8 %shard_map.96 = bf16[384,128]{1,0:T(8,128)(2,1)S(1)} custom-call(s32[1]{0:T(128)} %bitcast.2.place_ref, f32[2,5]{1,0:T(2,128)S(1)} %copy-done.3, bf16[2,6,4096]{2,1,0:T(8,128)(2,1)S(1)} %copy.11.background_ref), custom_call_target="tpu_custom_call" | custom-call | tf_op jit(solution)/shard_map/pallas_call | solution.py:76
  24.9 23.9 %all-gather = bf16[3072,128]{1,0:T(8,128)(2,1)S(1)} all-gather(bf16[384,128]{1,0:T(8,128)(2,1)S(1)} %shard_map.96), channel_id=2, replica_groups=mesh['own'=8,'dom'=64] {'own'}, dimensions={0}, use_global_device_ids=true | all-gather | bytes 884736 | tf_op jit(solution)/shard_map/all_gather | solution.py:366
  48.8 0.0 all-to-all-done.message_ref.before_ref.after_ref
  48.8 1.2 %slice_reduce_fusion.header_ref = s32[64]{0:T(128)S(1)} fusion(s32[64,16,128]{2,1,0:T(8,128)S(1)} %all-to-all-done.message_ref.before_ref.after_ref), kind=kLoop, calls=%fused_computation | loop fusion | bytes 512 | tf_op jit(solution)/shard_map/slice | solution.py:369
  50.0 16.0 %shard_map.97 = bf16[64,48,128]{2,1,0:T(8,128)(2,1)} custom-call(s32[64]{0:T(128)S(1)} %slice_reduce_fusion.header_ref, s32[64,16,128]{2,1,0:T(8,128)S(1)} %all-to-all-done.message_ref.before_ref.after_ref, bf16[8,384,128]{2,1,0:T(8,128)(2,1)S(1)} %bitcast.9), custom_call_target="tpu_custom_call" | custom-call | tf_op jit(solution)/shard_map/pallas_call | solution.py:239
  66.0 0.0 copy-start
  66.0 0.0 copy-start.1
  66.0 10.3 %all-to-all-start.1 = ((bf16[64,48,128]{2,1,0:T(8,128)(2,1)}), bf16[64,48,128]{2,1,0:T(8,128)(2,1)S(1)}, u32[]{:S(2)}, u32[]{:S(2)}) async-start(bf16[64,48,128]{2,1,0:T(8,128)(2,1)} %shard_map.97), calls=%async_computation.1 | async-start | bytes 1572864 | tf_op jit(solution)/shard_map/all_to_all | solution.py:355
  76.4 0.1 pad_add_fusion.place_ref
  76.4 0.0 copy-done
  76.4 0.0 copy-done.1
  76.4 0.0 copy-start.2
  76.5 1.3 %shard_map.98.surface_ref = f32[256,128]{1,0:T(8,128)S(1)} custom-call(s32[3]{0:T(128)S(1)} %pad_add_fusion.place_ref, s32[64,16,128]{2,1,0:T(8,128)S(1)} %all-to-all-done.message_ref.before_ref.after_ref, s32[64,16,128]{2,1,0:T(8,128)S(1)} %all-to-all-done.message_ref.before_ref.after_ref, f32[256,128]{1,0:T(8,128)S(1)} %bitcast.16, f32[256,128]{1,0:T(8,128)S(1)} %bitcast.12), custom_call_target="tpu_custom_call" | custom-call | tf_op jit(solution)/shard_map/pallas_call | solution.py:296
  77.8 25.2 %all-to-all-done.1.returned_ref = bf16[64,48,128]{2,1,0:T(8,128)(2,1)S(1)} async-done(((bf16[64,48,128]{2,1,0:T(8,128)(2,1)}), bf16[64,48,128]{2,1,0:T(8,128)(2,1)S(1)}, u32[]{:S(2)}, u32[]{:S(2)}) %all-to-all-start.1) | async-done | bytes 786464 | tf_op jit(solution)/shard_map/all_to_all | solution.py:355
  103.0 0.0 copy-done.2
  103.0 1.8 %shard_map.99 = (bf16[6,32,1024]{2,1,0:T(8,128)(2,1)}, f32[256,128]{1,0:T(8,128)}) custom-call(s32[1,32]{1,0:T(1,128)S(1)} %copy-done.2, bf16[64,48,128]{2,1,0:T(8,128)(2,1)S(1)} %all-to-all-done.1.returned_ref, f32[256,128]{1,0:T(8,128)S(1)} %shard_map.98.surface_ref, f32[256,128]{1,0:T(8,128)S(1)} %bitcast.13), custom_call_target="tpu_custom_call" | custom-call | tf_op jit(solution)/shard_map/pallas_call | solution.py:341
Async XLA Ops:
  3.1 19.2 %copy-start.4 = (bf16[2,6,4096]{2,0,1:T(2,128)(2,1)S(1)}, bf16[2,6,4096]{2,0,1:T(2,128)(2,1)}, u32[]{:S(2)}) copy-start(bf16[2,6,4096]{2,0,1:T(2,128)(2,1)} %param.8) | copy-start | bytes 294916
  3.1 45.7 %all-to-all-start = ((s32[64,16,128]{2,1,0:T(8,128)}), s32[64,16,128]{2,1,0:T(8,128)S(1)}, u32[]{:S(2)}, u32[]{:S(2)}) async-start(s32[64,16,128]{2,1,0:T(8,128)} %shard_map.95), calls=%async_computation | async-start | bytes 1048576 | tf_op jit(solution)/shard_map/all_to_all | solution.py:355
  22.3 0.7 copy-start.3
  66.0 10.4 %copy-start = (f32[1,32768]{1,0:T(1,128)S(1)}, f32[1,32768]{1,0:T(1,128)}, u32[]{:S(2)}) copy-start(f32[1,32768]{1,0:T(1,128)} %param.15) | copy-start | bytes 393220
  66.0 10.4 %copy-start.1 = (f32[1,32768]{1,0:T(1,128)S(1)}, f32[1,32768]{1,0:T(1,128)}, u32[]{:S(2)}) copy-start(f32[1,32768]{1,0:T(1,128)} %param.14) | copy-start | bytes 393220
  66.0 37.0 %all-to-all-start.1 = ((bf16[64,48,128]{2,1,0:T(8,128)(2,1)}), bf16[64,48,128]{2,1,0:T(8,128)(2,1)S(1)}, u32[]{:S(2)}, u32[]{:S(2)}) async-start(bf16[64,48,128]{2,1,0:T(8,128)(2,1)} %shard_map.97), calls=%async_computation.1 | async-start | bytes 1572864 | tf_op jit(solution)/shard_map/all_to_all | solution.py:355
  76.4 26.6 %copy-start.2 = (s32[1,32]{1,0:T(1,128)S(1)}, s32[1,32]{1,0:T(1,128)}, u32[]{:S(2)}) copy-start(s32[1,32]{1,0:T(1,128)} %need_ref.3) | copy-start | bytes 388

commit v3 on v2

v3 whole, which is shorter than its diff:
```python
import jax
import jax.numpy as jnp
from jax import lax
from jax.experimental import pallas as pl
from jax.experimental.pallas import tpu as pltpu
from jax.sharding import PartitionSpec as P

TILE = 64
TCOLS = 32
TILES_DEV = 2
FIELDS = 6
SWEEPS = 4
KAPPA = 0.08
NEED = 32
NPS = 1024
LANES = 128
GROUPS = NPS // LANES
N_OWN = 8
N_DOM = 64
BAND = TILES_DEV * N_DOM
CORES = 2
MSG = 16
CHUNK = 256
PER_CHUNK = CHUNK // LANES
CHUNKS = NPS // CHUNK
FIELD_BITS = 10
ABSENT = (CHUNKS - 1) * FIELD_BITS << 16
LIST = 8 * FIELD_BITS
DEAD_CELL = 0xFFC0
EDGE_SCALE = 2.0**29
FX_STEP = 2.0**-16
FY_TOP = 65535.0


SMALL = pltpu.CompilerParams(vmem_limit_bytes=8 * 2**20)


def iota(shape, dim):
    return lax.broadcasted_iota(jnp.int32, shape, dim)


def storm_field(place_ref, track_ref, background_ref, out_ref, rows_ref):
    field = iota((8, LANES), 0)
    lane = iota((8, LANES), 1)
    late = field >= 3
    centre_x, centre_y, deficit, max_radius, exponent = (
        jnp.where(late, track_ref[1, i], track_ref[0, i]) for i in range(5)
    )
    kind = jnp.where(late, field - 3, field)
    strength = exponent * deficit
    left = lane < TILE

    def one_field(tile, chunk):
        tile_index = place_ref[0] * TILES_DEV + tile
        north = (tile_index // TCOLS * TILE + 2 * chunk + lane // TILE).astype(jnp.float32)
        east = (tile_index % TCOLS * TILE + lane % TILE).astype(jnp.float32)
        offset_x = east - centre_x
        offset_y = north - centre_y
        radius = jnp.sqrt(offset_x * offset_x + offset_y * offset_y + 1.0)
        ratio = jnp.exp(exponent * jnp.log(max_radius / radius))
        decay = jnp.exp(-ratio)
        speed = jnp.sqrt(strength * ratio * decay)
        wind = speed * jnp.where(kind == 0, -offset_y, offset_x) / radius
        storm = jnp.where(kind == 2, -deficit * (1.0 - decay), wind)
        piece = background_ref[:, tile, pl.ds(pl.multiple_of(chunk * LANES, LANES), LANES)]
        return piece.astype(jnp.float32) + storm[:FIELDS]

    def step(chunk, carry):
        first = one_field(0, chunk)
        second = one_field(1, chunk)
        even = jnp.where(left[:FIELDS], first, pltpu.roll(second, TILE, 1))
        odd = jnp.where(left[:FIELDS], pltpu.roll(first, TILE, 1), second)
        rows_ref[pl.ds(2 * chunk, FIELDS, stride=TILE), :] = even
        rows_ref[pl.ds(2 * chunk + 1, FIELDS, stride=TILE), :] = odd
        return carry

    lax.fori_loop(0, TILE // 2, step, 0, unroll=4)
    out_ref[...] = rows_ref[...].astype(jnp.bfloat16)


def column_code(fraction):
    scaled = fraction * 32768.0
    whole = jnp.floor(scaled)
    code = 2.0 * whole + jnp.where(scaled > whole, 1.0, 0.0)
    return jnp.minimum(code, 65535.0).astype(jnp.int32)


def row_code(fraction):
    return jnp.floor(fraction * FY_TOP + 0.5).astype(jnp.int32)


def edge_code(value):
    return jnp.floor(value * EDGE_SCALE + 0.5).astype(jnp.int32)


def prepare_kernel(
    place_ref,
    track_ref,
    need_ref,
    count_ref,
    background_ref,
    cells_ref,
    fracs_ref,
    ehead_ref,
    etail_ref,
    bhead_ref,
    btail_ref,
    tiles_ref,
    out_ref,
    rows_ref,
    stage_ref,
):
    storm_field(place_ref, track_ref, background_ref, tiles_ref, rows_ref)
    for g in range(GROUPS):
        span = slice(g * LANES, (g + 1) * LANES)
        word = cells_ref[:, span] | (column_code(fracs_ref[0, :, span]) << 16)
        stage_ref[pl.ds(g, NEED, stride=MSG), :] = word
    for g in range(GROUPS // 2):
        low = row_code(fracs_ref[1, :, g * LANES : (g + 1) * LANES])
        high = row_code(fracs_ref[1, :, NPS // 2 + g * LANES : NPS // 2 + (g + 1) * LANES])
        stage_ref[pl.ds(GROUPS + g, NEED, stride=MSG), :] = low | (high << 16)
    row = iota((8, LANES), 0)
    lane = iota((8, LANES), 1)
    position = row * LANES + lane
    surface = jnp.where(lane < SWEEPS, ehead_ref[0:1, :], etail_ref[7:8, :])
    bed = jnp.where(lane < SWEEPS, bhead_ref[0:1, :], btail_ref[7:8, :])
    plain = jnp.where(row == 5, edge_code(surface), jnp.where(row == 6, edge_code(bed), ABSENT))

    def clear(d, carry):
        out_ref[d, 8:16, :] = plain
        return carry

    lax.fori_loop(0, N_DOM, clear, 0, unroll=8)

    def place(s, carry):
        tile = need_ref[0, s]
        count = count_ref[s]
        holder = tile % BAND // TILES_DEV
        live = jnp.maximum((count + CHUNK - 1) // CHUNK, 2)
        header = (tile // BAND * TILES_DEV + tile % TILES_DEV) | ((live - 2) * FIELD_BITS << 16)
        start = pl.multiple_of(s * MSG, MSG)
        out_ref[holder, 0:8, :] = jnp.where(position < count, stage_ref[pl.ds(start, 8), :], DEAD_CELL)
        out_ref[holder, 8:16, :] = jnp.where(
            row < 4, stage_ref[pl.ds(start + 8, 8), :], jnp.where(row == 4, header, plain)
        )
        return carry

    lax.fori_loop(0, NEED, place, 0, unroll=4)


def prepare(place, storm_track, need_tiles, slot_count, background, node_cells, node_fracs, elevation, bed_level):
    last = elevation.shape[0] // 8 - 1
    head = pl.BlockSpec((8, LANES), lambda i: (0, 0))
    tail = pl.BlockSpec((8, LANES), lambda i: (last, 0))
    vmem = pl.BlockSpec(memory_space=pltpu.VMEM)
    rows = FIELDS * TILE
    return pl.pallas_call(
        prepare_kernel,
        grid=(1,),
        out_shape=(
            jax.ShapeDtypeStruct((rows, LANES), jnp.bfloat16),
            jax.ShapeDtypeStruct((N_DOM, MSG, LANES), jnp.int32),
        ),
        in_specs=[pl.BlockSpec(memory_space=pltpu.SMEM)] * 4 + [vmem] * 3 + [head, tail, head, tail],
        out_specs=(vmem, vmem),
        scratch_shapes=[
            pltpu.VMEM((rows, LANES), jnp.float32),
            pltpu.VMEM((NEED * MSG, LANES), jnp.int32),
        ],
    )(
        place,
        storm_track,
        need_tiles,
        slot_count,
        background.transpose(1, 0, 2),
        node_cells,
        node_fracs,
        elevation,
        elevation,
        bed_level,
        bed_level,
    )


SLOT_ROWS = FIELDS * GROUPS * 8


def interpolate_kernel(
    place_ref,
    header_ref,
    message_ref,
    near0,
    near1,
    near2,
    near3,
    far_ref,
    out_ref,
    tiles_ref,
    x_ref,
    y_ref,
    part_ref,
    list_ref,
):
    own = place_ref[0] // N_DOM
    for shift, ref in enumerate((near0, near1, near2, near3)):
        band = (own + N_OWN - CORES * shift) % N_OWN
        tiles_ref[2 * band] = ref[:, 0:TILE]
        tiles_ref[2 * band + 1] = ref[:, TILE : 2 * TILE]
        band = band + 1 - 2 * (band % CORES)
        tiles_ref[2 * band] = far_ref[shift, :, 0:TILE]
        tiles_ref[2 * band + 1] = far_ref[shift, :, TILE : 2 * TILE]

    packed = jnp.int32(0)
    for s in range(N_DOM):
        shift = header_ref[s] >> 16
        list_ref[shift * 8 + (lax.shift_right_logical(packed, shift) & (2**FIELD_BITS - 1))] = s
        packed = packed + (1 << shift)
    counts = [packed >> i * FIELD_BITS & (2**FIELD_BITS - 1) for i in range(CHUNKS - 1)]
    spot = iota((TILE, LANES), 0).astype(jnp.float32)

    def add_up(i, slot):
        values = []
        for f in range(FIELDS):
            at = i * SLOT_ROWS + f * 64
            pieces = [part_ref[pl.ds(at + j, GROUPS, stride=8), :] for j in range(8)]
            while len(pieces) > 1:
                pieces = [a + b for a, b in zip(pieces[::2], pieces[1::2])]
            values.append(pieces[0])
        out_ref[slot] = jnp.concatenate(values, axis=0).astype(jnp.bfloat16)

    def hat(ref, at):
        return jnp.maximum(1.0 - jnp.abs(spot - ref[at : at + 1, :]), 0.0)

    def decode(i, s):
        word = message_ref[s, 0:8, :]
        pair = message_ref[s, 8:16, :]
        cell = word & 0xFFFF
        row = (cell // TILE).astype(jnp.float32)
        low = (pair[0:4] & 0xFFFF).astype(jnp.float32)
        high = lax.shift_right_logical(pair[0:4], 16).astype(jnp.float32)
        x_ref[8 * i : 8 * i + 8, :] = (cell & (TILE - 1)).astype(jnp.float32) + lax.shift_right_logical(
            word, 16
        ).astype(jnp.float32) * FX_STEP
        y_ref[8 * i : 8 * i + 4, :] = row[0:4] + low * (1.0 / FY_TOP)
        y_ref[8 * i + 4 : 8 * i + 8, :] = row[4:8] + high * (1.0 / FY_TOP)

    def two_slots(slots, before, live):
        for i in range(2):
            add_up(i, before[i])
        for i in range(2):
            decode(i, slots[i])
        tiles = [tiles_ref[header_ref[s] & 0xFFFF] for s in slots]
        for c in range(live):
            for i in range(2):
                groups = range(c * PER_CHUNK, (c + 1) * PER_CHUNK)
                columns = jnp.concatenate([hat(x_ref, 8 * i + g).astype(jnp.bfloat16) for g in groups], axis=1)
                spread = jnp.dot(tiles[i], columns, preferred_element_type=jnp.float32)
                for j, g in enumerate(groups):
                    rows = hat(y_ref, 8 * i + g)
                    for f in range(FIELDS):
                        weighed = spread[f * TILE : (f + 1) * TILE, j * LANES : (j + 1) * LANES] * rows
                        at = i * SLOT_ROWS + (f * GROUPS + g) * 8
                        part_ref[at : at + 8, :] = jnp.sum(weighed.reshape(TILE // 8, 8, LANES), axis=0)
        dead = (CHUNKS - live) * PER_CHUNK * 8
        if dead:
            for i in range(2):
                for f in range(FIELDS):
                    at = i * SLOT_ROWS + (f + 1) * GROUPS * 8 - dead
                    part_ref[at : at + dead, :] = jnp.zeros((dead, LANES), jnp.float32)

    before = (jnp.int32(-1), jnp.int32(-1))
    for i, n in enumerate(counts):

        @pl.when(n > 0)
        def _():
            list_ref[i * LIST + n] = list_ref[i * LIST + n - 1]

        def step(p, before):
            slots = (list_ref[i * LIST + 2 * p], list_ref[i * LIST + 2 * p + 1])
            two_slots(slots, tuple(jnp.where(b < 0, s, b) for b, s in zip(before, slots)), i + 2)
            return slots

        before = lax.fori_loop(0, (n + 1) // 2, step, before)
    for i in range(2):
        add_up(i, jnp.maximum(before[i], 0))


def interpolate(place, header, message, near, far):
    return pl.pallas_call(
        interpolate_kernel,
        out_shape=jax.ShapeDtypeStruct((N_DOM, FIELDS * GROUPS, LANES), jnp.bfloat16),
        in_specs=[pl.BlockSpec(memory_space=pltpu.SMEM)] * 2 + [pl.BlockSpec(memory_space=pltpu.VMEM)] * 6,
        out_specs=pl.BlockSpec(memory_space=pltpu.VMEM),
        scratch_shapes=[
            pltpu.VMEM((N_OWN * TILES_DEV, FIELDS * TILE, TILE), jnp.bfloat16),
            pltpu.VMEM((2 * GROUPS, LANES), jnp.float32),
            pltpu.VMEM((2 * GROUPS, LANES), jnp.float32),
            pltpu.VMEM((2 * SLOT_ROWS, LANES), jnp.float32),
            pltpu.SMEM((CHUNKS * LIST,), jnp.int32),
        ],
        compiler_params=SMALL,
    )(place, header, message, *near, far)


def following(x, lane):
    moved = pltpu.roll(x, LANES - 1, 1)
    return jnp.where(lane == LANES - 1, pltpu.roll(moved, x.shape[0] - 1, 0), moved)


def preceding(x, lane):
    moved = pltpu.roll(x, 1, 1)
    return jnp.where(lane == 0, pltpu.roll(moved, 1, 0), moved)


def flux_sweeps(place_ref, before_ref, after_ref, elevation_ref, bed_ref, out_ref):
    rows = elevation_ref.shape[0]
    lane8 = iota((8, LANES), 1)
    row8 = iota((8, LANES), 0)

    def ends(which):
        before = before_ref[0, which : which + 1, :].astype(jnp.float32) * (1.0 / EDGE_SCALE)
        after = after_ref[0, which : which + 1, :].astype(jnp.float32) * (1.0 / EDGE_SCALE)
        top = jnp.where((row8 == 7) & (lane8 >= LANES - SWEEPS), before, 0.0)
        bottom = jnp.where((row8 == 0) & (lane8 < SWEEPS), after, 0.0)
        return top, bottom

    surface_top, surface_bottom = ends(5)
    bed_top, bed_bottom = ends(6)
    surface = jnp.concatenate([surface_top, elevation_ref[...], surface_bottom], axis=0)
    bed = jnp.concatenate([bed_top, bed_ref[...], bed_bottom], axis=0)
    lane = iota(surface.shape, 1)
    node = iota(surface.shape, 0) * LANES + lane
    dom = place_ref[0] % N_DOM
    first_wall = jnp.where(dom == 0, 8 * LANES - 1, -1)
    last_wall = jnp.where(dom == N_DOM - 1, (8 + rows) * LANES - 1, -1)
    open_face = jnp.where((node == first_wall) | (node == last_wall), 0.0, KAPPA)
    for _ in range(SWEEPS):
        wet = jnp.maximum(surface - bed, 0.0)
        drop = surface - following(surface, lane)
        upwind = jnp.where(drop >= 0.0, wet, following(wet, lane))
        flux = open_face * upwind * drop
        surface = surface - (flux - preceding(flux, lane))
    out_ref[...] = surface[8 : 8 + rows]


SLOTS8 = 8


def finish_kernel(
    place_ref,
    need_ref,
    returned_ref,
    before_ref,
    after_ref,
    elevation_ref,
    bed_ref,
    forcing_ref,
    surge_ref,
    surface_ref,
    stage_ref,
):
    rows = FIELDS * GROUPS
    flux_sweeps(place_ref, before_ref, after_ref, elevation_ref, bed_ref, surface_ref)

    def eight_slots(b, carry):
        for i in range(SLOTS8):
            s = b * SLOTS8 + i
            block = returned_ref[need_ref[0, s] % BAND // TILES_DEV].astype(jnp.float32)
            stage_ref[i * rows : (i + 1) * rows, :] = block
            here = pl.ds(pl.multiple_of(s * GROUPS, GROUPS), GROUPS)
            surface = surface_ref[here, :]
            wet = jnp.minimum(jnp.maximum(surface - bed_ref[here, :], 0.0), 1.0)
            surge_ref[here, :] = surface - 0.5 * block[rows - GROUPS :] * wet
        slots = pl.ds(pl.multiple_of(b * SLOTS8, SLOTS8), SLOTS8)
        for f in range(FIELDS):
            for g in range(GROUPS):
                piece = stage_ref[pl.ds(f * GROUPS + g, SLOTS8, stride=rows), :]
                forcing_ref[f, slots, g * LANES : (g + 1) * LANES] = piece.astype(jnp.bfloat16)
        return carry

    lax.fori_loop(0, NEED // SLOTS8, eight_slots, 0)


def finish(place, need_tiles, returned, message, elevation, bed_level):
    def whole(shape):
        return pl.BlockSpec(shape, lambda i, *refs: (0,) * len(shape))

    def neighbour(step):
        return pl.BlockSpec((1, 8, LANES), lambda i, place_ref, need_ref: ((place_ref[0] + step) % N_DOM, 1, 0))

    forcing = (FIELDS, NEED, NPS)
    return pl.pallas_call(
        finish_kernel,
        out_shape=(
            jax.ShapeDtypeStruct(forcing, jnp.bfloat16),
            jax.ShapeDtypeStruct(elevation.shape, jnp.float32),
        ),
        grid_spec=pltpu.PrefetchScalarGridSpec(
            num_scalar_prefetch=2,
            grid=(1,),
            in_specs=[
                whole(returned.shape),
                neighbour(N_DOM - 1),
                neighbour(1),
                whole(elevation.shape),
                whole(elevation.shape),
            ],
            out_specs=(whole(forcing), whole(elevation.shape)),
            scratch_shapes=[
                pltpu.VMEM(elevation.shape, jnp.float32),
                pltpu.VMEM((SLOTS8 * FIELDS * GROUPS, LANES), jnp.float32),
            ],
        ),
        compiler_params=SMALL,
    )(place, need_tiles, returned, message, message, elevation, bed_level)


def exchange(blocks, axis):
    return lax.all_to_all(blocks, axis, split_axis=0, concat_axis=0, tiled=True)


def shards(
    background, storm_track, need_tiles, node_cells, node_fracs, slot_count, elevation, bed_level
):
    place = (lax.axis_index("own") * N_DOM + lax.axis_index("dom"))[None].astype(jnp.int32)
    elevation = elevation.reshape(-1, LANES)
    bed_level = bed_level.reshape(-1, LANES)
    tiles, question = prepare(
        place, storm_track, need_tiles, slot_count, background, node_cells, node_fracs, elevation, bed_level
    )
    near = [tiles]
    for shift in range(CORES, N_OWN, CORES):
        near.append(lax.ppermute(tiles, "own", [(i, (i + shift) % N_OWN) for i in range(N_OWN)]))
    message = exchange(question, "dom")
    far = lax.ppermute(jnp.stack(near), "own", [(i, i ^ 1) for i in range(N_OWN)])
    answers = interpolate(place, message[:, 12, 0], message, near, far)
    returned = exchange(answers, "dom")
    forcing, surge = finish(place, need_tiles, returned, message, elevation, bed_level)
    return forcing.transpose(1, 0, 2), surge.reshape(1, -1)


def solution(mesh):
    placed = (
        P(("own", "dom"), None, None),
        P(),
        P(("own", "dom"), None),
        P(("own", "dom"), None),
        P(None, ("own", "dom"), None),
        P(("own", "dom")),
        P("own", "dom"),
        P("own", "dom"),
    )
    return jax.shard_map(
        shards,
        mesh=mesh,
        in_specs=placed,
        out_specs=(P(("own", "dom"), None, None), P("own", "dom")),
        check_vma=False,
    )
```

time: 106 us -> 104 us (0.981)
  blocking collectives: 23.9 us -> 40 us
  waiting for transfers between devices: 25.2 us -> 14.1 us
  Pallas kernels: 23.4 us -> 16.1 us
  starting transfers between devices: 29.5 us -> 31.2 us
    all_to_all x0 -> x1, blocking collectives: none -> 40 us  [exchange(): return lax.all_to_all(blocks, axis, split_axis=0, concat_axis=0, tiled=True)]
    all_to_all x2 -> x1, waiting for transfers between devices: 25.2 us -> 0.01 us  [exchange(): return lax.all_to_all(blocks, axis, split_axis=0, concat_axis=0, tiled=True)]
    all_gather x1 -> x0, blocking collectives: 23.9 us -> none  [shards(): column = lax.all_gather(tiles, 'own')]
    ppermute x0 -> x4, waiting for transfers between devices: none -> 14.1 us  [the longest x3 13.7 us: shards(): lax.ppermute(tiles, 'own', [(i, (i + shift) % N_OWN) for i in range(N_OWN)])]
    ppermute x0 -> x4, starting transfers between devices: none -> 12.1 us  [the longest x3 10.1 us: shards(): lax.ppermute(tiles, 'own', [(i, (i + shift) % N_OWN) for i in range(N_OWN)])]
    all_to_all x2 -> x1, starting transfers between devices: 29.5 us -> 19.2 us  [exchange(): return lax.all_to_all(blocks, axis, split_axis=0, concat_axis=0, tiled=True)]
    pallas_call x1, Pallas kernels: 16 us -> 9.39 us  [interpolate(): pl.pallas_call(interpolate_kernel, out_shape=jax.ShapeDtypeStruct((N_DOM,...]
    pallas_call x4 -> x2, Pallas kernels: 7.39 us -> 6.68 us  [the longest x1 4.1 us: prepare(): pl.pallas_call(prepare_kernel, grid=(1,), out_shape=(jax.ShapeDtypeStruct...]
  transfers between devices with their start and end apart: 2 -> 5, of which waited for: 1 -> 3; matrix products, arithmetic and copies ran while one was open for 0% -> 1% of each run, Pallas kernels for 3% -> 0%
where the time goes in v3:
time: 104 us; the launch traced here: 103 us
  blocking collectives  40 us (38%)
  starting transfers between devices  31.2 us (30%)
  Pallas kernels  16.1 us (15%)
  waiting for transfers between devices  14.1 us (14%)
  local copies, waits for them, and re-layouts  1.25 us (1%)
    all_to_all x1, blocking collectives, exchange(): return lax.all_to_all(blocks, axis, split_axis=0, concat_axis=0, tiled=True)  40 us
    all_to_all x1, starting transfers between devices, exchange(): return lax.all_to_all(blocks, axis, split_axis=0, concat_axis=0, tiled=True)  19.2 us
    ppermute x3, waiting for transfers between devices, shards(): lax.ppermute(tiles, 'own', [(i, (i + shift) % N_OWN) for i in range(N_OWN)])  13.7 us
    ppermute x3, starting transfers between devices, shards(): lax.ppermute(tiles, 'own', [(i, (i + shift) % N_OWN) for i in range(N_OWN)])  10.1 us
    pallas_call x1, Pallas kernels, interpolate(): pl.pallas_call(interpolate_kernel, out_shape=jax.ShapeDtypeStruct((N_DOM,...  9.39 us
    pallas_call x1, Pallas kernels, prepare(): pl.pallas_call(prepare_kernel, grid=(1,), out_shape=(jax.ShapeDtypeStruct...  4.1 us
    pallas_call x1, Pallas kernels, finish(): pl.pallas_call(finish_kernel, out_shape=(jax.ShapeDtypeStruct(forcing, jn...  2.58 us
  transfers between devices with their start and end apart: 5, of which 3 were waited for; matrix products, arithmetic and copies ran while one was open for 1% of the time, Pallas kernels for 0%

profile of v3, /device:TPU:6, one launch (start us, length us, event | category | flops | bytes accessed | tf_op | source)
XLA Modules:
  0.0 103.4 jit_solution(3669262114499113419)
XLA Ops:
  0.6 4.1 %shard_map.95 = (bf16[384,128]{1,0:T(8,128)(2,1)}, s32[64,16,128]{2,1,0:T(8,128)}) custom-call(s32[1]{0:T(128)} %bitcast.place_ref, f32[2,5]{1,0:T(2,128)} %track_ref.1, s32[1,32]{1,0:T(1,128)} %need_ref.3, s32[32]{0:T(128)} %count_ref.1, bf16[6,2,4096]{2,1,0:T(2,128)(2,1)} %bitcast.20, s32[32,1024]{1,0:T(8,128)} %cells_ref.1, f32[2,32,1024]{2,1,0:T(8,128)} %fracs_ref.1, ...), custom_call_target="tpu_custom_call" | custom-call | tf_op jit(solution)/shard_map/pallas_call | solution.py:157
  4.7 0.0 copy-start.2
  4.7 19.2 %all-to-all-start = ((s32[64,16,128]{2,1,0:T(8,128)}), s32[64,16,128]{2,1,0:T(8,128)S(1)}, u32[]{:S(2)}, u32[]{:S(2)}) async-start(s32[64,16,128]{2,1,0:T(8,128)} %get-tuple-element.6), calls=%async_computation | async-start | bytes 1048576 | tf_op jit(solution)/shard_map/all_to_all | solution.py:419
  23.9 0.0 copy-done.2
  23.9 5.2 %collective-permute-start.2 = (bf16[384,128]{1,0:T(8,128)(2,1)S(1)}, bf16[384,128]{1,0:T(8,128)(2,1)S(1)}, u32[]{:S(2)}, u32[]{:S(2)}) collective-permute-start(bf16[384,128]{1,0:T(8,128)(2,1)S(1)} %copy-done.2), channel_id=1, source_target_pairs={{0,384},{64,448},{128,0},{192,64},{256,128},{320,192},{384,256},{4... | collective-permute-start | bytes 294920 | tf_op jit(solution)/shard_map/ppermute | solution.py:433
  29.1 1.9 %collective-permute-start.1 = (bf16[384,128]{1,0:T(8,128)(2,1)S(1)}, bf16[384,128]{1,0:T(8,128)(2,1)S(1)}, u32[]{:S(2)}, u32[]{:S(2)}) collective-permute-start(bf16[384,128]{1,0:T(8,128)(2,1)S(1)} %copy-done.2), channel_id=1, source_target_pairs={{0,256},{64,320},{128,384},{192,448},{256,0},{320,64},{384,128},{4... | collective-permute-start | bytes 294920 | tf_op jit(solution)/shard_map/ppermute | solution.py:433
  31.1 3.0 %collective-permute-start = (bf16[384,128]{1,0:T(8,128)(2,1)S(1)}, bf16[384,128]{1,0:T(8,128)(2,1)S(1)}, u32[]{:S(2)}, u32[]{:S(2)}) collective-permute-start(bf16[384,128]{1,0:T(8,128)(2,1)S(1)} %copy-done.2), channel_id=1, source_target_pairs={{0,128},{64,192},{128,256},{192,320},{256,384},{320,448},{384,0},{... | collective-permute-start | bytes 294920 | tf_op jit(solution)/shard_map/ppermute | solution.py:433
  34.1 5.6 %collective-permute-done.2.near3 = bf16[384,128]{1,0:T(8,128)(2,1)S(1)} collective-permute-done((bf16[384,128]{1,0:T(8,128)(2,1)S(1)}, bf16[384,128]{1,0:T(8,128)(2,1)S(1)}, u32[]{:S(2)}, u32[]{:S(2)}) %collective-permute-start.2) | collective-permute-done | bytes 98336 | tf_op jit(solution)/shard_map/ppermute | solution.py:433
  39.7 8.0 %collective-permute-done.1.near2 = bf16[384,128]{1,0:T(8,128)(2,1)S(1)} collective-permute-done((bf16[384,128]{1,0:T(8,128)(2,1)S(1)}, bf16[384,128]{1,0:T(8,128)(2,1)S(1)}, u32[]{:S(2)}, u32[]{:S(2)}) %collective-permute-start.1) | collective-permute-done | bytes 98336 | tf_op jit(solution)/shard_map/ppermute | solution.py:433
  47.7 0.0 collective-permute-done.near1
  47.7 0.1 pad_maximum_fusion
  47.8 1.9 %collective-permute-start.3 = (bf16[4,384,128]{2,1,0:T(8,128)(2,1)S(1)}, bf16[4,384,128]{2,1,0:T(8,128)(2,1)S(1)}, u32[]{:S(2)}, u32[]{:S(2)}) collective-permute-start(bf16[4,384,128]{2,1,0:T(8,128)(2,1)S(1)} %pad_maximum_fusion), channel_id=1, source_target_pairs={{0,64},{64,0},{128,192},{192,128},{256,320},{320,256},{384,448},{4... | collective-permute-start | bytes 1179656 | tf_op jit(solution)/shard_map/ppermute | solution.py:435
  49.7 0.0 all-to-all-done.message_ref.before_ref.after_ref
  49.7 1.2 %slice_reduce_fusion.header_ref = s32[64]{0:T(128)S(1)} fusion(s32[64,16,128]{2,1,0:T(8,128)S(1)} %all-to-all-done.message_ref.before_ref.after_ref), kind=kLoop, calls=%fused_computation.1 | loop fusion | bytes 512 | tf_op jit(solution)/shard_map/slice | solution.py:436
  51.0 0.5 collective-permute-done.3.far_ref
  51.4 9.4 %shard_map.96 = bf16[64,48,128]{2,1,0:T(8,128)(2,1)S(1)} custom-call(s32[1]{0:T(128)} %bitcast.place_ref, s32[64]{0:T(128)S(1)} %slice_reduce_fusion.header_ref, s32[64,16,128]{2,1,0:T(8,128)S(1)} %all-to-all-done.message_ref.before_ref.after_ref, bf16[384,128]{1,0:T(8,128)(2,1)S(1)} %copy-done.2, bf16[384,128]{1,0:T(8,128)(2,1)S(1)} %collective-permute-done.near1, ...), custom_call_target="tpu_custom_call" | custom-call | tf_op jit(solution)/shard_map/pallas_call | solution.py:289
  60.8 0.0 copy-start
  60.8 0.0 copy-start.1
  60.8 0.0 copy-start.3
  60.8 40.0 %all_to_all.10.returned_ref = bf16[64,48,128]{2,1,0:T(8,128)(2,1)S(1)} all-to-all(bf16[64,48,128]{2,1,0:T(8,128)(2,1)S(1)} %shard_map.96), channel_id=1, replica_groups=mesh['own'=8,'dom'=64] {'dom'}, dimensions={0} | all-to-all | bytes 1572864 | tf_op jit(solution)/shard_map/all_to_all | solution.py:419
  100.8 0.0 copy-done
  100.8 0.0 copy-done.1
  100.8 0.0 copy-done.3
  100.8 2.6 %shard_map.97 = (bf16[6,32,1024]{2,1,0:T(8,128)(2,1)}, f32[256,128]{1,0:T(8,128)}) custom-call(s32[1]{0:T(128)} %bitcast.place_ref, s32[1,32]{1,0:T(1,128)S(1)} %copy-done.3, bf16[64,48,128]{2,1,0:T(8,128)(2,1)S(1)} %all_to_all.10.returned_ref, s32[64,16,128]{2,1,0:T(8,128)S(1)} %all-to-all-done.message_ref.before_ref.after_ref, ...), custom_call_target="tpu_custom_call" | custom-call | tf_op jit(solution)/shard_map/pallas_call | solution.py:392
Async XLA Ops:
  4.7 19.2 %copy-start.2 = (bf16[384,128]{1,0:T(8,128)(2,1)S(1)}, bf16[384,128]{1,0:T(8,128)(2,1)}, u32[]{:S(2)}) copy-start(bf16[384,128]{1,0:T(8,128)(2,1)} %get-tuple-element.7.near0) | copy-start | bytes 294916
  4.7 45.0 %all-to-all-start = ((s32[64,16,128]{2,1,0:T(8,128)}), s32[64,16,128]{2,1,0:T(8,128)S(1)}, u32[]{:S(2)}, u32[]{:S(2)}) async-start(s32[64,16,128]{2,1,0:T(8,128)} %get-tuple-element.6), calls=%async_computation | async-start | bytes 1048576 | tf_op jit(solution)/shard_map/all_to_all | solution.py:419
  23.9 15.8 %collective-permute-start.2 = (bf16[384,128]{1,0:T(8,128)(2,1)S(1)}, bf16[384,128]{1,0:T(8,128)(2,1)S(1)}, u32[]{:S(2)}, u32[]{:S(2)}) collective-permute-start(bf16[384,128]{1,0:T(8,128)(2,1)S(1)} %copy-done.2), channel_id=1, source_target_pairs={{0,384},{64,448},{128,0},{192,64},{256,128},{320,192},{384,256},{4... | collective-permute-start | bytes 294920 | tf_op jit(solution)/shard_map/ppermute | solution.py:433
  29.1 18.6 %collective-permute-start.1 = (bf16[384,128]{1,0:T(8,128)(2,1)S(1)}, bf16[384,128]{1,0:T(8,128)(2,1)S(1)}, u32[]{:S(2)}, u32[]{:S(2)}) collective-permute-start(bf16[384,128]{1,0:T(8,128)(2,1)S(1)} %copy-done.2), channel_id=1, source_target_pairs={{0,256},{64,320},{128,384},{192,448},{256,0},{320,64},{384,128},{4... | collective-permute-start | bytes 294920 | tf_op jit(solution)/shard_map/ppermute | solution.py:433
  31.1 16.7 %collective-permute-start = (bf16[384,128]{1,0:T(8,128)(2,1)S(1)}, bf16[384,128]{1,0:T(8,128)(2,1)S(1)}, u32[]{:S(2)}, u32[]{:S(2)}) collective-permute-start(bf16[384,128]{1,0:T(8,128)(2,1)S(1)} %copy-done.2), channel_id=1, source_target_pairs={{0,128},{64,192},{128,256},{192,320},{256,384},{320,448},{384,0},{... | collective-permute-start | bytes 294920 | tf_op jit(solution)/shard_map/ppermute | solution.py:433
  47.8 3.6 %collective-permute-start.3 = (bf16[4,384,128]{2,1,0:T(8,128)(2,1)S(1)}, bf16[4,384,128]{2,1,0:T(8,128)(2,1)S(1)}, u32[]{:S(2)}, u32[]{:S(2)}) collective-permute-start(bf16[4,384,128]{2,1,0:T(8,128)(2,1)S(1)} %pad_maximum_fusion), channel_id=1, source_target_pairs={{0,64},{64,0},{128,192},{192,128},{256,320},{320,256},{384,448},{4... | collective-permute-start | bytes 1179656 | tf_op jit(solution)/shard_map/ppermute | solution.py:435
  60.8 40.0 %copy-start = (f32[1,32768]{1,0:T(1,128)S(1)}, f32[1,32768]{1,0:T(1,128)}, u32[]{:S(2)}) copy-start(f32[1,32768]{1,0:T(1,128)} %param.14) | copy-start | bytes 393220
  60.8 40.0 %copy-start.1 = (f32[1,32768]{1,0:T(1,128)S(1)}, f32[1,32768]{1,0:T(1,128)}, u32[]{:S(2)}) copy-start(f32[1,32768]{1,0:T(1,128)} %param.15) | copy-start | bytes 393220
  60.8 40.0 %copy-start.3 = (s32[1,32]{1,0:T(1,128)S(1)}, s32[1,32]{1,0:T(1,128)}, u32[]{:S(2)}) copy-start(s32[1,32]{1,0:T(1,128)} %need_ref.3) | copy-start | bytes 388

commit v4 on v3

--- a/solution.py
+++ b/solution.py
@@ -19,6 +19,7 @@
 N_DOM = 64
 BAND = TILES_DEV * N_DOM
 CORES = 2
+CHIPS = N_OWN // CORES
 MSG = 16
 CHUNK = 256
 PER_CHUNK = CHUNK // LANES
@@ -74,7 +75,7 @@
         rows_ref[pl.ds(2 * chunk + 1, FIELDS, stride=TILE), :] = odd
         return carry
 
-    lax.fori_loop(0, TILE // 2, step, 0, unroll=4)
+    lax.fori_loop(0, TILE // 2, step, 0, unroll=8)
     out_ref[...] = rows_ref[...].astype(jnp.bfloat16)
 
 
@@ -189,10 +190,10 @@
     place_ref,
     header_ref,
     message_ref,
-    near0,
-    near1,
-    near2,
-    near3,
+    own_ref,
+    other_ref,
+    beside_ref,
+    across_ref,
     far_ref,
     out_ref,
     tiles_ref,
@@ -202,13 +203,23 @@
     list_ref,
 ):
     own = place_ref[0] // N_DOM
-    for shift, ref in enumerate((near0, near1, near2, near3)):
-        band = (own + N_OWN - CORES * shift) % N_OWN
-        tiles_ref[2 * band] = ref[:, 0:TILE]
-        tiles_ref[2 * band + 1] = ref[:, TILE : 2 * TILE]
-        band = band + 1 - 2 * (band % CORES)
-        tiles_ref[2 * band] = far_ref[shift, :, 0:TILE]
-        tiles_ref[2 * band + 1] = far_ref[shift, :, TILE : 2 * TILE]
+    core = own % CORES
+    side = 2 * core - 1
+
+    def keep(step, flip, ref, *index):
+        z = (own // CORES + step + CHIPS) % CHIPS
+        at = 2 * (z * CORES + (1 - core if flip else core))
+        tiles_ref[at] = ref[(*index, slice(None), slice(0, TILE))]
+        tiles_ref[at + 1] = ref[(*index, slice(None), slice(TILE, 2 * TILE))]
+
+    keep(0, False, own_ref)
+    keep(0, True, other_ref)
+    keep(side, False, beside_ref, 0)
+    keep(side, True, beside_ref, 1)
+    keep(2, False, across_ref)
+    keep(-side, True, far_ref, 0)
+    keep(-side, False, far_ref, 1)
+    keep(2, True, far_ref, 2)
 
     packed = jnp.int32(0)
     for s in range(N_DOM):
@@ -428,11 +439,13 @@
     tiles, question = prepare(
         place, storm_track, need_tiles, slot_count, background, node_cells, node_fracs, elevation, bed_level
     )
-    near = [tiles]
-    for shift in range(CORES, N_OWN, CORES):
-        near.append(lax.ppermute(tiles, "own", [(i, (i + shift) % N_OWN) for i in range(N_OWN)]))
+    other = lax.ppermute(tiles, "own", [(i, i ^ 1) for i in range(N_OWN)])
     message = exchange(question, "dom")
-    far = lax.ppermute(jnp.stack(near), "own", [(i, i ^ 1) for i in range(N_OWN)])
+    turn = [(i, (i + CORES if i % CORES == 0 else i - CORES) % N_OWN) for i in range(N_OWN)]
+    beside = lax.ppermute(jnp.stack([tiles, other]), "own", turn)
+    across = lax.ppermute(tiles, "own", [(i, (i + 2 * CORES) % N_OWN) for i in range(N_OWN)])
+    far = lax.ppermute(jnp.concatenate([beside, across[None]]), "own", [(i, i ^ 1) for i in range(N_OWN)])
+    near = (tiles, other, beside, across)
     answers = interpolate(place, message[:, 12, 0], message, near, far)
     returned = exchange(answers, "dom")
     forcing, surge = finish(place, need_tiles, returned, message, elevation, bed_level)

time: 104 us -> 104 us (level); the launches traced: 103 us -> 102 us
  blocking collectives: 40 us -> 38.3 us
  starting transfers between devices: 31.2 us -> 32.3 us
    all_to_all x1, blocking collectives: 40 us -> 38.3 us  [exchange(): return lax.all_to_all(blocks, axis, split_axis=0, concat_axis=0, tiled=True)]
    ppermute x4, starting transfers between devices: 12.1 us -> 13.1 us  [the longest x1 4.29 us: shards(): lax.ppermute(tiles, 'own', [(i, (i + 2 * CORES) % N_OWN) for i in range(N...]
  transfers between devices with their start and end apart: 5 -> 5, of which waited for: 3 -> 2; matrix products, arithmetic and copies ran while one was open for 1% -> 1% of each run, Pallas kernels for 0% -> 0%
where the time goes in v4:
time: 104 us; the launch traced here: 102 us
  blocking collectives  38.3 us (37%)
  starting transfers between devices  32.3 us (31%)
  Pallas kernels  15.7 us (15%)
  waiting for transfers between devices  13.8 us (13%)
  local copies, waits for them, and re-layouts  1.25 us (1%)
    all_to_all x1, blocking collectives, exchange(): return lax.all_to_all(blocks, axis, split_axis=0, concat_axis=0, tiled=True)  38.3 us
    all_to_all x1, starting transfers between devices, exchange(): return lax.all_to_all(blocks, axis, split_axis=0, concat_axis=0, tiled=True)  19.2 us
    ppermute x1, waiting for transfers between devices, shards(): lax.ppermute(tiles, 'own', [(i, (i + 2 * CORES) % N_OWN) for i in range(N...  12.6 us
    pallas_call x1, Pallas kernels, interpolate(): pl.pallas_call(interpolate_kernel, out_shape=jax.ShapeDtypeStruct((N_DOM,...  9.4 us
    ppermute x1, starting transfers between devices, shards(): lax.ppermute(tiles, 'own', [(i, (i + 2 * CORES) % N_OWN) for i in range(N...  4.29 us
    pallas_call x1, Pallas kernels, prepare(): pl.pallas_call(prepare_kernel, grid=(1,), out_shape=(jax.ShapeDtypeStruct...  3.76 us
    ppermute x1, starting transfers between devices, shards(): lax.ppermute(jnp.concatenate([beside, across[None]]), 'own', [(i, i ^ 1)...  3.53 us
    ppermute x1, starting transfers between devices, shards(): beside = lax.ppermute(jnp.stack([tiles, other]), 'own', turn)  3.38 us
  transfers between devices with their start and end apart: 5, of which 2 were waited for; matrix products, arithmetic and copies ran while one was open for 1% of the time, Pallas kernels for 0%

profile of v4, /device:TPU:6, one launch (start us, length us, event | category | flops | bytes accessed | tf_op | source)
XLA Modules:
  0.0 102.2 jit_solution(8216655974923769014)
XLA Ops:
  0.6 3.8 %shard_map.95 = (bf16[384,128]{1,0:T(8,128)(2,1)}, s32[64,16,128]{2,1,0:T(8,128)}) custom-call(s32[1]{0:T(128)} %bitcast.place_ref, f32[2,5]{1,0:T(2,128)} %track_ref.1, s32[1,32]{1,0:T(1,128)} %need_ref.3, s32[32]{0:T(128)} %count_ref.1, bf16[6,2,4096]{2,1,0:T(2,128)(2,1)} %bitcast.18, s32[32,1024]{1,0:T(8,128)} %cells_ref.1, f32[2,32,1024]{2,1,0:T(8,128)} %fracs_ref.1, ...), custom_call_target="tpu_custom_call" | custom-call | tf_op jit(solution)/shard_map/pallas_call | solution.py:158
  4.4 0.0 copy-start.2
  4.4 19.2 %all-to-all-start = ((s32[64,16,128]{2,1,0:T(8,128)}), s32[64,16,128]{2,1,0:T(8,128)S(1)}, u32[]{:S(2)}, u32[]{:S(2)}) async-start(s32[64,16,128]{2,1,0:T(8,128)} %get-tuple-element.6), calls=%async_computation | async-start | bytes 1048576 | tf_op jit(solution)/shard_map/all_to_all | solution.py:430
  23.6 0.0 copy-done.2
  23.6 1.9 %collective-permute-start = (bf16[384,128]{1,0:T(8,128)(2,1)S(1)}, bf16[384,128]{1,0:T(8,128)(2,1)S(1)}, u32[]{:S(2)}, u32[]{:S(2)}) collective-permute-start(bf16[384,128]{1,0:T(8,128)(2,1)S(1)} %copy-done.2), channel_id=1, source_target_pairs={{0,64},{64,0},{128,192},{192,128},{256,320},{320,256},{384,448},{4... | collective-permute-start | bytes 294920 | tf_op jit(solution)/shard_map/ppermute | solution.py:442
  25.5 1.3 %collective-permute-done.other_ref = bf16[384,128]{1,0:T(8,128)(2,1)S(1)} collective-permute-done((bf16[384,128]{1,0:T(8,128)(2,1)S(1)}, bf16[384,128]{1,0:T(8,128)(2,1)S(1)}, u32[]{:S(2)}, u32[]{:S(2)}) %collective-permute-start) | collective-permute-done | bytes 98336 | tf_op jit(solution)/shard_map/ppermute | solution.py:442
  26.8 3.4 %collective-permute-start.1 = (bf16[2,384,128]{2,1,0:T(8,128)(2,1)S(1)}, bf16[2,384,128]{2,1,0:T(8,128)(2,1)S(1)}, u32[]{:S(2)}, u32[]{:S(2)}) collective-permute-start(bf16[2,384,128]{2,1,0:T(8,128)(2,1)S(1)} %pad_maximum_fusion.1), channel_id=1, source_target_pairs={{0,128},{64,448},{128,256},{192,64},{256,384},{320,192},{384,0},{4... | collective-permute-start | bytes 589832 | tf_op jit(solution)/shard_map/ppermute | solution.py:445
  30.2 4.3 %collective-permute-start.2 = (bf16[384,128]{1,0:T(8,128)(2,1)S(1)}, bf16[384,128]{1,0:T(8,128)(2,1)S(1)}, u32[]{:S(2)}, u32[]{:S(2)}) collective-permute-start(bf16[384,128]{1,0:T(8,128)(2,1)S(1)} %copy-done.2), channel_id=1, source_target_pairs={{0,256},{64,320},{128,384},{192,448},{256,0},{320,64},{384,128},{4... | collective-permute-start | bytes 294920 | tf_op jit(solution)/shard_map/ppermute | solution.py:446
  34.5 12.6 %collective-permute-done.2.across_ref = bf16[384,128]{1,0:T(8,128)(2,1)S(1)} collective-permute-done((bf16[384,128]{1,0:T(8,128)(2,1)S(1)}, bf16[384,128]{1,0:T(8,128)(2,1)S(1)}, u32[]{:S(2)}, u32[]{:S(2)}) %collective-permute-start.2) | collective-permute-done | bytes 98336 | tf_op jit(solution)/shard_map/ppermute | solution.py:446
  47.1 0.0 collective-permute-done.1.beside_ref
  47.1 3.5 %collective-permute-start.3 = (bf16[3,384,128]{2,1,0:T(8,128)(2,1)S(1)}, bf16[3,384,128]{2,1,0:T(8,128)(2,1)S(1)}, u32[]{:S(2)}, u32[]{:S(2)}) collective-permute-start(bf16[3,384,128]{2,1,0:T(8,128)(2,1)S(1)} %pad_maximum_fusion), channel_id=1, source_target_pairs={{0,64},{64,0},{128,192},{192,128},{256,320},{320,256},{384,448},{4... | collective-permute-start | bytes 884744 | tf_op jit(solution)/shard_map/ppermute | solution.py:447
  50.6 0.0 all-to-all-done.message_ref.before_ref.after_ref
  50.6 1.2 %slice_reduce_fusion.header_ref = s32[64]{0:T(128)S(1)} fusion(s32[64,16,128]{2,1,0:T(8,128)S(1)} %all-to-all-done.message_ref.before_ref.after_ref), kind=kLoop, calls=%fused_computation.2 | loop fusion | bytes 512 | tf_op jit(solution)/shard_map/slice | solution.py:449
  51.9 0.0 collective-permute-done.3.far_ref
  51.9 9.4 %shard_map.96 = bf16[64,48,128]{2,1,0:T(8,128)(2,1)S(1)} custom-call(s32[1]{0:T(128)} %bitcast.place_ref, s32[64]{0:T(128)S(1)} %slice_reduce_fusion.header_ref, s32[64,16,128]{2,1,0:T(8,128)S(1)} %all-to-all-done.message_ref.before_ref.after_ref, bf16[384,128]{1,0:T(8,128)(2,1)S(1)} %copy-done.2, bf16[384,128]{1,0:T(8,128)(2,1)S(1)} %collective-permute-done.other_ref, ...), custom_call_target="tpu_custom_call" | custom-call | tf_op jit(solution)/shard_map/pallas_call | solution.py:300
  61.3 0.0 copy-start
  61.3 0.0 copy-start.1
  61.3 0.0 copy-start.3
  61.3 38.3 %all_to_all.10.returned_ref = bf16[64,48,128]{2,1,0:T(8,128)(2,1)S(1)} all-to-all(bf16[64,48,128]{2,1,0:T(8,128)(2,1)S(1)} %shard_map.96), channel_id=1, replica_groups=mesh['own'=8,'dom'=64] {'dom'}, dimensions={0} | all-to-all | bytes 1572864 | tf_op jit(solution)/shard_map/all_to_all | solution.py:430
  99.7 0.0 copy-done
  99.7 0.0 copy-done.1
  99.7 0.0 copy-done.3
  99.7 2.6 %shard_map.97 = (bf16[6,32,1024]{2,1,0:T(8,128)(2,1)}, f32[256,128]{1,0:T(8,128)}) custom-call(s32[1]{0:T(128)} %bitcast.place_ref, s32[1,32]{1,0:T(1,128)S(1)} %copy-done.3, bf16[64,48,128]{2,1,0:T(8,128)(2,1)S(1)} %all_to_all.10.returned_ref, s32[64,16,128]{2,1,0:T(8,128)S(1)} %all-to-all-done.message_ref.before_ref.after_ref, ...), custom_call_target="tpu_custom_call" | custom-call | tf_op jit(solution)/shard_map/pallas_call | solution.py:403
  (2 shorter events, 0.0 us)
Async XLA Ops:
  4.4 19.2 %copy-start.2 = (bf16[384,128]{1,0:T(8,128)(2,1)S(1)}, bf16[384,128]{1,0:T(8,128)(2,1)}, u32[]{:S(2)}) copy-start(bf16[384,128]{1,0:T(8,128)(2,1)} %get-tuple-element.7.own_ref) | copy-start | bytes 294916
  4.4 46.2 %all-to-all-start = ((s32[64,16,128]{2,1,0:T(8,128)}), s32[64,16,128]{2,1,0:T(8,128)S(1)}, u32[]{:S(2)}, u32[]{:S(2)}) async-start(s32[64,16,128]{2,1,0:T(8,128)} %get-tuple-element.6), calls=%async_computation | async-start | bytes 1048576 | tf_op jit(solution)/shard_map/all_to_all | solution.py:430
  23.6 3.2 %collective-permute-start = (bf16[384,128]{1,0:T(8,128)(2,1)S(1)}, bf16[384,128]{1,0:T(8,128)(2,1)S(1)}, u32[]{:S(2)}, u32[]{:S(2)}) collective-permute-start(bf16[384,128]{1,0:T(8,128)(2,1)S(1)} %copy-done.2), channel_id=1, source_target_pairs={{0,64},{64,0},{128,192},{192,128},{256,320},{320,256},{384,448},{4... | collective-permute-start | bytes 294920 | tf_op jit(solution)/shard_map/ppermute | solution.py:442
  26.8 20.3 %collective-permute-start.1 = (bf16[2,384,128]{2,1,0:T(8,128)(2,1)S(1)}, bf16[2,384,128]{2,1,0:T(8,128)(2,1)S(1)}, u32[]{:S(2)}, u32[]{:S(2)}) collective-permute-start(bf16[2,384,128]{2,1,0:T(8,128)(2,1)S(1)} %pad_maximum_fusion.1), channel_id=1, source_target_pairs={{0,128},{64,448},{128,256},{192,64},{256,384},{320,192},{384,0},{4... | collective-permute-start | bytes 589832 | tf_op jit(solution)/shard_map/ppermute | solution.py:445
  30.2 16.9 %collective-permute-start.2 = (bf16[384,128]{1,0:T(8,128)(2,1)S(1)}, bf16[384,128]{1,0:T(8,128)(2,1)S(1)}, u32[]{:S(2)}, u32[]{:S(2)}) collective-permute-start(bf16[384,128]{1,0:T(8,128)(2,1)S(1)} %copy-done.2), channel_id=1, source_target_pairs={{0,256},{64,320},{128,384},{192,448},{256,0},{320,64},{384,128},{4... | collective-permute-start | bytes 294920 | tf_op jit(solution)/shard_map/ppermute | solution.py:446
  47.1 4.8 %collective-permute-start.3 = (bf16[3,384,128]{2,1,0:T(8,128)(2,1)S(1)}, bf16[3,384,128]{2,1,0:T(8,128)(2,1)S(1)}, u32[]{:S(2)}, u32[]{:S(2)}) collective-permute-start(bf16[3,384,128]{2,1,0:T(8,128)(2,1)S(1)} %pad_maximum_fusion), channel_id=1, source_target_pairs={{0,64},{64,0},{128,192},{192,128},{256,320},{320,256},{384,448},{4... | collective-permute-start | bytes 884744 | tf_op jit(solution)/shard_map/ppermute | solution.py:447
  61.3 38.4 %copy-start = (f32[1,32768]{1,0:T(1,128)S(1)}, f32[1,32768]{1,0:T(1,128)}, u32[]{:S(2)}) copy-start(f32[1,32768]{1,0:T(1,128)} %param.14) | copy-start | bytes 393220
  61.3 38.4 %copy-start.1 = (f32[1,32768]{1,0:T(1,128)S(1)}, f32[1,32768]{1,0:T(1,128)}, u32[]{:S(2)}) copy-start(f32[1,32768]{1,0:T(1,128)} %param.15) | copy-start | bytes 393220
  61.3 38.4 %copy-start.3 = (s32[1,32]{1,0:T(1,128)S(1)}, s32[1,32]{1,0:T(1,128)}, u32[]{:S(2)}) copy-start(s32[1,32]{1,0:T(1,128)} %need_ref.3) | copy-start | bytes 388

commit v5 on v3

--- a/solution.py
+++ b/solution.py
@@ -18,7 +18,6 @@
 N_OWN = 8
 N_DOM = 64
 BAND = TILES_DEV * N_DOM
-CORES = 2
 MSG = 16
 CHUNK = 256
 PER_CHUNK = CHUNK // LANES
@@ -74,7 +73,7 @@
         rows_ref[pl.ds(2 * chunk + 1, FIELDS, stride=TILE), :] = odd
         return carry
 
-    lax.fori_loop(0, TILE // 2, step, 0, unroll=4)
+    lax.fori_loop(0, TILE // 2, step, 0, unroll=8)
     out_ref[...] = rows_ref[...].astype(jnp.bfloat16)
 
 
@@ -186,14 +185,9 @@
 
 
 def interpolate_kernel(
-    place_ref,
     header_ref,
     message_ref,
-    near0,
-    near1,
-    near2,
-    near3,
-    far_ref,
+    column_ref,
     out_ref,
     tiles_ref,
     x_ref,
@@ -201,14 +195,9 @@
     part_ref,
     list_ref,
 ):
-    own = place_ref[0] // N_DOM
-    for shift, ref in enumerate((near0, near1, near2, near3)):
-        band = (own + N_OWN - CORES * shift) % N_OWN
-        tiles_ref[2 * band] = ref[:, 0:TILE]
-        tiles_ref[2 * band + 1] = ref[:, TILE : 2 * TILE]
-        band = band + 1 - 2 * (band % CORES)
-        tiles_ref[2 * band] = far_ref[shift, :, 0:TILE]
-        tiles_ref[2 * band + 1] = far_ref[shift, :, TILE : 2 * TILE]
+    for k in range(N_OWN):
+        tiles_ref[2 * k] = column_ref[k, :, 0:TILE]
+        tiles_ref[2 * k + 1] = column_ref[k, :, TILE : 2 * TILE]
 
     packed = jnp.int32(0)
     for s in range(N_DOM):
@@ -285,11 +274,11 @@
         add_up(i, jnp.maximum(before[i], 0))
 
 
-def interpolate(place, header, message, near, far):
+def interpolate(header, message, column):
     return pl.pallas_call(
         interpolate_kernel,
         out_shape=jax.ShapeDtypeStruct((N_DOM, FIELDS * GROUPS, LANES), jnp.bfloat16),
-        in_specs=[pl.BlockSpec(memory_space=pltpu.SMEM)] * 2 + [pl.BlockSpec(memory_space=pltpu.VMEM)] * 6,
+        in_specs=[pl.BlockSpec(memory_space=pltpu.SMEM)] + [pl.BlockSpec(memory_space=pltpu.VMEM)] * 2,
         out_specs=pl.BlockSpec(memory_space=pltpu.VMEM),
         scratch_shapes=[
             pltpu.VMEM((N_OWN * TILES_DEV, FIELDS * TILE, TILE), jnp.bfloat16),
@@ -299,7 +288,7 @@
             pltpu.SMEM((CHUNKS * LIST,), jnp.int32),
         ],
         compiler_params=SMALL,
-    )(place, header, message, *near, far)
+    )(header, message, column)
 
 
 def following(x, lane):
@@ -428,12 +417,9 @@
     tiles, question = prepare(
         place, storm_track, need_tiles, slot_count, background, node_cells, node_fracs, elevation, bed_level
     )
-    near = [tiles]
-    for shift in range(CORES, N_OWN, CORES):
-        near.append(lax.ppermute(tiles, "own", [(i, (i + shift) % N_OWN) for i in range(N_OWN)]))
     message = exchange(question, "dom")
-    far = lax.ppermute(jnp.stack(near), "own", [(i, i ^ 1) for i in range(N_OWN)])
-    answers = interpolate(place, message[:, 12, 0], message, near, far)
+    column = lax.all_gather(tiles, "own")
+    answers = interpolate(message[:, 12, 0], message, column)
     returned = exchange(answers, "dom")
     forcing, surge = finish(place, need_tiles, returned, message, elevation, bed_level)
     return forcing.transpose(1, 0, 2), surge.reshape(1, -1)

time: 104 us -> 104 us (level)
  blocking collectives: 40 us -> 66.5 us
  waiting for transfers between devices: 14.1 us -> 0.01 us
  starting transfers between devices: 31.2 us -> 19.2 us
    all_gather x0 -> x1, blocking collectives: none -> 24.7 us  [shards(): column = lax.all_gather(tiles, 'own')]
    ppermute x4 -> x0, waiting for transfers between devices: 14.1 us -> none  [the longest x3 13.7 us: shards(): lax.ppermute(tiles, 'own', [(i, (i + shift) % N_OWN) for i in range(N_OWN)])]
    ppermute x4 -> x0, starting transfers between devices: 12.1 us -> none  [the longest x3 10.1 us: shards(): lax.ppermute(tiles, 'own', [(i, (i + shift) % N_OWN) for i in range(N_OWN)])]
    all_to_all x1, blocking collectives: 40 us -> 41.7 us  [exchange(): return lax.all_to_all(blocks, axis, split_axis=0, concat_axis=0, tiled=True)]
  transfers between devices with their start and end apart: 5 -> 1, of which waited for: 3 -> 0; matrix products, arithmetic and copies ran while one was open for 1% -> 0% of each run, Pallas kernels for 0% -> 0%
where the time goes in v5:
time: 104 us; the launch traced here: 103 us
  blocking collectives  66.5 us (64%)
  starting transfers between devices  19.2 us (18%)
  Pallas kernels  15.9 us (15%)
  local copies, waits for them, and re-layouts  1.25 us (1%)
    all_to_all x1, blocking collectives, exchange(): return lax.all_to_all(blocks, axis, split_axis=0, concat_axis=0, tiled=True)  41.7 us
    all_gather x1, blocking collectives, shards(): column = lax.all_gather(tiles, 'own')  24.7 us
    all_to_all x1, starting transfers between devices, exchange(): return lax.all_to_all(blocks, axis, split_axis=0, concat_axis=0, tiled=True)  19.2 us
    pallas_call x1, Pallas kernels, interpolate(): pl.pallas_call(interpolate_kernel, out_shape=jax.ShapeDtypeStruct((N_DOM,...  9.52 us
    pallas_call x1, Pallas kernels, prepare(): pl.pallas_call(prepare_kernel, grid=(1,), out_shape=(jax.ShapeDtypeStruct...  3.75 us
    pallas_call x1, Pallas kernels, finish(): pl.pallas_call(finish_kernel, out_shape=(jax.ShapeDtypeStruct(forcing, jn...  2.58 us
  transfers between devices with their start and end apart: 1, of which 0 were waited for; matrix products, arithmetic and copies ran while one was open for 0% of the time, Pallas kernels for 0%

profile of v5, /device:TPU:6, one launch (start us, length us, event | category | flops | bytes accessed | tf_op | source)
XLA Modules:
  0.0 103.4 jit_solution(2516680820357546201)
XLA Ops:
  0.6 3.8 %shard_map.95 = (bf16[384,128]{1,0:T(8,128)(2,1)}, s32[64,16,128]{2,1,0:T(8,128)}) custom-call(s32[1]{0:T(128)} %bitcast.place_ref, f32[2,5]{1,0:T(2,128)} %track_ref.1, s32[1,32]{1,0:T(1,128)} %need_ref.3, s32[32]{0:T(128)} %count_ref.1, bf16[6,2,4096]{2,1,0:T(2,128)(2,1)} %bitcast.14, s32[32,1024]{1,0:T(8,128)} %cells_ref.1, f32[2,32,1024]{2,1,0:T(8,128)} %fracs_ref.1, ...), custom_call_target="tpu_custom_call" | custom-call | tf_op jit(solution)/shard_map/pallas_call | solution.py:156
  4.4 0.0 copy-start.3
  4.4 19.2 %all-to-all-start = ((s32[64,16,128]{2,1,0:T(8,128)}), s32[64,16,128]{2,1,0:T(8,128)S(1)}, u32[]{:S(2)}, u32[]{:S(2)}) async-start(s32[64,16,128]{2,1,0:T(8,128)} %get-tuple-element.6), calls=%async_computation | async-start | bytes 1048576 | tf_op jit(solution)/shard_map/all_to_all | solution.py:408
  23.6 0.0 copy-done.3
  23.6 24.7 %all-gather = bf16[3072,128]{1,0:T(8,128)(2,1)S(1)} all-gather(bf16[384,128]{1,0:T(8,128)(2,1)S(1)} %copy-done.3), channel_id=2, replica_groups=mesh['own'=8,'dom'=64] {'own'}, dimensions={0}, use_global_device_ids=true | all-gather | bytes 884736 | tf_op jit(solution)/shard_map/all_gather | solution.py:421
  48.3 0.0 all-to-all-done.message_ref.before_ref.after_ref
  48.3 1.2 %slice_reduce_fusion.header_ref = s32[64]{0:T(128)S(1)} fusion(s32[64,16,128]{2,1,0:T(8,128)S(1)} %all-to-all-done.message_ref.before_ref.after_ref), kind=kLoop, calls=%fused_computation | loop fusion | bytes 512 | tf_op jit(solution)/shard_map/slice | solution.py:422
  49.5 9.5 %shard_map.96 = bf16[64,48,128]{2,1,0:T(8,128)(2,1)S(1)} custom-call(s32[64]{0:T(128)S(1)} %slice_reduce_fusion.header_ref, s32[64,16,128]{2,1,0:T(8,128)S(1)} %all-to-all-done.message_ref.before_ref.after_ref, bf16[8,384,128]{2,1,0:T(8,128)(2,1)S(1)} %bitcast.7), custom_call_target="tpu_custom_call" | custom-call | tf_op jit(solution)/shard_map/pallas_call | solution.py:278
  59.1 0.0 copy-start
  59.1 0.0 copy-start.1
  59.1 0.0 copy-start.2
  59.1 41.7 %all_to_all.10.returned_ref = bf16[64,48,128]{2,1,0:T(8,128)(2,1)S(1)} all-to-all(bf16[64,48,128]{2,1,0:T(8,128)(2,1)S(1)} %shard_map.96), channel_id=1, replica_groups=mesh['own'=8,'dom'=64] {'dom'}, dimensions={0} | all-to-all | bytes 1572864 | tf_op jit(solution)/shard_map/all_to_all | solution.py:408
  100.8 0.0 copy-done
  100.8 0.0 copy-done.1
  100.8 0.0 copy-done.2
  100.8 2.6 %shard_map.97 = (bf16[6,32,1024]{2,1,0:T(8,128)(2,1)}, f32[256,128]{1,0:T(8,128)}) custom-call(s32[1]{0:T(128)} %bitcast.place_ref, s32[1,32]{1,0:T(1,128)S(1)} %copy-done.2, bf16[64,48,128]{2,1,0:T(8,128)(2,1)S(1)} %all_to_all.10.returned_ref, s32[64,16,128]{2,1,0:T(8,128)S(1)} %all-to-all-done.message_ref.before_ref.after_ref, ...), custom_call_target="tpu_custom_call" | custom-call | tf_op jit(solution)/shard_map/pallas_call | solution.py:381
Async XLA Ops:
  4.4 19.2 %copy-start.3 = (bf16[384,128]{1,0:T(8,128)(2,1)S(1)}, bf16[384,128]{1,0:T(8,128)(2,1)}, u32[]{:S(2)}) copy-start(bf16[384,128]{1,0:T(8,128)(2,1)} %get-tuple-element.7) | copy-start | bytes 294916
  4.4 43.9 %all-to-all-start = ((s32[64,16,128]{2,1,0:T(8,128)}), s32[64,16,128]{2,1,0:T(8,128)S(1)}, u32[]{:S(2)}, u32[]{:S(2)}) async-start(s32[64,16,128]{2,1,0:T(8,128)} %get-tuple-element.6), calls=%async_computation | async-start | bytes 1048576 | tf_op jit(solution)/shard_map/all_to_all | solution.py:408
  59.1 41.8 %copy-start = (f32[1,32768]{1,0:T(1,128)S(1)}, f32[1,32768]{1,0:T(1,128)}, u32[]{:S(2)}) copy-start(f32[1,32768]{1,0:T(1,128)} %param.14) | copy-start | bytes 393220
  59.1 41.8 %copy-start.1 = (f32[1,32768]{1,0:T(1,128)S(1)}, f32[1,32768]{1,0:T(1,128)}, u32[]{:S(2)}) copy-start(f32[1,32768]{1,0:T(1,128)} %param.15) | copy-start | bytes 393220
  59.1 41.7 %copy-start.2 = (s32[1,32]{1,0:T(1,128)S(1)}, s32[1,32]{1,0:T(1,128)}, u32[]{:S(2)}) copy-start(s32[1,32]{1,0:T(1,128)} %need_ref.3) | copy-start | bytes 388

commit v6 on v3

--- a/solution.py
+++ b/solution.py
@@ -74,7 +74,7 @@
         rows_ref[pl.ds(2 * chunk + 1, FIELDS, stride=TILE), :] = odd
         return carry
 
-    lax.fori_loop(0, TILE // 2, step, 0, unroll=4)
+    lax.fori_loop(0, TILE // 2, step, 0, unroll=8)
     out_ref[...] = rows_ref[...].astype(jnp.bfloat16)
 
 
@@ -183,6 +183,7 @@
 
 
 SLOT_ROWS = FIELDS * GROUPS * 8
+HALF = FIELDS // 2
 
 
 def interpolate_kernel(
@@ -202,13 +203,15 @@
     list_ref,
 ):
     own = place_ref[0] // N_DOM
+
+    def keep(band, pair):
+        tiles_ref[2 * band] = pair
+        tiles_ref[2 * band + 1] = pltpu.roll(pair, TILE, 1)
+
     for shift, ref in enumerate((near0, near1, near2, near3)):
         band = (own + N_OWN - CORES * shift) % N_OWN
-        tiles_ref[2 * band] = ref[:, 0:TILE]
-        tiles_ref[2 * band + 1] = ref[:, TILE : 2 * TILE]
-        band = band + 1 - 2 * (band % CORES)
-        tiles_ref[2 * band] = far_ref[shift, :, 0:TILE]
-        tiles_ref[2 * band + 1] = far_ref[shift, :, TILE : 2 * TILE]
+        keep(band, ref[...])
+        keep(band + 1 - 2 * (band % CORES), far_ref[shift])
 
     packed = jnp.int32(0)
     for s in range(N_DOM):
@@ -249,18 +252,21 @@
             add_up(i, before[i])
         for i in range(2):
             decode(i, slots[i])
-        tiles = [tiles_ref[header_ref[s] & 0xFFFF] for s in slots]
+        tiles = [tiles_ref[header_ref[s] & 0xFFFF, :, 0:TILE] for s in slots]
         for c in range(live):
             for i in range(2):
                 groups = range(c * PER_CHUNK, (c + 1) * PER_CHUNK)
                 columns = jnp.concatenate([hat(x_ref, 8 * i + g).astype(jnp.bfloat16) for g in groups], axis=1)
-                spread = jnp.dot(tiles[i], columns, preferred_element_type=jnp.float32)
-                for j, g in enumerate(groups):
-                    rows = hat(y_ref, 8 * i + g)
-                    for f in range(FIELDS):
-                        weighed = spread[f * TILE : (f + 1) * TILE, j * LANES : (j + 1) * LANES] * rows
+                rows = jnp.concatenate([hat(y_ref, 8 * i + g) for g in groups], axis=1)
+                for f in range(FIELDS):
+                    if f % HALF == 0:
+                        part = tiles[i][f * TILE : (f + HALF) * TILE]
+                        spread = jnp.dot(part, columns, preferred_element_type=jnp.float32)
+                    weighed = spread[f % HALF * TILE : (f % HALF + 1) * TILE] * rows
+                    total = jnp.sum(weighed.reshape(TILE // 8, 8, CHUNK), axis=0)
+                    for j, g in enumerate(groups):
                         at = i * SLOT_ROWS + (f * GROUPS + g) * 8
-                        part_ref[at : at + 8, :] = jnp.sum(weighed.reshape(TILE // 8, 8, LANES), axis=0)
+                        part_ref[at : at + 8, :] = total[:, j * LANES : (j + 1) * LANES]
         dead = (CHUNKS - live) * PER_CHUNK * 8
         if dead:
             for i in range(2):
@@ -292,7 +298,7 @@
         in_specs=[pl.BlockSpec(memory_space=pltpu.SMEM)] * 2 + [pl.BlockSpec(memory_space=pltpu.VMEM)] * 6,
         out_specs=pl.BlockSpec(memory_space=pltpu.VMEM),
         scratch_shapes=[
-            pltpu.VMEM((N_OWN * TILES_DEV, FIELDS * TILE, TILE), jnp.bfloat16),
+            pltpu.VMEM((N_OWN * TILES_DEV, FIELDS * TILE, LANES), jnp.bfloat16),
             pltpu.VMEM((2 * GROUPS, LANES), jnp.float32),
             pltpu.VMEM((2 * GROUPS, LANES), jnp.float32),
             pltpu.VMEM((2 * SLOT_ROWS, LANES), jnp.float32),

time: 104 us -> 104 us (level)
  no operation moved by 1% of the time
where the time goes in v6:
time: 104 us; the launch traced here: 103 us
  blocking collectives  40 us (38%)
  starting transfers between devices  31.2 us (30%)
  Pallas kernels  15.4 us (15%)
  waiting for transfers between devices  14.1 us (14%)
  local copies, waits for them, and re-layouts  1.25 us (1%)
    all_to_all x1, blocking collectives, exchange(): return lax.all_to_all(blocks, axis, split_axis=0, concat_axis=0, tiled=True)  40 us
    all_to_all x1, starting transfers between devices, exchange(): return lax.all_to_all(blocks, axis, split_axis=0, concat_axis=0, tiled=True)  19.2 us
    ppermute x3, waiting for transfers between devices, shards(): lax.ppermute(tiles, 'own', [(i, (i + shift) % N_OWN) for i in range(N_OWN)])  13.7 us
    ppermute x3, starting transfers between devices, shards(): lax.ppermute(tiles, 'own', [(i, (i + shift) % N_OWN) for i in range(N_OWN)])  10.1 us
    pallas_call x1, Pallas kernels, interpolate(): pl.pallas_call(interpolate_kernel, out_shape=jax.ShapeDtypeStruct((N_DOM,...  9.03 us
    pallas_call x1, Pallas kernels, prepare(): pl.pallas_call(prepare_kernel, grid=(1,), out_shape=(jax.ShapeDtypeStruct...  3.76 us
    pallas_call x1, Pallas kernels, finish(): pl.pallas_call(finish_kernel, out_shape=(jax.ShapeDtypeStruct(forcing, jn...  2.58 us
  transfers between devices with their start and end apart: 5, of which 3 were waited for; matrix products, arithmetic and copies ran while one was open for 1% of the time, Pallas kernels for 0%

profile of v6, /device:TPU:6, one launch (start us, length us, event | category | flops | bytes accessed | tf_op | source)
XLA Modules:
  0.0 102.7 jit_solution(13168711900687784223)
XLA Ops:
  0.6 3.8 %shard_map.95 = (bf16[384,128]{1,0:T(8,128)(2,1)}, s32[64,16,128]{2,1,0:T(8,128)}) custom-call(s32[1]{0:T(128)} %bitcast.place_ref, f32[2,5]{1,0:T(2,128)} %track_ref.1, s32[1,32]{1,0:T(1,128)} %need_ref.3, s32[32]{0:T(128)} %count_ref.1, bf16[6,2,4096]{2,1,0:T(2,128)(2,1)} %bitcast.20, s32[32,1024]{1,0:T(8,128)} %cells_ref.1, f32[2,32,1024]{2,1,0:T(8,128)} %fracs_ref.1, ...), custom_call_target="tpu_custom_call" | custom-call | tf_op jit(solution)/shard_map/pallas_call | solution.py:157
  4.4 0.0 copy-start.2
  4.4 19.2 %all-to-all-start = ((s32[64,16,128]{2,1,0:T(8,128)}), s32[64,16,128]{2,1,0:T(8,128)S(1)}, u32[]{:S(2)}, u32[]{:S(2)}) async-start(s32[64,16,128]{2,1,0:T(8,128)} %get-tuple-element.6), calls=%async_computation | async-start | bytes 1048576 | tf_op jit(solution)/shard_map/all_to_all | solution.py:425
  23.6 0.0 copy-done.2
  23.6 5.2 %collective-permute-start.2 = (bf16[384,128]{1,0:T(8,128)(2,1)S(1)}, bf16[384,128]{1,0:T(8,128)(2,1)S(1)}, u32[]{:S(2)}, u32[]{:S(2)}) collective-permute-start(bf16[384,128]{1,0:T(8,128)(2,1)S(1)} %copy-done.2), channel_id=1, source_target_pairs={{0,384},{64,448},{128,0},{192,64},{256,128},{320,192},{384,256},{4... | collective-permute-start | bytes 294920 | tf_op jit(solution)/shard_map/ppermute | solution.py:439
  28.8 1.9 %collective-permute-start.1 = (bf16[384,128]{1,0:T(8,128)(2,1)S(1)}, bf16[384,128]{1,0:T(8,128)(2,1)S(1)}, u32[]{:S(2)}, u32[]{:S(2)}) collective-permute-start(bf16[384,128]{1,0:T(8,128)(2,1)S(1)} %copy-done.2), channel_id=1, source_target_pairs={{0,256},{64,320},{128,384},{192,448},{256,0},{320,64},{384,128},{4... | collective-permute-start | bytes 294920 | tf_op jit(solution)/shard_map/ppermute | solution.py:439
  30.7 3.0 %collective-permute-start = (bf16[384,128]{1,0:T(8,128)(2,1)S(1)}, bf16[384,128]{1,0:T(8,128)(2,1)S(1)}, u32[]{:S(2)}, u32[]{:S(2)}) collective-permute-start(bf16[384,128]{1,0:T(8,128)(2,1)S(1)} %copy-done.2), channel_id=1, source_target_pairs={{0,128},{64,192},{128,256},{192,320},{256,384},{320,448},{384,0},{... | collective-permute-start | bytes 294920 | tf_op jit(solution)/shard_map/ppermute | solution.py:439
  33.7 5.6 %collective-permute-done.2.near3 = bf16[384,128]{1,0:T(8,128)(2,1)S(1)} collective-permute-done((bf16[384,128]{1,0:T(8,128)(2,1)S(1)}, bf16[384,128]{1,0:T(8,128)(2,1)S(1)}, u32[]{:S(2)}, u32[]{:S(2)}) %collective-permute-start.2) | collective-permute-done | bytes 98336 | tf_op jit(solution)/shard_map/ppermute | solution.py:439
  39.4 8.0 %collective-permute-done.1.near2 = bf16[384,128]{1,0:T(8,128)(2,1)S(1)} collective-permute-done((bf16[384,128]{1,0:T(8,128)(2,1)S(1)}, bf16[384,128]{1,0:T(8,128)(2,1)S(1)}, u32[]{:S(2)}, u32[]{:S(2)}) %collective-permute-start.1) | collective-permute-done | bytes 98336 | tf_op jit(solution)/shard_map/ppermute | solution.py:439
  47.4 0.0 collective-permute-done.near1
  47.4 0.1 pad_maximum_fusion
  47.5 1.9 %collective-permute-start.3 = (bf16[4,384,128]{2,1,0:T(8,128)(2,1)S(1)}, bf16[4,384,128]{2,1,0:T(8,128)(2,1)S(1)}, u32[]{:S(2)}, u32[]{:S(2)}) collective-permute-start(bf16[4,384,128]{2,1,0:T(8,128)(2,1)S(1)} %pad_maximum_fusion), channel_id=1, source_target_pairs={{0,64},{64,0},{128,192},{192,128},{256,320},{320,256},{384,448},{4... | collective-permute-start | bytes 1179656 | tf_op jit(solution)/shard_map/ppermute | solution.py:441
  49.4 0.0 all-to-all-done.message_ref.before_ref.after_ref
  49.4 1.2 %slice_reduce_fusion.header_ref = s32[64]{0:T(128)S(1)} fusion(s32[64,16,128]{2,1,0:T(8,128)S(1)} %all-to-all-done.message_ref.before_ref.after_ref), kind=kLoop, calls=%fused_computation.1 | loop fusion | bytes 512 | tf_op jit(solution)/shard_map/slice | solution.py:442
  50.6 0.5 collective-permute-done.3.far_ref
  51.1 9.0 %shard_map.96 = bf16[64,48,128]{2,1,0:T(8,128)(2,1)S(1)} custom-call(s32[1]{0:T(128)} %bitcast.place_ref, s32[64]{0:T(128)S(1)} %slice_reduce_fusion.header_ref, s32[64,16,128]{2,1,0:T(8,128)S(1)} %all-to-all-done.message_ref.before_ref.after_ref, bf16[384,128]{1,0:T(8,128)(2,1)S(1)} %copy-done.2, bf16[384,128]{1,0:T(8,128)(2,1)S(1)} %collective-permute-done.near1, ...), custom_call_target="tpu_custom_call" | custom-call | tf_op jit(solution)/shard_map/pallas_call | solution.py:295
  60.1 0.0 copy-start
  60.1 0.0 copy-start.1
  60.1 0.0 copy-start.3
  60.1 40.0 %all_to_all.10.returned_ref = bf16[64,48,128]{2,1,0:T(8,128)(2,1)S(1)} all-to-all(bf16[64,48,128]{2,1,0:T(8,128)(2,1)S(1)} %shard_map.96), channel_id=1, replica_groups=mesh['own'=8,'dom'=64] {'dom'}, dimensions={0} | all-to-all | bytes 1572864 | tf_op jit(solution)/shard_map/all_to_all | solution.py:425
  100.1 0.0 copy-done
  100.2 0.0 copy-done.1
  100.2 0.0 copy-done.3
  100.2 2.6 %shard_map.97 = (bf16[6,32,1024]{2,1,0:T(8,128)(2,1)}, f32[256,128]{1,0:T(8,128)}) custom-call(s32[1]{0:T(128)} %bitcast.place_ref, s32[1,32]{1,0:T(1,128)S(1)} %copy-done.3, bf16[64,48,128]{2,1,0:T(8,128)(2,1)S(1)} %all_to_all.10.returned_ref, s32[64,16,128]{2,1,0:T(8,128)S(1)} %all-to-all-done.message_ref.before_ref.after_ref, ...), custom_call_target="tpu_custom_call" | custom-call | tf_op jit(solution)/shard_map/pallas_call | solution.py:398
Async XLA Ops:
  4.4 19.2 %copy-start.2 = (bf16[384,128]{1,0:T(8,128)(2,1)S(1)}, bf16[384,128]{1,0:T(8,128)(2,1)}, u32[]{:S(2)}) copy-start(bf16[384,128]{1,0:T(8,128)(2,1)} %get-tuple-element.7.near0) | copy-start | bytes 294916
  4.4 45.0 %all-to-all-start = ((s32[64,16,128]{2,1,0:T(8,128)}), s32[64,16,128]{2,1,0:T(8,128)S(1)}, u32[]{:S(2)}, u32[]{:S(2)}) async-start(s32[64,16,128]{2,1,0:T(8,128)} %get-tuple-element.6), calls=%async_computation | async-start | bytes 1048576 | tf_op jit(solution)/shard_map/all_to_all | solution.py:425
  23.6 15.8 %collective-permute-start.2 = (bf16[384,128]{1,0:T(8,128)(2,1)S(1)}, bf16[384,128]{1,0:T(8,128)(2,1)S(1)}, u32[]{:S(2)}, u32[]{:S(2)}) collective-permute-start(bf16[384,128]{1,0:T(8,128)(2,1)S(1)} %copy-done.2), channel_id=1, source_target_pairs={{0,384},{64,448},{128,0},{192,64},{256,128},{320,192},{384,256},{4... | collective-permute-start | bytes 294920 | tf_op jit(solution)/shard_map/ppermute | solution.py:439
  28.8 18.6 %collective-permute-start.1 = (bf16[384,128]{1,0:T(8,128)(2,1)S(1)}, bf16[384,128]{1,0:T(8,128)(2,1)S(1)}, u32[]{:S(2)}, u32[]{:S(2)}) collective-permute-start(bf16[384,128]{1,0:T(8,128)(2,1)S(1)} %copy-done.2), channel_id=1, source_target_pairs={{0,256},{64,320},{128,384},{192,448},{256,0},{320,64},{384,128},{4... | collective-permute-start | bytes 294920 | tf_op jit(solution)/shard_map/ppermute | solution.py:439
  30.7 16.7 %collective-permute-start = (bf16[384,128]{1,0:T(8,128)(2,1)S(1)}, bf16[384,128]{1,0:T(8,128)(2,1)S(1)}, u32[]{:S(2)}, u32[]{:S(2)}) collective-permute-start(bf16[384,128]{1,0:T(8,128)(2,1)S(1)} %copy-done.2), channel_id=1, source_target_pairs={{0,128},{64,192},{128,256},{192,320},{256,384},{320,448},{384,0},{... | collective-permute-start | bytes 294920 | tf_op jit(solution)/shard_map/ppermute | solution.py:439
  47.5 3.6 %collective-permute-start.3 = (bf16[4,384,128]{2,1,0:T(8,128)(2,1)S(1)}, bf16[4,384,128]{2,1,0:T(8,128)(2,1)S(1)}, u32[]{:S(2)}, u32[]{:S(2)}) collective-permute-start(bf16[4,384,128]{2,1,0:T(8,128)(2,1)S(1)} %pad_maximum_fusion), channel_id=1, source_target_pairs={{0,64},{64,0},{128,192},{192,128},{256,320},{320,256},{384,448},{4... | collective-permute-start | bytes 1179656 | tf_op jit(solution)/shard_map/ppermute | solution.py:441
  60.1 40.0 %copy-start = (f32[1,32768]{1,0:T(1,128)S(1)}, f32[1,32768]{1,0:T(1,128)}, u32[]{:S(2)}) copy-start(f32[1,32768]{1,0:T(1,128)} %param.14) | copy-start | bytes 393220
  60.1 40.0 %copy-start.1 = (f32[1,32768]{1,0:T(1,128)S(1)}, f32[1,32768]{1,0:T(1,128)}, u32[]{:S(2)}) copy-start(f32[1,32768]{1,0:T(1,128)} %param.15) | copy-start | bytes 393220
  60.1 40.0 %copy-start.3 = (s32[1,32]{1,0:T(1,128)S(1)}, s32[1,32]{1,0:T(1,128)}, u32[]{:S(2)}) copy-start(s32[1,32]{1,0:T(1,128)} %need_ref.3) | copy-start | bytes 388

commit v7 on v6

--- a/solution.py
+++ b/solution.py
@@ -19,15 +19,15 @@
 N_DOM = 64
 BAND = TILES_DEV * N_DOM
 CORES = 2
-MSG = 16
+MSG = 12
+QUARTERS = 3
+NOTHING = 0xFFFF
 CHUNK = 256
 PER_CHUNK = CHUNK // LANES
 CHUNKS = NPS // CHUNK
 FIELD_BITS = 10
 ABSENT = (CHUNKS - 1) * FIELD_BITS << 16
 LIST = 8 * FIELD_BITS
-DEAD_CELL = 0xFFC0
-EDGE_SCALE = 2.0**29
 FX_STEP = 2.0**-16
 FY_TOP = 65535.0
 
@@ -82,15 +82,11 @@
     scaled = fraction * 32768.0
     whole = jnp.floor(scaled)
     code = 2.0 * whole + jnp.where(scaled > whole, 1.0, 0.0)
-    return jnp.minimum(code, 65535.0).astype(jnp.int32)
+    return jnp.minimum(code, 65534.0).astype(jnp.int32)
 
 
 def row_code(fraction):
     return jnp.floor(fraction * FY_TOP + 0.5).astype(jnp.int32)
-
-
-def edge_code(value):
-    return jnp.floor(value * EDGE_SCALE + 0.5).astype(jnp.int32)
 
 
 def prepare_kernel(
@@ -107,6 +103,8 @@
     btail_ref,
     tiles_ref,
     out_ref,
+    first_ref,
+    last_ref,
     rows_ref,
     stage_ref,
 ):
@@ -119,33 +117,34 @@
         low = row_code(fracs_ref[1, :, g * LANES : (g + 1) * LANES])
         high = row_code(fracs_ref[1, :, NPS // 2 + g * LANES : NPS // 2 + (g + 1) * LANES])
         stage_ref[pl.ds(GROUPS + g, NEED, stride=MSG), :] = low | (high << 16)
-    row = iota((8, LANES), 0)
-    lane = iota((8, LANES), 1)
-    position = row * LANES + lane
-    surface = jnp.where(lane < SWEEPS, ehead_ref[0:1, :], etail_ref[7:8, :])
-    bed = jnp.where(lane < SWEEPS, bhead_ref[0:1, :], btail_ref[7:8, :])
-    plain = jnp.where(row == 5, edge_code(surface), jnp.where(row == 6, edge_code(bed), ABSENT))
+    first_ref[0:1, :] = ehead_ref[0:1, :]
+    first_ref[1:2, :] = bhead_ref[0:1, :]
+    last_ref[0:1, :] = etail_ref[7:8, :]
+    last_ref[1:2, :] = btail_ref[7:8, :]
+    first_ref[2:8, :] = jnp.zeros((6, LANES), jnp.float32)
+    last_ref[2:8, :] = jnp.zeros((6, LANES), jnp.float32)
+    position = iota((4, LANES), 0) * LANES + iota((4, LANES), 1)
+    nothing = jnp.full((4, LANES), -1, jnp.int32)
 
     def clear(d, carry):
-        out_ref[d, 8:16, :] = plain
+        out_ref[d, 0] = nothing
         return carry
 
     lax.fori_loop(0, N_DOM, clear, 0, unroll=8)
 
-    def place(s, carry):
+    def ask(s, carry):
         tile = need_ref[0, s]
         count = count_ref[s]
         holder = tile % BAND // TILES_DEV
-        live = jnp.maximum((count + CHUNK - 1) // CHUNK, 2)
-        header = (tile // BAND * TILES_DEV + tile % TILES_DEV) | ((live - 2) * FIELD_BITS << 16)
-        start = pl.multiple_of(s * MSG, MSG)
-        out_ref[holder, 0:8, :] = jnp.where(position < count, stage_ref[pl.ds(start, 8), :], DEAD_CELL)
-        out_ref[holder, 8:16, :] = jnp.where(
-            row < 4, stage_ref[pl.ds(start + 8, 8), :], jnp.where(row == 4, header, plain)
-        )
+        start = (tile // BAND * TILES_DEV + tile % TILES_DEV) * (TILE * TILE)
+        at = pl.multiple_of(s * MSG, 4)
+        for h in range(2):
+            words = stage_ref[pl.ds(at + 4 * h, 4), :] | start
+            out_ref[holder, h] = jnp.where(position + h * (NPS // 2) < count, words, nothing)
+        out_ref[holder, 2] = stage_ref[pl.ds(at + 8, 4), :]
         return carry
 
-    lax.fori_loop(0, NEED, place, 0, unroll=4)
+    lax.fori_loop(0, NEED, ask, 0, unroll=4)
 
 
 def prepare(place, storm_track, need_tiles, slot_count, background, node_cells, node_fracs, elevation, bed_level):
@@ -159,10 +158,12 @@
         grid=(1,),
         out_shape=(
             jax.ShapeDtypeStruct((rows, LANES), jnp.bfloat16),
-            jax.ShapeDtypeStruct((N_DOM, MSG, LANES), jnp.int32),
+            jax.ShapeDtypeStruct((N_DOM, QUARTERS, 4, LANES), jnp.int32),
+            jax.ShapeDtypeStruct((8, LANES), jnp.float32),
+            jax.ShapeDtypeStruct((8, LANES), jnp.float32),
         ),
         in_specs=[pl.BlockSpec(memory_space=pltpu.SMEM)] * 4 + [vmem] * 3 + [head, tail, head, tail],
-        out_specs=(vmem, vmem),
+        out_specs=(vmem,) * 4,
         scratch_shapes=[
             pltpu.VMEM((rows, LANES), jnp.float32),
             pltpu.VMEM((NEED * MSG, LANES), jnp.int32),
@@ -235,17 +236,15 @@
         return jnp.maximum(1.0 - jnp.abs(spot - ref[at : at + 1, :]), 0.0)
 
     def decode(i, s):
-        word = message_ref[s, 0:8, :]
-        pair = message_ref[s, 8:16, :]
-        cell = word & 0xFFFF
-        row = (cell // TILE).astype(jnp.float32)
-        low = (pair[0:4] & 0xFFFF).astype(jnp.float32)
-        high = lax.shift_right_logical(pair[0:4], 16).astype(jnp.float32)
-        x_ref[8 * i : 8 * i + 8, :] = (cell & (TILE - 1)).astype(jnp.float32) + lax.shift_right_logical(
-            word, 16
-        ).astype(jnp.float32) * FX_STEP
-        y_ref[8 * i : 8 * i + 4, :] = row[0:4] + low * (1.0 / FY_TOP)
-        y_ref[8 * i + 4 : 8 * i + 8, :] = row[4:8] + high * (1.0 / FY_TOP)
+        pair = message_ref[s, 2]
+        for h in range(2):
+            word = message_ref[s, h]
+            column = lax.shift_right_logical(word, 16)
+            row_part = lax.shift_right_logical(pair, 16) if h else pair & 0xFFFF
+            row = ((word >> 6) & (TILE - 1)).astype(jnp.float32) + row_part.astype(jnp.float32) * (1.0 / FY_TOP)
+            here = slice(8 * i + 4 * h, 8 * i + 4 * h + 4)
+            x_ref[here, :] = (word & (TILE - 1)).astype(jnp.float32) + column.astype(jnp.float32) * FX_STEP
+            y_ref[here, :] = jnp.where(column == NOTHING, -4.0, row)
 
     def two_slots(slots, before, live):
         for i in range(2):
@@ -324,14 +323,14 @@
     row8 = iota((8, LANES), 0)
 
     def ends(which):
-        before = before_ref[0, which : which + 1, :].astype(jnp.float32) * (1.0 / EDGE_SCALE)
-        after = after_ref[0, which : which + 1, :].astype(jnp.float32) * (1.0 / EDGE_SCALE)
+        before = before_ref[which : which + 1, :]
+        after = after_ref[which : which + 1, :]
         top = jnp.where((row8 == 7) & (lane8 >= LANES - SWEEPS), before, 0.0)
         bottom = jnp.where((row8 == 0) & (lane8 < SWEEPS), after, 0.0)
         return top, bottom
 
-    surface_top, surface_bottom = ends(5)
-    bed_top, bed_bottom = ends(6)
+    surface_top, surface_bottom = ends(0)
+    bed_top, bed_bottom = ends(1)
     surface = jnp.concatenate([surface_top, elevation_ref[...], surface_bottom], axis=0)
     bed = jnp.concatenate([bed_top, bed_ref[...], bed_bottom], axis=0)
     lane = iota(surface.shape, 1)
@@ -387,12 +386,9 @@
     lax.fori_loop(0, NEED // SLOTS8, eight_slots, 0)
 
 
-def finish(place, need_tiles, returned, message, elevation, bed_level):
+def finish(place, need_tiles, returned, before, after, elevation, bed_level):
     def whole(shape):
         return pl.BlockSpec(shape, lambda i, *refs: (0,) * len(shape))
-
-    def neighbour(step):
-        return pl.BlockSpec((1, 8, LANES), lambda i, place_ref, need_ref: ((place_ref[0] + step) % N_DOM, 1, 0))
 
     forcing = (FIELDS, NEED, NPS)
     return pl.pallas_call(
@@ -406,8 +402,8 @@
             grid=(1,),
             in_specs=[
                 whole(returned.shape),
-                neighbour(N_DOM - 1),
-                neighbour(1),
+                whole(before.shape),
+                whole(after.shape),
                 whole(elevation.shape),
                 whole(elevation.shape),
             ],
@@ -418,7 +414,7 @@
             ],
         ),
         compiler_params=SMALL,
-    )(place, need_tiles, returned, message, message, elevation, bed_level)
+    )(place, need_tiles, returned, before, after, elevation, bed_level)
 
 
 def exchange(blocks, axis):
@@ -431,7 +427,7 @@
     place = (lax.axis_index("own") * N_DOM + lax.axis_index("dom"))[None].astype(jnp.int32)
     elevation = elevation.reshape(-1, LANES)
     bed_level = bed_level.reshape(-1, LANES)
-    tiles, question = prepare(
+    tiles, question, first, last = prepare(
         place, storm_track, need_tiles, slot_count, background, node_cells, node_fracs, elevation, bed_level
     )
     near = [tiles]
@@ -439,9 +435,15 @@
         near.append(lax.ppermute(tiles, "own", [(i, (i + shift) % N_OWN) for i in range(N_OWN)]))
     message = exchange(question, "dom")
     far = lax.ppermute(jnp.stack(near), "own", [(i, i ^ 1) for i in range(N_OWN)])
-    answers = interpolate(place, message[:, 12, 0], message, near, far)
+    before = lax.ppermute(last, "dom", [(i, i + 1) for i in range(N_DOM - 1)])
+    after = lax.ppermute(first, "dom", [(i + 1, i) for i in range(N_DOM - 1)])
+    start, middle, late = message[:, 0, 0, 0], message[:, 1, 0, 0], message[:, 1, 2, 0]
+    live = FIELD_BITS * ((middle >> 16 != -1).astype(jnp.int32) + (late >> 16 != -1).astype(jnp.int32))
+    header = jnp.where(start >> 16 == -1, ABSENT, (start >> 12 & 15) | live << 16)
+    header, before, after = lax.optimization_barrier((header, before, after))
+    answers = interpolate(place, header, message, near, far)
     returned = exchange(answers, "dom")
-    forcing, surge = finish(place, need_tiles, returned, message, elevation, bed_level)
+    forcing, surge = finish(place, need_tiles, returned, before, after, elevation, bed_level)
     return forcing.transpose(1, 0, 2), surge.reshape(1, -1)
 
 

time: 104 us -> 115 us (1.11)
  starting transfers between devices: 31.2 us -> 39.4 us
  waiting for transfers between devices: 14.1 us -> 19.3 us
  other arithmetic: 0.05 us -> 1.28 us
  local copies, waits for them, and re-layouts: 1.25 us -> 0.03 us
    ppermute x0 -> x2, waiting for transfers between devices: none -> 8.34 us  [the longest x1 8.34 us: shards(): after = lax.ppermute(first, 'dom', [(i + 1, i) for i in range(N_DOM - 1)])]
    ppermute x0 -> x2, starting transfers between devices: none -> 8.21 us  [the longest x1 6.29 us: shards(): before = lax.ppermute(last, 'dom', [(i, i + 1) for i in range(N_DOM - 1)])]
    ppermute x3, waiting for transfers between devices: 13.7 us -> 10.9 us  [shards(): lax.ppermute(tiles, 'own', [(i, (i + shift) % N_OWN) for i in range(N_OWN)])]
    select_n x0 -> x1, other arithmetic: none -> 1.23 us  [shards(): header = jnp.where(start >> 16 == -1, ABSENT, start >> 12 & 15 | live << 16)]
    slice x1 -> x0, local copies, waits for them, and re-layouts: 1.22 us -> none  [shards(): answers = interpolate(place, message[:, 12, 0], message, near, far)]
  transfers between devices with their start and end apart: 5 -> 7, of which waited for: 3 -> 3; matrix products, arithmetic and copies ran while one was open for 1% -> 1% of each run, Pallas kernels for 0% -> 0%
where the time goes in v7:
time: 115 us
  starting transfers between devices  39.4 us (34%)
  blocking collectives  38.9 us (34%)
  waiting for transfers between devices  19.3 us (17%)
  Pallas kernels  15.1 us (13%)
  other arithmetic  1.28 us (1%)
    all_to_all x1, blocking collectives, exchange(): return lax.all_to_all(blocks, axis, split_axis=0, concat_axis=0, tiled=True)  38.9 us
    all_to_all x1, starting transfers between devices, exchange(): return lax.all_to_all(blocks, axis, split_axis=0, concat_axis=0, tiled=True)  19.2 us
    ppermute x3, waiting for transfers between devices, shards(): lax.ppermute(tiles, 'own', [(i, (i + shift) % N_OWN) for i in range(N_OWN)])  10.9 us
    ppermute x3, starting transfers between devices, shards(): lax.ppermute(tiles, 'own', [(i, (i + shift) % N_OWN) for i in range(N_OWN)])  10.1 us
    pallas_call x1, Pallas kernels, interpolate(): pl.pallas_call(interpolate_kernel, out_shape=jax.ShapeDtypeStruct((N_DOM,...  9.06 us
    ppermute x1, waiting for transfers between devices, shards(): after = lax.ppermute(first, 'dom', [(i + 1, i) for i in range(N_DOM - 1)])  8.34 us
    ppermute x1, starting transfers between devices, shards(): before = lax.ppermute(last, 'dom', [(i, i + 1) for i in range(N_DOM - 1)])  6.29 us
    pallas_call x1, Pallas kernels, prepare(): pl.pallas_call(prepare_kernel, grid=(1,), out_shape=(jax.ShapeDtypeStruct...  3.5 us
  transfers between devices with their start and end apart: 7, of which 3 were waited for; matrix products, arithmetic and copies ran while one was open for 1% of the time, Pallas kernels for 0%

profile of v7, /device:TPU:6, one launch (start us, length us, event | category | flops | bytes accessed | tf_op | source)
XLA Modules:
  0.0 114.8 jit_solution(9512643402697859225)
XLA Ops:
  0.6 3.5 %shard_map.95 = (bf16[384,128]{1,0:T(8,128)(2,1)}, s32[64,3,4,128]{3,2,1,0:T(4,128)}, f32[8,128]{1,0:T(8,128)}, f32[8,128]{1,0:T(8,128)}) custom-call(s32[1]{0:T(128)} %bitcast.place_ref, f32[2,5]{1,0:T(2,128)} %track_ref.1, s32[1,32]{1,0:T(1,128)} %need_ref.3, s32[32]{0:T(128)} %count_ref.1, bf16[6,2,4096]{2,1,0:T(2,128)(2,1)} %bitcast.20, ...), custom_call_target="tpu_custom_call" | custom-call | tf_op jit(solution)/shard_map/pallas_call | solution.py:156
  4.1 0.0 copy-start.2
  4.1 19.2 %all-to-all-start = ((s32[64,3,4,128]{3,2,1,0:T(4,128)}), s32[64,3,4,128]{3,2,1,0:T(4,128)S(1)}, u32[]{:S(2)}, u32[]{:S(2)}) async-start(s32[64,3,4,128]{3,2,1,0:T(4,128)} %get-tuple-element.11), calls=%async_computation | async-start | bytes 786432 | tf_op jit(solution)/shard_map/all_to_all | solution.py:421
  23.3 0.0 copy-done.2
  23.3 5.2 %collective-permute-start.4 = (bf16[384,128]{1,0:T(8,128)(2,1)S(1)}, bf16[384,128]{1,0:T(8,128)(2,1)S(1)}, u32[]{:S(2)}, u32[]{:S(2)}) collective-permute-start(bf16[384,128]{1,0:T(8,128)(2,1)S(1)} %copy-done.2), channel_id=1, source_target_pairs={{0,384},{64,448},{128,0},{192,64},{256,128},{320,192},{384,256},{4... | collective-permute-start | bytes 294920 | tf_op jit(solution)/shard_map/ppermute | solution.py:435
  28.5 1.9 %collective-permute-start.3 = (bf16[384,128]{1,0:T(8,128)(2,1)S(1)}, bf16[384,128]{1,0:T(8,128)(2,1)S(1)}, u32[]{:S(2)}, u32[]{:S(2)}) collective-permute-start(bf16[384,128]{1,0:T(8,128)(2,1)S(1)} %copy-done.2), channel_id=1, source_target_pairs={{0,256},{64,320},{128,384},{192,448},{256,0},{320,64},{384,128},{4... | collective-permute-start | bytes 294920 | tf_op jit(solution)/shard_map/ppermute | solution.py:435
  30.5 3.0 %collective-permute-start.2 = (bf16[384,128]{1,0:T(8,128)(2,1)S(1)}, bf16[384,128]{1,0:T(8,128)(2,1)S(1)}, u32[]{:S(2)}, u32[]{:S(2)}) collective-permute-start(bf16[384,128]{1,0:T(8,128)(2,1)S(1)} %copy-done.2), channel_id=1, source_target_pairs={{0,128},{64,192},{128,256},{192,320},{256,384},{320,448},{384,0},{... | collective-permute-start | bytes 294920 | tf_op jit(solution)/shard_map/ppermute | solution.py:435
  33.5 2.9 %collective-permute-done.4.near3 = bf16[384,128]{1,0:T(8,128)(2,1)S(1)} collective-permute-done((bf16[384,128]{1,0:T(8,128)(2,1)S(1)}, bf16[384,128]{1,0:T(8,128)(2,1)S(1)}, u32[]{:S(2)}, u32[]{:S(2)}) %collective-permute-start.4) | collective-permute-done | bytes 98336 | tf_op jit(solution)/shard_map/ppermute | solution.py:435
  36.4 8.0 %collective-permute-done.3.near2 = bf16[384,128]{1,0:T(8,128)(2,1)S(1)} collective-permute-done((bf16[384,128]{1,0:T(8,128)(2,1)S(1)}, bf16[384,128]{1,0:T(8,128)(2,1)S(1)}, u32[]{:S(2)}, u32[]{:S(2)}) %collective-permute-start.3) | collective-permute-done | bytes 98336 | tf_op jit(solution)/shard_map/ppermute | solution.py:435
  44.4 0.0 collective-permute-done.2.near1
  44.4 0.0 copy-start.5
  44.4 0.0 copy-start.4
  44.4 0.1 pad_maximum_fusion
  44.5 1.9 %collective-permute-start.5 = (bf16[4,384,128]{2,1,0:T(8,128)(2,1)S(1)}, bf16[4,384,128]{2,1,0:T(8,128)(2,1)S(1)}, u32[]{:S(2)}, u32[]{:S(2)}) collective-permute-start(bf16[4,384,128]{2,1,0:T(8,128)(2,1)S(1)} %pad_maximum_fusion), channel_id=1, source_target_pairs={{0,64},{64,0},{128,192},{192,128},{256,320},{320,256},{384,448},{4... | collective-permute-start | bytes 1179656 | tf_op jit(solution)/shard_map/ppermute | solution.py:437
  46.4 0.0 copy-done.5
  46.4 6.3 %collective-permute-start = (f32[8,128]{1,0:T(8,128)S(1)}, f32[8,128]{1,0:T(8,128)S(1)}, u32[]{:S(2)}, u32[]{:S(2)}) collective-permute-start(f32[8,128]{1,0:T(8,128)S(1)} %copy-done.5), channel_id=1, source_target_pairs={{0,1},{1,2},{2,3},{3,4},{4,5},{5,6},{6,7},{7,8},{8,9},{9,10},{10,1... | collective-permute-start | bytes 12296 | tf_op jit(solution)/shard_map/ppermute | solution.py:438
  52.7 0.0 copy-done.4
  52.7 1.9 %collective-permute-start.1 = (f32[8,128]{1,0:T(8,128)S(1)}, f32[8,128]{1,0:T(8,128)S(1)}, u32[]{:S(2)}, u32[]{:S(2)}) collective-permute-start(f32[8,128]{1,0:T(8,128)S(1)} %copy-done.4), channel_id=1, source_target_pairs={{1,0},{2,1},{3,2},{4,3},{5,4},{6,5},{7,6},{8,7},{9,8},{10,9},{11,1... | collective-permute-start | bytes 12296 | tf_op jit(solution)/shard_map/ppermute | solution.py:439
  54.6 0.0 all-to-all-done.message_ref
  54.6 1.2 %fusion.2.header_ref = s32[64]{0:T(128)S(1)} fusion(s32[64,3,4,128]{3,2,1,0:T(4,128)S(1)} %all-to-all-done.message_ref), kind=kLoop, calls=%fused_computation.8 | loop fusion | flops 960 | bytes 1024 | tf_op jit(solution)/shard_map/jit(_where)/select_n | solution.py:442
  55.9 0.0 collective-permute-done.before_ref
  55.9 8.3 %collective-permute-done.1.after_ref = f32[8,128]{1,0:T(8,128)S(1)} collective-permute-done((f32[8,128]{1,0:T(8,128)S(1)}, f32[8,128]{1,0:T(8,128)S(1)}, u32[]{:S(2)}, u32[]{:S(2)}) %collective-permute-start.1) | collective-permute-done | bytes 4128 | tf_op jit(solution)/shard_map/ppermute | solution.py:439
  64.2 0.0 collective-permute-done.5.far_ref
  64.2 9.1 %shard_map.96 = bf16[64,48,128]{2,1,0:T(8,128)(2,1)S(1)} custom-call(s32[1]{0:T(128)} %bitcast.place_ref, s32[64]{0:T(128)S(1)} %fusion.2.header_ref, s32[64,3,4,128]{3,2,1,0:T(4,128)S(1)} %all-to-all-done.message_ref, bf16[384,128]{1,0:T(8,128)(2,1)S(1)} %copy-done.2, bf16[384,128]{1,0:T(8,128)(2,1)S(1)} %collective-permute-done.2.near1, ...), custom_call_target="tpu_custom_call" | custom-call | tf_op jit(solution)/shard_map/pallas_call | solution.py:294
  73.3 0.0 copy-start
  73.3 0.0 copy-start.1
  73.3 0.0 copy-start.3
  73.3 38.9 %all_to_all.10.returned_ref = bf16[64,48,128]{2,1,0:T(8,128)(2,1)S(1)} all-to-all(bf16[64,48,128]{2,1,0:T(8,128)(2,1)S(1)} %shard_map.96), channel_id=1, replica_groups=mesh['own'=8,'dom'=64] {'dom'}, dimensions={0} | all-to-all | bytes 1572864 | tf_op jit(solution)/shard_map/all_to_all | solution.py:421
  112.2 0.0 copy-done
  112.2 0.0 copy-done.1
  112.2 0.0 copy-done.3
  112.2 2.6 %shard_map.97 = (bf16[6,32,1024]{2,1,0:T(8,128)(2,1)}, f32[256,128]{1,0:T(8,128)}) custom-call(s32[1]{0:T(128)} %bitcast.place_ref, s32[1,32]{1,0:T(1,128)S(1)} %copy-done.3, bf16[64,48,128]{2,1,0:T(8,128)(2,1)S(1)} %all_to_all.10.returned_ref, f32[8,128]{1,0:T(8,128)S(1)} %collective-permute-done.before_ref, f32[8,128]{1,0:T(8,128)S(1)} %collective-permute-done.1.after_ref, ...), custom_call_target="tpu_custom_call" | custom-call | tf_op jit(solution)/shard_map/pallas_call | solution.py:394
Async XLA Ops:
  4.1 19.2 %copy-start.2 = (bf16[384,128]{1,0:T(8,128)(2,1)S(1)}, bf16[384,128]{1,0:T(8,128)(2,1)}, u32[]{:S(2)}) copy-start(bf16[384,128]{1,0:T(8,128)(2,1)} %get-tuple-element.15.near0) | copy-start | bytes 294916
  4.1 50.5 %all-to-all-start = ((s32[64,3,4,128]{3,2,1,0:T(4,128)}), s32[64,3,4,128]{3,2,1,0:T(4,128)S(1)}, u32[]{:S(2)}, u32[]{:S(2)}) async-start(s32[64,3,4,128]{3,2,1,0:T(4,128)} %get-tuple-element.11), calls=%async_computation | async-start | bytes 786432 | tf_op jit(solution)/shard_map/all_to_all | solution.py:421
  23.3 13.1 %collective-permute-start.4 = (bf16[384,128]{1,0:T(8,128)(2,1)S(1)}, bf16[384,128]{1,0:T(8,128)(2,1)S(1)}, u32[]{:S(2)}, u32[]{:S(2)}) collective-permute-start(bf16[384,128]{1,0:T(8,128)(2,1)S(1)} %copy-done.2), channel_id=1, source_target_pairs={{0,384},{64,448},{128,0},{192,64},{256,128},{320,192},{384,256},{4... | collective-permute-start | bytes 294920 | tf_op jit(solution)/shard_map/ppermute | solution.py:435
  28.5 15.9 %collective-permute-start.3 = (bf16[384,128]{1,0:T(8,128)(2,1)S(1)}, bf16[384,128]{1,0:T(8,128)(2,1)S(1)}, u32[]{:S(2)}, u32[]{:S(2)}) collective-permute-start(bf16[384,128]{1,0:T(8,128)(2,1)S(1)} %copy-done.2), channel_id=1, source_target_pairs={{0,256},{64,320},{128,384},{192,448},{256,0},{320,64},{384,128},{4... | collective-permute-start | bytes 294920 | tf_op jit(solution)/shard_map/ppermute | solution.py:435
  30.5 13.9 %collective-permute-start.2 = (bf16[384,128]{1,0:T(8,128)(2,1)S(1)}, bf16[384,128]{1,0:T(8,128)(2,1)S(1)}, u32[]{:S(2)}, u32[]{:S(2)}) collective-permute-start(bf16[384,128]{1,0:T(8,128)(2,1)S(1)} %copy-done.2), channel_id=1, source_target_pairs={{0,128},{64,192},{128,256},{192,320},{256,384},{320,448},{384,0},{... | collective-permute-start | bytes 294920 | tf_op jit(solution)/shard_map/ppermute | solution.py:435
  44.4 2.0 %copy-start.5 = (f32[8,128]{1,0:T(8,128)S(1)}, f32[8,128]{1,0:T(8,128)}, u32[]{:S(2)}) copy-start(f32[8,128]{1,0:T(8,128)} %get-tuple-element.12) | copy-start | bytes 12292
  44.4 8.3 %copy-start.4 = (f32[8,128]{1,0:T(8,128)S(1)}, f32[8,128]{1,0:T(8,128)}, u32[]{:S(2)}) copy-start(f32[8,128]{1,0:T(8,128)} %get-tuple-element.13) | copy-start | bytes 12292
  44.5 19.8 %collective-permute-start.5 = (bf16[4,384,128]{2,1,0:T(8,128)(2,1)S(1)}, bf16[4,384,128]{2,1,0:T(8,128)(2,1)S(1)}, u32[]{:S(2)}, u32[]{:S(2)}) collective-permute-start(bf16[4,384,128]{2,1,0:T(8,128)(2,1)S(1)} %pad_maximum_fusion), channel_id=1, source_target_pairs={{0,64},{64,0},{128,192},{192,128},{256,320},{320,256},{384,448},{4... | collective-permute-start | bytes 1179656 | tf_op jit(solution)/shard_map/ppermute | solution.py:437
  46.4 9.5 %collective-permute-start = (f32[8,128]{1,0:T(8,128)S(1)}, f32[8,128]{1,0:T(8,128)S(1)}, u32[]{:S(2)}, u32[]{:S(2)}) collective-permute-start(f32[8,128]{1,0:T(8,128)S(1)} %copy-done.5), channel_id=1, source_target_pairs={{0,1},{1,2},{2,3},{3,4},{4,5},{5,6},{6,7},{7,8},{8,9},{9,10},{10,1... | collective-permute-start | bytes 12296 | tf_op jit(solution)/shard_map/ppermute | solution.py:438
  52.7 11.5 %collective-permute-start.1 = (f32[8,128]{1,0:T(8,128)S(1)}, f32[8,128]{1,0:T(8,128)S(1)}, u32[]{:S(2)}, u32[]{:S(2)}) collective-permute-start(f32[8,128]{1,0:T(8,128)S(1)} %copy-done.4), channel_id=1, source_target_pairs={{1,0},{2,1},{3,2},{4,3},{5,4},{6,5},{7,6},{8,7},{9,8},{10,9},{11,1... | collective-permute-start | bytes 12296 | tf_op jit(solution)/shard_map/ppermute | solution.py:439
  73.3 38.9 %copy-start = (f32[1,32768]{1,0:T(1,128)S(1)}, f32[1,32768]{1,0:T(1,128)}, u32[]{:S(2)}) copy-start(f32[1,32768]{1,0:T(1,128)} %param.14) | copy-start | bytes 393220
  73.3 38.9 %copy-start.1 = (f32[1,32768]{1,0:T(1,128)S(1)}, f32[1,32768]{1,0:T(1,128)}, u32[]{:S(2)}) copy-start(f32[1,32768]{1,0:T(1,128)} %param.15) | copy-start | bytes 393220
  73.3 38.9 %copy-start.3 = (s32[1,32]{1,0:T(1,128)S(1)}, s32[1,32]{1,0:T(1,128)}, u32[]{:S(2)}) copy-start(s32[1,32]{1,0:T(1,128)} %need_ref.3) | copy-start | bytes 388

commit v8 on v6

--- a/solution.py
+++ b/solution.py
@@ -188,7 +188,6 @@
 
 def interpolate_kernel(
     place_ref,
-    header_ref,
     message_ref,
     near0,
     near1,
@@ -201,7 +200,11 @@
     y_ref,
     part_ref,
     list_ref,
+    header_ref,
+    sem,
 ):
+    headers = pltpu.make_async_copy(message_ref.at[:, 12:13, :], header_ref, sem)
+    headers.start()
     own = place_ref[0] // N_DOM
 
     def keep(band, pair):
@@ -213,9 +216,10 @@
         keep(band, ref[...])
         keep(band + 1 - 2 * (band % CORES), far_ref[shift])
 
+    headers.wait()
     packed = jnp.int32(0)
     for s in range(N_DOM):
-        shift = header_ref[s] >> 16
+        shift = header_ref[s, 0, 0] >> 16
         list_ref[shift * 8 + (lax.shift_right_logical(packed, shift) & (2**FIELD_BITS - 1))] = s
         packed = packed + (1 << shift)
     counts = [packed >> i * FIELD_BITS & (2**FIELD_BITS - 1) for i in range(CHUNKS - 1)]
@@ -252,7 +256,7 @@
             add_up(i, before[i])
         for i in range(2):
             decode(i, slots[i])
-        tiles = [tiles_ref[header_ref[s] & 0xFFFF, :, 0:TILE] for s in slots]
+        tiles = [tiles_ref[header_ref[s, 0, 0] & 0xFFFF, :, 0:TILE] for s in slots]
         for c in range(live):
             for i in range(2):
                 groups = range(c * PER_CHUNK, (c + 1) * PER_CHUNK)
@@ -291,11 +295,11 @@
         add_up(i, jnp.maximum(before[i], 0))
 
 
-def interpolate(place, header, message, near, far):
+def interpolate(place, message, near, far):
     return pl.pallas_call(
         interpolate_kernel,
         out_shape=jax.ShapeDtypeStruct((N_DOM, FIELDS * GROUPS, LANES), jnp.bfloat16),
-        in_specs=[pl.BlockSpec(memory_space=pltpu.SMEM)] * 2 + [pl.BlockSpec(memory_space=pltpu.VMEM)] * 6,
+        in_specs=[pl.BlockSpec(memory_space=pltpu.SMEM)] + [pl.BlockSpec(memory_space=pltpu.VMEM)] * 6,
         out_specs=pl.BlockSpec(memory_space=pltpu.VMEM),
         scratch_shapes=[
             pltpu.VMEM((N_OWN * TILES_DEV, FIELDS * TILE, LANES), jnp.bfloat16),
@@ -303,9 +307,11 @@
             pltpu.VMEM((2 * GROUPS, LANES), jnp.float32),
             pltpu.VMEM((2 * SLOT_ROWS, LANES), jnp.float32),
             pltpu.SMEM((CHUNKS * LIST,), jnp.int32),
+            pltpu.SMEM((N_DOM, 1, LANES), jnp.int32),
+            pltpu.SemaphoreType.DMA,
         ],
         compiler_params=SMALL,
-    )(place, header, message, *near, far)
+    )(place, message, *near, far)
 
 
 def following(x, lane):
@@ -439,7 +445,7 @@
         near.append(lax.ppermute(tiles, "own", [(i, (i + shift) % N_OWN) for i in range(N_OWN)]))
     message = exchange(question, "dom")
     far = lax.ppermute(jnp.stack(near), "own", [(i, i ^ 1) for i in range(N_OWN)])
-    answers = interpolate(place, message[:, 12, 0], message, near, far)
+    answers = interpolate(place, message, near, far)
     returned = exchange(answers, "dom")
     forcing, surge = finish(place, need_tiles, returned, message, elevation, bed_level)
     return forcing.transpose(1, 0, 2), surge.reshape(1, -1)

time: 104 us -> 104 us (level)
  local copies, waits for them, and re-layouts: 1.25 us -> 0.02 us
  waiting for transfers between devices: 14.1 us -> 15.3 us
    ppermute x1, waiting for transfers between devices: 0.45 us -> 1.69 us  [shards(): lax.ppermute(jnp.stack(near), 'own', [(i, i ^ 1) for i in range(N_OWN)])]
    slice x1 -> x0, local copies, waits for them, and re-layouts: 1.22 us -> none  [shards(): answers = interpolate(place, message[:, 12, 0], message, near, far)]
  transfers between devices with their start and end apart: 5 -> 5, of which waited for: 3 -> 3; matrix products, arithmetic and copies ran while one was open for 1% -> 0% of each run, Pallas kernels for 0% -> 0%
where the time goes in v8:
time: 104 us; the launch traced here: 103 us
  blocking collectives  40 us (38%)
  starting transfers between devices  31.2 us (30%)
  Pallas kernels  16 us (15%)
  waiting for transfers between devices  15.3 us (15%)
    all_to_all x1, blocking collectives, exchange(): return lax.all_to_all(blocks, axis, split_axis=0, concat_axis=0, tiled=True)  40 us
    all_to_all x1, starting transfers between devices, exchange(): return lax.all_to_all(blocks, axis, split_axis=0, concat_axis=0, tiled=True)  19.2 us
    ppermute x3, waiting for transfers between devices, shards(): lax.ppermute(tiles, 'own', [(i, (i + shift) % N_OWN) for i in range(N_OWN)])  13.7 us
    ppermute x3, starting transfers between devices, shards(): lax.ppermute(tiles, 'own', [(i, (i + shift) % N_OWN) for i in range(N_OWN)])  10.1 us
    pallas_call x1, Pallas kernels, interpolate(): pl.pallas_call(interpolate_kernel, out_shape=jax.ShapeDtypeStruct((N_DOM,...  9.61 us
    pallas_call x1, Pallas kernels, prepare(): pl.pallas_call(prepare_kernel, grid=(1,), out_shape=(jax.ShapeDtypeStruct...  3.75 us
    pallas_call x1, Pallas kernels, finish(): pl.pallas_call(finish_kernel, out_shape=(jax.ShapeDtypeStruct(forcing, jn...  2.58 us
  transfers between devices with their start and end apart: 5, of which 3 were waited for; matrix products, arithmetic and copies ran while one was open for 0% of the time, Pallas kernels for 0%

profile of v8, /device:TPU:6, one launch (start us, length us, event | category | flops | bytes accessed | tf_op | source)
XLA Modules:
  0.0 103.3 jit_solution(6284355996134425959)
XLA Ops:
  0.6 3.8 %shard_map.95 = (bf16[384,128]{1,0:T(8,128)(2,1)}, s32[64,16,128]{2,1,0:T(8,128)}) custom-call(s32[1]{0:T(128)} %bitcast.place_ref, f32[2,5]{1,0:T(2,128)} %track_ref.1, s32[1,32]{1,0:T(1,128)} %need_ref.3, s32[32]{0:T(128)} %count_ref.1, bf16[6,2,4096]{2,1,0:T(2,128)(2,1)} %bitcast.20, s32[32,1024]{1,0:T(8,128)} %cells_ref.1, f32[2,32,1024]{2,1,0:T(8,128)} %fracs_ref.1, ...), custom_call_target="tpu_custom_call" | custom-call | tf_op jit(solution)/shard_map/pallas_call | solution.py:157
  4.4 0.0 copy-start.2
  4.4 19.2 %all-to-all-start = ((s32[64,16,128]{2,1,0:T(8,128)}), s32[64,16,128]{2,1,0:T(8,128)S(1)}, u32[]{:S(2)}, u32[]{:S(2)}) async-start(s32[64,16,128]{2,1,0:T(8,128)} %get-tuple-element.6), calls=%async_computation | async-start | bytes 1048576 | tf_op jit(solution)/shard_map/all_to_all | solution.py:431
  23.6 0.0 copy-done.2
  23.6 5.2 %collective-permute-start.2 = (bf16[384,128]{1,0:T(8,128)(2,1)S(1)}, bf16[384,128]{1,0:T(8,128)(2,1)S(1)}, u32[]{:S(2)}, u32[]{:S(2)}) collective-permute-start(bf16[384,128]{1,0:T(8,128)(2,1)S(1)} %copy-done.2), channel_id=1, source_target_pairs={{0,384},{64,448},{128,0},{192,64},{256,128},{320,192},{384,256},{4... | collective-permute-start | bytes 294920 | tf_op jit(solution)/shard_map/ppermute | solution.py:445
  28.8 1.9 %collective-permute-start.1 = (bf16[384,128]{1,0:T(8,128)(2,1)S(1)}, bf16[384,128]{1,0:T(8,128)(2,1)S(1)}, u32[]{:S(2)}, u32[]{:S(2)}) collective-permute-start(bf16[384,128]{1,0:T(8,128)(2,1)S(1)} %copy-done.2), channel_id=1, source_target_pairs={{0,256},{64,320},{128,384},{192,448},{256,0},{320,64},{384,128},{4... | collective-permute-start | bytes 294920 | tf_op jit(solution)/shard_map/ppermute | solution.py:445
  30.7 3.0 %collective-permute-start = (bf16[384,128]{1,0:T(8,128)(2,1)S(1)}, bf16[384,128]{1,0:T(8,128)(2,1)S(1)}, u32[]{:S(2)}, u32[]{:S(2)}) collective-permute-start(bf16[384,128]{1,0:T(8,128)(2,1)S(1)} %copy-done.2), channel_id=1, source_target_pairs={{0,128},{64,192},{128,256},{192,320},{256,384},{320,448},{384,0},{... | collective-permute-start | bytes 294920 | tf_op jit(solution)/shard_map/ppermute | solution.py:445
  33.7 5.6 %collective-permute-done.2.near3 = bf16[384,128]{1,0:T(8,128)(2,1)S(1)} collective-permute-done((bf16[384,128]{1,0:T(8,128)(2,1)S(1)}, bf16[384,128]{1,0:T(8,128)(2,1)S(1)}, u32[]{:S(2)}, u32[]{:S(2)}) %collective-permute-start.2) | collective-permute-done | bytes 98336 | tf_op jit(solution)/shard_map/ppermute | solution.py:445
  39.4 8.0 %collective-permute-done.1.near2 = bf16[384,128]{1,0:T(8,128)(2,1)S(1)} collective-permute-done((bf16[384,128]{1,0:T(8,128)(2,1)S(1)}, bf16[384,128]{1,0:T(8,128)(2,1)S(1)}, u32[]{:S(2)}, u32[]{:S(2)}) %collective-permute-start.1) | collective-permute-done | bytes 98336 | tf_op jit(solution)/shard_map/ppermute | solution.py:445
  47.4 0.0 collective-permute-done.near1
  47.4 0.1 pad_maximum_fusion
  47.4 1.9 %collective-permute-start.3 = (bf16[4,384,128]{2,1,0:T(8,128)(2,1)S(1)}, bf16[4,384,128]{2,1,0:T(8,128)(2,1)S(1)}, u32[]{:S(2)}, u32[]{:S(2)}) collective-permute-start(bf16[4,384,128]{2,1,0:T(8,128)(2,1)S(1)} %pad_maximum_fusion), channel_id=1, source_target_pairs={{0,64},{64,0},{128,192},{192,128},{256,320},{320,256},{384,448},{4... | collective-permute-start | bytes 1179656 | tf_op jit(solution)/shard_map/ppermute | solution.py:447
  49.4 1.7 %collective-permute-done.3.far_ref = bf16[4,384,128]{2,1,0:T(8,128)(2,1)S(1)} collective-permute-done((bf16[4,384,128]{2,1,0:T(8,128)(2,1)S(1)}, bf16[4,384,128]{2,1,0:T(8,128)(2,1)S(1)}, u32[]{:S(2)}, u32[]{:S(2)}) %collective-permute-start.3) | collective-permute-done | bytes 393248 | tf_op jit(solution)/shard_map/ppermute | solution.py:447
  51.1 0.0 all-to-all-done.message_ref.before_ref.after_ref
  51.1 9.6 %shard_map.96 = bf16[64,48,128]{2,1,0:T(8,128)(2,1)S(1)} custom-call(s32[1]{0:T(128)} %bitcast.place_ref, s32[64,16,128]{2,1,0:T(8,128)S(1)} %all-to-all-done.message_ref.before_ref.after_ref, bf16[384,128]{1,0:T(8,128)(2,1)S(1)} %copy-done.2, bf16[384,128]{1,0:T(8,128)(2,1)S(1)} %collective-permute-done.near1, ...), custom_call_target="tpu_custom_call" | custom-call | tf_op jit(solution)/shard_map/pallas_call | solution.py:299
  60.7 0.0 copy-start
  60.7 0.0 copy-start.1
  60.7 0.0 copy-start.3
  60.7 40.0 %all_to_all.10.returned_ref = bf16[64,48,128]{2,1,0:T(8,128)(2,1)S(1)} all-to-all(bf16[64,48,128]{2,1,0:T(8,128)(2,1)S(1)} %shard_map.96), channel_id=1, replica_groups=mesh['own'=8,'dom'=64] {'dom'}, dimensions={0} | all-to-all | bytes 1572864 | tf_op jit(solution)/shard_map/all_to_all | solution.py:431
  100.7 0.0 copy-done
  100.7 0.0 copy-done.1
  100.7 0.0 copy-done.3
  100.7 2.6 %shard_map.97 = (bf16[6,32,1024]{2,1,0:T(8,128)(2,1)}, f32[256,128]{1,0:T(8,128)}) custom-call(s32[1]{0:T(128)} %bitcast.place_ref, s32[1,32]{1,0:T(1,128)S(1)} %copy-done.3, bf16[64,48,128]{2,1,0:T(8,128)(2,1)S(1)} %all_to_all.10.returned_ref, s32[64,16,128]{2,1,0:T(8,128)S(1)} %all-to-all-done.message_ref.before_ref.after_ref, ...), custom_call_target="tpu_custom_call" | custom-call | tf_op jit(solution)/shard_map/pallas_call | solution.py:404
Async XLA Ops:
  4.4 19.2 %copy-start.2 = (bf16[384,128]{1,0:T(8,128)(2,1)S(1)}, bf16[384,128]{1,0:T(8,128)(2,1)}, u32[]{:S(2)}) copy-start(bf16[384,128]{1,0:T(8,128)(2,1)} %get-tuple-element.7.near0) | copy-start | bytes 294916
  4.4 46.7 %all-to-all-start = ((s32[64,16,128]{2,1,0:T(8,128)}), s32[64,16,128]{2,1,0:T(8,128)S(1)}, u32[]{:S(2)}, u32[]{:S(2)}) async-start(s32[64,16,128]{2,1,0:T(8,128)} %get-tuple-element.6), calls=%async_computation | async-start | bytes 1048576 | tf_op jit(solution)/shard_map/all_to_all | solution.py:431
  23.6 15.8 %collective-permute-start.2 = (bf16[384,128]{1,0:T(8,128)(2,1)S(1)}, bf16[384,128]{1,0:T(8,128)(2,1)S(1)}, u32[]{:S(2)}, u32[]{:S(2)}) collective-permute-start(bf16[384,128]{1,0:T(8,128)(2,1)S(1)} %copy-done.2), channel_id=1, source_target_pairs={{0,384},{64,448},{128,0},{192,64},{256,128},{320,192},{384,256},{4... | collective-permute-start | bytes 294920 | tf_op jit(solution)/shard_map/ppermute | solution.py:445
  28.8 18.6 %collective-permute-start.1 = (bf16[384,128]{1,0:T(8,128)(2,1)S(1)}, bf16[384,128]{1,0:T(8,128)(2,1)S(1)}, u32[]{:S(2)}, u32[]{:S(2)}) collective-permute-start(bf16[384,128]{1,0:T(8,128)(2,1)S(1)} %copy-done.2), channel_id=1, source_target_pairs={{0,256},{64,320},{128,384},{192,448},{256,0},{320,64},{384,128},{4... | collective-permute-start | bytes 294920 | tf_op jit(solution)/shard_map/ppermute | solution.py:445
  30.7 16.7 %collective-permute-start = (bf16[384,128]{1,0:T(8,128)(2,1)S(1)}, bf16[384,128]{1,0:T(8,128)(2,1)S(1)}, u32[]{:S(2)}, u32[]{:S(2)}) collective-permute-start(bf16[384,128]{1,0:T(8,128)(2,1)S(1)} %copy-done.2), channel_id=1, source_target_pairs={{0,128},{64,192},{128,256},{192,320},{256,384},{320,448},{384,0},{... | collective-permute-start | bytes 294920 | tf_op jit(solution)/shard_map/ppermute | solution.py:445
  47.4 3.6 %collective-permute-start.3 = (bf16[4,384,128]{2,1,0:T(8,128)(2,1)S(1)}, bf16[4,384,128]{2,1,0:T(8,128)(2,1)S(1)}, u32[]{:S(2)}, u32[]{:S(2)}) collective-permute-start(bf16[4,384,128]{2,1,0:T(8,128)(2,1)S(1)} %pad_maximum_fusion), channel_id=1, source_target_pairs={{0,64},{64,0},{128,192},{192,128},{256,320},{320,256},{384,448},{4... | collective-permute-start | bytes 1179656 | tf_op jit(solution)/shard_map/ppermute | solution.py:447
  60.7 40.0 %copy-start = (f32[1,32768]{1,0:T(1,128)S(1)}, f32[1,32768]{1,0:T(1,128)}, u32[]{:S(2)}) copy-start(f32[1,32768]{1,0:T(1,128)} %param.14) | copy-start | bytes 393220
  60.7 40.0 %copy-start.1 = (f32[1,32768]{1,0:T(1,128)S(1)}, f32[1,32768]{1,0:T(1,128)}, u32[]{:S(2)}) copy-start(f32[1,32768]{1,0:T(1,128)} %param.15) | copy-start | bytes 393220
  60.7 40.0 %copy-start.3 = (s32[1,32]{1,0:T(1,128)S(1)}, s32[1,32]{1,0:T(1,128)}, u32[]{:S(2)}) copy-start(s32[1,32]{1,0:T(1,128)} %need_ref.3) | copy-start | bytes 388

commit v9 on v8

--- a/solution.py
+++ b/solution.py
@@ -75,7 +75,7 @@
         return carry
 
     lax.fori_loop(0, TILE // 2, step, 0, unroll=8)
-    out_ref[...] = rows_ref[...].astype(jnp.bfloat16)
+    out_ref[...] = rows_ref[0 : FIELDS * TILE, :].astype(jnp.bfloat16)
 
 
 def column_code(fraction):
@@ -164,7 +164,7 @@
         in_specs=[pl.BlockSpec(memory_space=pltpu.SMEM)] * 4 + [vmem] * 3 + [head, tail, head, tail],
         out_specs=(vmem, vmem),
         scratch_shapes=[
-            pltpu.VMEM((rows, LANES), jnp.float32),
+            pltpu.VMEM((8 * TILE, LANES), jnp.float32),
             pltpu.VMEM((NEED * MSG, LANES), jnp.int32),
         ],
     )(
@@ -303,8 +303,8 @@
         out_specs=pl.BlockSpec(memory_space=pltpu.VMEM),
         scratch_shapes=[
             pltpu.VMEM((N_OWN * TILES_DEV, FIELDS * TILE, LANES), jnp.bfloat16),
-            pltpu.VMEM((2 * GROUPS, LANES), jnp.float32),
-            pltpu.VMEM((2 * GROUPS, LANES), jnp.float32),
+            pltpu.VMEM((3 * GROUPS, LANES), jnp.float32),
+            pltpu.VMEM((3 * GROUPS, LANES), jnp.float32),
             pltpu.VMEM((2 * SLOT_ROWS, LANES), jnp.float32),
             pltpu.SMEM((CHUNKS * LIST,), jnp.int32),
             pltpu.SMEM((N_DOM, 1, LANES), jnp.int32),

time: 104 us -> 104 us (level)
  no operation moved by 1% of the time
where the time goes in v9:
time: 104 us; the launch traced here: 103 us
  blocking collectives  40 us (38%)
  starting transfers between devices  31.2 us (30%)
  Pallas kernels  16 us (15%)
  waiting for transfers between devices  15.3 us (15%)
    all_to_all x1, blocking collectives, exchange(): return lax.all_to_all(blocks, axis, split_axis=0, concat_axis=0, tiled=True)  40 us
    all_to_all x1, starting transfers between devices, exchange(): return lax.all_to_all(blocks, axis, split_axis=0, concat_axis=0, tiled=True)  19.2 us
    ppermute x3, waiting for transfers between devices, shards(): lax.ppermute(tiles, 'own', [(i, (i + shift) % N_OWN) for i in range(N_OWN)])  13.7 us
    ppermute x3, starting transfers between devices, shards(): lax.ppermute(tiles, 'own', [(i, (i + shift) % N_OWN) for i in range(N_OWN)])  10.1 us
    pallas_call x1, Pallas kernels, interpolate(): pl.pallas_call(interpolate_kernel, out_shape=jax.ShapeDtypeStruct((N_DOM,...  9.61 us
    pallas_call x1, Pallas kernels, prepare(): pl.pallas_call(prepare_kernel, grid=(1,), out_shape=(jax.ShapeDtypeStruct...  3.75 us
    pallas_call x1, Pallas kernels, finish(): pl.pallas_call(finish_kernel, out_shape=(jax.ShapeDtypeStruct(forcing, jn...  2.58 us
  transfers between devices with their start and end apart: 5, of which 3 were waited for; matrix products, arithmetic and copies ran while one was open for 0% of the time, Pallas kernels for 0%

profile of v9, /device:TPU:6, one launch (start us, length us, event | category | flops | bytes accessed | tf_op | source)
XLA Modules:
  0.0 103.3 jit_solution(13546190508075897387)
XLA Ops:
  0.6 3.8 %shard_map.95 = (bf16[384,128]{1,0:T(8,128)(2,1)}, s32[64,16,128]{2,1,0:T(8,128)}) custom-call(s32[1]{0:T(128)} %bitcast.place_ref, f32[2,5]{1,0:T(2,128)} %track_ref.1, s32[1,32]{1,0:T(1,128)} %need_ref.3, s32[32]{0:T(128)} %count_ref.1, bf16[6,2,4096]{2,1,0:T(2,128)(2,1)} %bitcast.20, s32[32,1024]{1,0:T(8,128)} %cells_ref.1, f32[2,32,1024]{2,1,0:T(8,128)} %fracs_ref.1, ...), custom_call_target="tpu_custom_call" | custom-call | tf_op jit(solution)/shard_map/pallas_call | solution.py:157
  4.4 0.0 copy-start.2
  4.4 19.2 %all-to-all-start = ((s32[64,16,128]{2,1,0:T(8,128)}), s32[64,16,128]{2,1,0:T(8,128)S(1)}, u32[]{:S(2)}, u32[]{:S(2)}) async-start(s32[64,16,128]{2,1,0:T(8,128)} %get-tuple-element.6), calls=%async_computation | async-start | bytes 1048576 | tf_op jit(solution)/shard_map/all_to_all | solution.py:431
  23.6 0.0 copy-done.2
  23.6 5.2 %collective-permute-start.2 = (bf16[384,128]{1,0:T(8,128)(2,1)S(1)}, bf16[384,128]{1,0:T(8,128)(2,1)S(1)}, u32[]{:S(2)}, u32[]{:S(2)}) collective-permute-start(bf16[384,128]{1,0:T(8,128)(2,1)S(1)} %copy-done.2), channel_id=1, source_target_pairs={{0,384},{64,448},{128,0},{192,64},{256,128},{320,192},{384,256},{4... | collective-permute-start | bytes 294920 | tf_op jit(solution)/shard_map/ppermute | solution.py:445
  28.8 1.9 %collective-permute-start.1 = (bf16[384,128]{1,0:T(8,128)(2,1)S(1)}, bf16[384,128]{1,0:T(8,128)(2,1)S(1)}, u32[]{:S(2)}, u32[]{:S(2)}) collective-permute-start(bf16[384,128]{1,0:T(8,128)(2,1)S(1)} %copy-done.2), channel_id=1, source_target_pairs={{0,256},{64,320},{128,384},{192,448},{256,0},{320,64},{384,128},{4... | collective-permute-start | bytes 294920 | tf_op jit(solution)/shard_map/ppermute | solution.py:445
  30.7 3.0 %collective-permute-start = (bf16[384,128]{1,0:T(8,128)(2,1)S(1)}, bf16[384,128]{1,0:T(8,128)(2,1)S(1)}, u32[]{:S(2)}, u32[]{:S(2)}) collective-permute-start(bf16[384,128]{1,0:T(8,128)(2,1)S(1)} %copy-done.2), channel_id=1, source_target_pairs={{0,128},{64,192},{128,256},{192,320},{256,384},{320,448},{384,0},{... | collective-permute-start | bytes 294920 | tf_op jit(solution)/shard_map/ppermute | solution.py:445
  33.7 5.6 %collective-permute-done.2.near3 = bf16[384,128]{1,0:T(8,128)(2,1)S(1)} collective-permute-done((bf16[384,128]{1,0:T(8,128)(2,1)S(1)}, bf16[384,128]{1,0:T(8,128)(2,1)S(1)}, u32[]{:S(2)}, u32[]{:S(2)}) %collective-permute-start.2) | collective-permute-done | bytes 98336 | tf_op jit(solution)/shard_map/ppermute | solution.py:445
  39.4 8.0 %collective-permute-done.1.near2 = bf16[384,128]{1,0:T(8,128)(2,1)S(1)} collective-permute-done((bf16[384,128]{1,0:T(8,128)(2,1)S(1)}, bf16[384,128]{1,0:T(8,128)(2,1)S(1)}, u32[]{:S(2)}, u32[]{:S(2)}) %collective-permute-start.1) | collective-permute-done | bytes 98336 | tf_op jit(solution)/shard_map/ppermute | solution.py:445
  47.4 0.0 collective-permute-done.near1
  47.4 0.1 pad_maximum_fusion
  47.4 1.9 %collective-permute-start.3 = (bf16[4,384,128]{2,1,0:T(8,128)(2,1)S(1)}, bf16[4,384,128]{2,1,0:T(8,128)(2,1)S(1)}, u32[]{:S(2)}, u32[]{:S(2)}) collective-permute-start(bf16[4,384,128]{2,1,0:T(8,128)(2,1)S(1)} %pad_maximum_fusion), channel_id=1, source_target_pairs={{0,64},{64,0},{128,192},{192,128},{256,320},{320,256},{384,448},{4... | collective-permute-start | bytes 1179656 | tf_op jit(solution)/shard_map/ppermute | solution.py:447
  49.4 1.7 %collective-permute-done.3.far_ref = bf16[4,384,128]{2,1,0:T(8,128)(2,1)S(1)} collective-permute-done((bf16[4,384,128]{2,1,0:T(8,128)(2,1)S(1)}, bf16[4,384,128]{2,1,0:T(8,128)(2,1)S(1)}, u32[]{:S(2)}, u32[]{:S(2)}) %collective-permute-start.3) | collective-permute-done | bytes 393248 | tf_op jit(solution)/shard_map/ppermute | solution.py:447
  51.1 0.0 all-to-all-done.message_ref.before_ref.after_ref
  51.1 9.6 %shard_map.96 = bf16[64,48,128]{2,1,0:T(8,128)(2,1)S(1)} custom-call(s32[1]{0:T(128)} %bitcast.place_ref, s32[64,16,128]{2,1,0:T(8,128)S(1)} %all-to-all-done.message_ref.before_ref.after_ref, bf16[384,128]{1,0:T(8,128)(2,1)S(1)} %copy-done.2, bf16[384,128]{1,0:T(8,128)(2,1)S(1)} %collective-permute-done.near1, ...), custom_call_target="tpu_custom_call" | custom-call | tf_op jit(solution)/shard_map/pallas_call | solution.py:299
  60.7 0.0 copy-start
  60.7 0.0 copy-start.1
  60.7 0.0 copy-start.3
  60.7 40.0 %all_to_all.10.returned_ref = bf16[64,48,128]{2,1,0:T(8,128)(2,1)S(1)} all-to-all(bf16[64,48,128]{2,1,0:T(8,128)(2,1)S(1)} %shard_map.96), channel_id=1, replica_groups=mesh['own'=8,'dom'=64] {'dom'}, dimensions={0} | all-to-all | bytes 1572864 | tf_op jit(solution)/shard_map/all_to_all | solution.py:431
  100.7 0.0 copy-done
  100.7 0.0 copy-done.1
  100.7 0.0 copy-done.3
  100.7 2.6 %shard_map.97 = (bf16[6,32,1024]{2,1,0:T(8,128)(2,1)}, f32[256,128]{1,0:T(8,128)}) custom-call(s32[1]{0:T(128)} %bitcast.place_ref, s32[1,32]{1,0:T(1,128)S(1)} %copy-done.3, bf16[64,48,128]{2,1,0:T(8,128)(2,1)S(1)} %all_to_all.10.returned_ref, s32[64,16,128]{2,1,0:T(8,128)S(1)} %all-to-all-done.message_ref.before_ref.after_ref, ...), custom_call_target="tpu_custom_call" | custom-call | tf_op jit(solution)/shard_map/pallas_call | solution.py:404
Async XLA Ops:
  4.4 19.2 %copy-start.2 = (bf16[384,128]{1,0:T(8,128)(2,1)S(1)}, bf16[384,128]{1,0:T(8,128)(2,1)}, u32[]{:S(2)}) copy-start(bf16[384,128]{1,0:T(8,128)(2,1)} %get-tuple-element.7.near0) | copy-start | bytes 294916
  4.4 46.7 %all-to-all-start = ((s32[64,16,128]{2,1,0:T(8,128)}), s32[64,16,128]{2,1,0:T(8,128)S(1)}, u32[]{:S(2)}, u32[]{:S(2)}) async-start(s32[64,16,128]{2,1,0:T(8,128)} %get-tuple-element.6), calls=%async_computation | async-start | bytes 1048576 | tf_op jit(solution)/shard_map/all_to_all | solution.py:431
  23.6 15.8 %collective-permute-start.2 = (bf16[384,128]{1,0:T(8,128)(2,1)S(1)}, bf16[384,128]{1,0:T(8,128)(2,1)S(1)}, u32[]{:S(2)}, u32[]{:S(2)}) collective-permute-start(bf16[384,128]{1,0:T(8,128)(2,1)S(1)} %copy-done.2), channel_id=1, source_target_pairs={{0,384},{64,448},{128,0},{192,64},{256,128},{320,192},{384,256},{4... | collective-permute-start | bytes 294920 | tf_op jit(solution)/shard_map/ppermute | solution.py:445
  28.8 18.6 %collective-permute-start.1 = (bf16[384,128]{1,0:T(8,128)(2,1)S(1)}, bf16[384,128]{1,0:T(8,128)(2,1)S(1)}, u32[]{:S(2)}, u32[]{:S(2)}) collective-permute-start(bf16[384,128]{1,0:T(8,128)(2,1)S(1)} %copy-done.2), channel_id=1, source_target_pairs={{0,256},{64,320},{128,384},{192,448},{256,0},{320,64},{384,128},{4... | collective-permute-start | bytes 294920 | tf_op jit(solution)/shard_map/ppermute | solution.py:445
  30.7 16.7 %collective-permute-start = (bf16[384,128]{1,0:T(8,128)(2,1)S(1)}, bf16[384,128]{1,0:T(8,128)(2,1)S(1)}, u32[]{:S(2)}, u32[]{:S(2)}) collective-permute-start(bf16[384,128]{1,0:T(8,128)(2,1)S(1)} %copy-done.2), channel_id=1, source_target_pairs={{0,128},{64,192},{128,256},{192,320},{256,384},{320,448},{384,0},{... | collective-permute-start | bytes 294920 | tf_op jit(solution)/shard_map/ppermute | solution.py:445
  47.4 3.6 %collective-permute-start.3 = (bf16[4,384,128]{2,1,0:T(8,128)(2,1)S(1)}, bf16[4,384,128]{2,1,0:T(8,128)(2,1)S(1)}, u32[]{:S(2)}, u32[]{:S(2)}) collective-permute-start(bf16[4,384,128]{2,1,0:T(8,128)(2,1)S(1)} %pad_maximum_fusion), channel_id=1, source_target_pairs={{0,64},{64,0},{128,192},{192,128},{256,320},{320,256},{384,448},{4... | collective-permute-start | bytes 1179656 | tf_op jit(solution)/shard_map/ppermute | solution.py:447
  60.7 40.0 %copy-start = (f32[1,32768]{1,0:T(1,128)S(1)}, f32[1,32768]{1,0:T(1,128)}, u32[]{:S(2)}) copy-start(f32[1,32768]{1,0:T(1,128)} %param.14) | copy-start | bytes 393220
  60.7 40.0 %copy-start.1 = (f32[1,32768]{1,0:T(1,128)S(1)}, f32[1,32768]{1,0:T(1,128)}, u32[]{:S(2)}) copy-start(f32[1,32768]{1,0:T(1,128)} %param.15) | copy-start | bytes 393220
  60.7 40.0 %copy-start.3 = (s32[1,32]{1,0:T(1,128)S(1)}, s32[1,32]{1,0:T(1,128)}, u32[]{:S(2)}) copy-start(s32[1,32]{1,0:T(1,128)} %need_ref.3) | copy-start | bytes 388
